TPU v7x, 768 devices: a whole 4x8x12 slice. The times are simulated.
768 devices in a mesh: slab: 192 (over z_lo, x, y, core), cross: 4 (over z_hi).
Axes of the slice: x: 4, y: 8, z: 12 (z_hi: 4, z_lo: 3; z = z_hi * 3 + z_lo), core: 2. Of those that a mesh axis runs over, the one named last changes fastest.
Arguments:
- velocity: float32 [3, 768, 64, 128], P(None, 'slab', 'cross'), may hold values from -6 to 6
- density: float32 [768, 64, 128], P('slab', 'cross'), may hold values from 0.5 to 2
- source: float32 [768, 64, 128], P('slab', 'cross'), may hold values from -6 to 6
- species: float32 [9, 768, 64, 128], P(None, 'slab', 'cross'), may hold values from 0 to 1
Outputs:
- velocity_out: float32 [3, 768, 64, 128], P(None, 'slab', 'cross')
- pressure: float32 [768, 64, 128], P('slab', 'cross')
- species_out: float32 [9, 768, 64, 128], P(None, 'slab', 'cross')
All inputs are finite; a program needn't handle non-finite values.
Results may differ from a plain program's by a relative error of at most 0.0001.
Values sent between devices are 32-bit elements; how exact they have to be, the bound alone decides.
No kernel may reach another device: no remote copies, remote signals or barrier semaphores. Data moves between devices by JAX's collectives and lax.ppermute only.
A program may use at most 32 MiB of HBM per device.

v0:
```python
import jax
import jax.numpy as jnp
from jax import lax
from jax.sharding import PartitionSpec as P

CYCLES = 2
COARSE = 4


damping = 0.8
time_step = 0.25


def with_halo(block, sides, width):
    for axis, dim in sides:
        count = lax.axis_size(axis)
        forward = [(i, i + 1) for i in range(count - 1)]
        backward = [(target, source) for source, target in forward]
        low = lax.ppermute(
            lax.slice_in_dim(block, block.shape[dim] - width, None, axis=dim), axis, forward
        )
        high = lax.ppermute(lax.slice_in_dim(block, 0, width, axis=dim), axis, backward)
        block = jnp.concatenate([low, block, high], axis=dim)
    return block


def sent_to_all(shard, axis):
    copies = jnp.broadcast_to(shard, (lax.axis_size(axis), *shard.shape))
    return lax.all_to_all(copies, axis, split_axis=0, concat_axis=0, tiled=True)


def joined_along(pieces, dim):
    lengths = list(pieces.shape[1:])
    lengths[dim] *= pieces.shape[0]
    return jnp.moveaxis(pieces, 0, dim).reshape(lengths)


def collect_2(shard, axis, dim):
    pieces = sent_to_all(shard, axis)
    return joined_along(pieces, dim)


def pad_depth(field):
    return jnp.pad(field, ((0, 0), (0, 0), (1, 1)))


def face_weights(mobile):
    face_x = 0.5 * (mobile[:-1, 1:-1] + mobile[1:, 1:-1])
    face_y = 0.5 * (mobile[1:-1, :-1] + mobile[1:-1, 1:])
    inner = pad_depth(mobile[1:-1, 1:-1])
    face_z = 0.5 * (inner[..., :-1] + inner[..., 1:])
    diagonal = (
        face_x[:-1]
        + face_x[1:]
        + face_y[:, :-1]
        + face_y[:, 1:]
        + face_z[..., :-1]
        + face_z[..., 1:]
    )
    return (face_x, face_y, face_z, diagonal)


def operate(field, weights):
    face_x, face_y, face_z = (weights[0], weights[1], weights[2])
    center = field[1:-1, 1:-1]
    column = pad_depth(center)
    total = face_x[1:] * (field[2:, 1:-1] - center) + face_x[:-1] * (field[:-2, 1:-1] - center)
    total = (
        total
        + face_y[:, 1:] * (field[1:-1, 2:] - center)
        + face_y[:, :-1] * (field[1:-1, :-2] - center)
    )
    total = (
        total
        + face_z[..., 1:] * (column[..., 2:] - center)
        + face_z[..., :-1] * (column[..., :-2] - center)
    )
    return total


def jacobi_step(field, target, weights):
    center = field[1:-1, 1:-1]
    return center + damping * (operate(field, weights) - target) / weights[3]


def divergence(moving):
    column = pad_depth(moving[2][1:-1, 1:-1])
    total = (
        moving[0][2:, 1:-1] - moving[0][:-2, 1:-1] + (moving[1][1:-1, 2:] - moving[1][1:-1, :-2])
    )
    return 0.5 * (total + (column[..., 2:] - column[..., :-2]))


def gradient(field):
    column = pad_depth(field[1:-1, 1:-1])
    along_x = 0.5 * (field[2:, 1:-1] - field[:-2, 1:-1])
    along_y = 0.5 * (field[1:-1, 2:] - field[1:-1, :-2])
    along_z = 0.5 * (column[..., 2:] - column[..., :-2])
    return jnp.stack([along_x, along_y, along_z], 0)


def restrict(field):
    cells_x, cells_y, cells_z = field.shape
    return field.reshape(cells_x // 2, 2, cells_y // 2, 2, cells_z // 2, 2).mean(axis=(1, 3, 5))


def prolong(field):
    cells_x, cells_y, cells_z = field.shape
    spread = jnp.broadcast_to(
        field[:, None, :, None, :, None], (cells_x, 2, cells_y, 2, cells_z, 2)
    )
    return spread.reshape(2 * cells_x, 2 * cells_y, 2 * cells_z)


def advect(amounts, moving):
    flow_x = 0.5 * (moving[0][:-1, 1:-1] + moving[0][1:, 1:-1])
    flux_x = (
        jnp.maximum(flow_x, 0.0) * amounts[:, :-1, 1:-1]
        + jnp.minimum(flow_x, 0.0) * amounts[:, 1:, 1:-1]
    )
    flow_y = 0.5 * (moving[1][1:-1, :-1] + moving[1][1:-1, 1:])
    flux_y = (
        jnp.maximum(flow_y, 0.0) * amounts[:, 1:-1, :-1]
        + jnp.minimum(flow_y, 0.0) * amounts[:, 1:-1, 1:]
    )
    column = pad_depth(moving[2][1:-1, 1:-1])
    flow_z = 0.5 * (column[..., :-1] + column[..., 1:])
    center = amounts[:, 1:-1, 1:-1]
    stacked = jnp.pad(center, ((0, 0), (0, 0), (0, 0), (1, 1)))
    flux_z = (
        jnp.maximum(flow_z, 0.0) * stacked[..., :-1] + jnp.minimum(flow_z, 0.0) * stacked[..., 1:]
    )
    change = (
        flux_x[:, 1:]
        - flux_x[:, :-1]
        + (flux_y[:, :, 1:] - flux_y[:, :, :-1])
        + (flux_z[..., 1:] - flux_z[..., :-1])
    )
    return center - time_step * change


def trim_rim(field, offset):
    if offset == 0:
        return field
    return field[offset:-offset, offset:-offset]


def extend(field, width):
    return with_halo(field, (("slab", 0), ("cross", 1)), width)


def local(velocity, density, source, species):
    cells_x, cells_y, cells_z = density.shape
    halo_depth = 2
    reach = halo_depth - 1
    mobility = 1.0 / density
    bundle = jnp.concatenate([mobility[None], source[None], velocity, species], 0)
    grown = with_halo(bundle, (("slab", 1), ("cross", 2)), halo_depth)
    mobile_grown = grown[0]
    weights = face_weights(mobile_grown)
    target = divergence(grown[2:5]) - grown[1][1:-1, 1:-1]
    slab_cells = lax.axis_index("slab") * cells_x + jnp.arange(cells_x + 2) - 1
    cross_cells = lax.axis_index("cross") * cells_y + jnp.arange(cells_y + 2) - 1
    inside_x = ((slab_cells >= 0) & (slab_cells < cells_x * lax.axis_size("slab"))).astype(
        jnp.float32
    )
    inside_y = ((cross_cells >= 0) & (cross_cells < cells_y * lax.axis_size("cross"))).astype(
        jnp.float32
    )
    inside = inside_x[:, None, None] * inside_y[None, :, None]

    def sweep_once(field, extent):
        offset = reach - extent
        local_weights = tuple((trim_rim(part, offset) for part in weights))
        result = jacobi_step(field, trim_rim(target, offset), local_weights)
        if extent > 0:
            result = result * inside
        return result

    def smooth(pressure):
        pressure = sweep_once(sweep_once(extend(pressure, 2), 1), 0)
        return pressure

    fine_weights = tuple((trim_rim(part, reach) for part in weights))
    fine_target = trim_rim(target, reach)
    coarse_mobility = restrict(mobility)
    coarse_x, coarse_y, coarse_z = coarse_mobility.shape

    def collect(field):
        return collect_2(field, "cross", 1)

    def slab_extend(field):
        grown_slab = with_halo(field, (("slab", 0),), 1)
        return jnp.pad(grown_slab, ((0, 0), (1, 1), (0, 0)))

    coarse_weights = tuple(
        (0.25 * part for part in face_weights(slab_extend(collect(coarse_mobility))))
    )
    pressure = jnp.zeros_like(density)
    for cycle_index in range(CYCLES):
        pressure = smooth(pressure)
        residual = fine_target - operate(extend(pressure, 1), fine_weights)
        whole_target = collect(restrict(residual))
        correction = jnp.zeros_like(whole_target)
        for sweep_index in range(COARSE):
            correction = jacobi_step(slab_extend(correction), whole_target, coarse_weights)
        pressure = pressure + prolong(
            lax.dynamic_slice_in_dim(correction, lax.axis_index("cross") * coarse_y, coarse_y, 1)
        )
        pressure = smooth(pressure)
    offset = halo_depth - 1
    mobile_rim = trim_rim(mobile_grown, offset)
    velocity_rim = grown[2:5][:, offset : grown.shape[1] - offset, offset : grown.shape[2] - offset]
    species_rim = grown[5:][:, offset : grown.shape[1] - offset, offset : grown.shape[2] - offset]
    moved = (velocity_rim - mobile_rim[None] * gradient(extend(pressure, 2))) * inside[None]
    species_out = advect(species_rim, moved)
    return (moved[:, 1:-1, 1:-1], pressure, species_out)


def solution(mesh):
    return jax.shard_map(
        local,
        mesh=mesh,
        in_specs=(
            P(None, "slab", "cross", None),
            P("slab", "cross", None),
            P("slab", "cross", None),
            P(None, "slab", "cross", None),
        ),
        out_specs=(
            P(None, "slab", "cross", None),
            P("slab", "cross", None),
            P(None, "slab", "cross", None),
        ),
        check_vma=False,
    )
```

profile of v0, /device:TPU:127, one launch (start us, length us, event | category | flops | bytes accessed | tf_op | source)
XLA Modules:
  0.0 363.2 jit_solution(16427551672705971396)
XLA Ops:
  0.6 2.6 collective-permute-start.5
  3.2 7.2 %collective-permute-start.4 = (f32[2,16,128]{2,1,0:T(8,128)S(1)}, f32[2,16,128]{2,1,0:T(8,128)S(1)}, u32[]{:S(2)}, u32[]{:S(2)}) collective-permute-start(f32[2,16,128]{2,1,0:T(8,128)S(1)} %broadcast.205), channel_id=1, source_target_pairs={{0,4},{4,8},{8,12},{12,16},{16,20},{20,24},{24,28},{28,32},{32,36}... | collective-permute-start | bytes 49160 | tf_op jit(solution)/shard_map/ppermute | solution.py:19
  12.4 2.4 collective-permute-start.10
  17.3 7.4 %collective-permute-start = (f32[14,2,16,128]{3,2,1,0:T(8,128)}, f32[14,2,16,128]{3,2,1,0:T(8,128)S(1)}, u32[]{:S(2)}, u32[]{:S(2)}) collective-permute-start(f32[14,2,16,128]{3,2,1,0:T(8,128)} %get-tuple-element.15), channel_id=1, source_target_pairs={{0,4},{4,8},{8,12},{12,16},{16,20},{20,24},{24,28},{28,32},{32,36}... | collective-permute-start | bytes 688136 | tf_op jit(solution)/shard_map/ppermute | solution.py:19
  27.7 15.7 %all-to-all-start = ((f32[4,1,1024]{2,1,0:T(1,128)}), f32[4,1,1024]{2,1,0:T(1,128)S(1)}, u32[]{:S(2)}, u32[]{:S(2)}) async-start(f32[4,1,1024]{2,1,0:T(1,128)} %reshape.125), calls=%async_computation | async-start | bytes 32768 | tf_op jit(solution)/shard_map/all_to_all | solution.py:29
  45.5 6.4 %collective-permute-start.6 = (f32[8,2,128]{2,1,0:T(2,128)S(1)}, f32[8,2,128]{2,1,0:T(2,128)S(1)}, u32[]{:S(2)}, u32[]{:S(2)}) collective-permute-start(f32[8,2,128]{2,1,0:T(2,128)S(1)} %get-tuple-element.38), channel_id=1, source_target_pairs={{0,1},{1,2},{2,3},{4,5},{5,6},{6,7},{8,9},{9,10},{10,11},{12,13},{... | collective-permute-start | bytes 24584 | tf_op jit(solution)/shard_map/ppermute | solution.py:19
  53.9 5.4 %collective-permute-done.7 = f32[8,2,128]{2,1,0:T(2,128)S(1)} collective-permute-done((f32[8,2,128]{2,1,0:T(2,128)S(1)}, f32[8,2,128]{2,1,0:T(2,128)S(1)}, u32[]{:S(2)}, u32[]{:S(2)}) %collective-permute-start.7) | collective-permute-done | bytes 8224 | tf_op jit(solution)/shard_map/ppermute | solution.py:22
  61.0 4.3 %collective-permute-start.2 = (f32[14,8,2,128]{3,2,1,0:T(2,128)S(1)}, f32[14,8,2,128]{3,2,1,0:T(2,128)S(1)}, u32[]{:S(2)}, u32[]{:S(2)}) collective-permute-start(f32[14,8,2,128]{3,2,1,0:T(2,128)S(1)} %get-tuple-element.13), channel_id=1, source_target_pairs={{0,1},{1,2},{2,3},{4,5},{5,6},{6,7},{8,9},{9,10},{10,11},{12,13},{... | collective-permute-start | bytes 344072 | tf_op jit(solution)/shard_map/ppermute | solution.py:19
  66.6 12.8 %collective-permute-start.8 = (f32[1,32,64]{2,1,0:T(8,128)S(1)}, f32[1,32,64]{2,1,0:T(8,128)S(1)}, u32[]{:S(2)}, u32[]{:S(2)}) collective-permute-start(f32[1,32,64]{2,1,0:T(8,128)S(1)} %get-tuple-element.78), channel_id=1, source_target_pairs={{0,4},{4,8},{8,12},{12,16},{16,20},{20,24},{24,28},{28,32},{32,36}... | collective-permute-start | bytes 24584 | tf_op jit(solution)/shard_map/ppermute | solution.py:19
  84.6 7.9 %collective-permute-start.13 = (f32[1,16,128]{2,1,0:T(8,128)S(1)}, f32[1,16,128]{2,1,0:T(8,128)S(1)}, u32[]{:S(2)}, u32[]{:S(2)}) collective-permute-start(f32[1,16,128]{2,1,0:T(8,128)S(1)} %get-tuple-element.84), channel_id=1, source_target_pairs={{0,4},{4,8},{8,12},{12,16},{16,20},{20,24},{24,28},{28,32},{32,36}... | collective-permute-start | bytes 24584 | tf_op jit(solution)/shard_map/ppermute | solution.py:19
  94.5 7.2 %collective-permute-done.12 = f32[1,16,128]{2,1,0:T(8,128)S(1)} collective-permute-done((f32[1,16,128]{2,1,0:T(8,128)S(1)}, f32[1,16,128]{2,1,0:T(8,128)S(1)}, u32[]{:S(2)}, u32[]{:S(2)}) %collective-permute-start.12) | collective-permute-done | bytes 8224 | tf_op jit(solution)/shard_map/ppermute | solution.py:22
  102.9 7.9 %collective-permute-start.15 = (f32[6,1,128]{2,1,0:T(1,128)S(1)}, f32[6,1,128]{2,1,0:T(1,128)S(1)}, u32[]{:S(2)}, u32[]{:S(2)}) collective-permute-start(f32[6,1,128]{2,1,0:T(1,128)S(1)} %get-tuple-element.43), channel_id=1, source_target_pairs={{0,1},{1,2},{2,3},{4,5},{5,6},{6,7},{8,9},{9,10},{10,11},{12,13},{... | collective-permute-start | bytes 9224 | tf_op jit(solution)/shard_map/ppermute | solution.py:19
  112.3 2.8 reshape.119
  117.4 8.7 %all-to-all-start.1 = ((f32[4,1,1024]{2,1,0:T(1,128)}), f32[4,1,1024]{2,1,0:T(1,128)S(1)}, u32[]{:S(2)}, u32[]{:S(2)}) async-start(f32[4,1,1024]{2,1,0:T(1,128)} %reshape.127), calls=%async_computation.1 | async-start | bytes 32768 | tf_op jit(solution)/shard_map/all_to_all | solution.py:29
  126.8 8.3 %all-to-all-done.1 = f32[4,1,1024]{2,1,0:T(1,128)S(1)} async-done(((f32[4,1,1024]{2,1,0:T(1,128)}), f32[4,1,1024]{2,1,0:T(1,128)S(1)}, u32[]{:S(2)}, u32[]{:S(2)}) %all-to-all-start.1) | async-done | bytes 16416 | tf_op jit(solution)/shard_map/all_to_all | solution.py:29
  137.6 5.6 %collective-permute-start.17 = (f32[1,32,64]{2,1,0:T(8,128)S(1)}, f32[1,32,64]{2,1,0:T(8,128)S(1)}, u32[]{:S(2)}, u32[]{:S(2)}) collective-permute-start(f32[1,32,64]{2,1,0:T(8,128)S(1)} %get-tuple-element.74), channel_id=1, source_target_pairs={{0,4},{4,8},{8,12},{12,16},{16,20},{20,24},{24,28},{28,32},{32,36}... | collective-permute-start | bytes 24584 | tf_op jit(solution)/shard_map/ppermute | solution.py:19
  145.2 7.3 %collective-permute-done.16 = f32[1,32,64]{2,1,0:T(8,128)S(1)} collective-permute-done((f32[1,32,64]{2,1,0:T(8,128)S(1)}, f32[1,32,64]{2,1,0:T(8,128)S(1)}, u32[]{:S(2)}, u32[]{:S(2)}) %collective-permute-start.16) | collective-permute-done | bytes 8224 | tf_op jit(solution)/shard_map/ppermute | solution.py:22
  154.6 2.4 collective-permute-start.18
  157.0 6.9 %collective-permute-done.18 = f32[1,32,64]{2,1,0:T(8,128)S(1)} collective-permute-done((f32[1,32,64]{2,1,0:T(8,128)S(1)}, f32[1,32,64]{2,1,0:T(8,128)S(1)}, u32[]{:S(2)}, u32[]{:S(2)}) %collective-permute-start.18) | collective-permute-done | bytes 8224 | tf_op jit(solution)/shard_map/ppermute | solution.py:22
  166.0 2.4 collective-permute-start.20
  168.4 6.9 %collective-permute-done.20 = f32[1,32,64]{2,1,0:T(8,128)S(1)} collective-permute-done((f32[1,32,64]{2,1,0:T(8,128)S(1)}, f32[1,32,64]{2,1,0:T(8,128)S(1)}, u32[]{:S(2)}, u32[]{:S(2)}) %collective-permute-start.20) | collective-permute-done | bytes 8224 | tf_op jit(solution)/shard_map/ppermute | solution.py:22
  180.3 2.4 collective-permute-start.23
  182.7 6.9 %collective-permute-done.23 = f32[2,16,128]{2,1,0:T(8,128)S(1)} collective-permute-done((f32[2,16,128]{2,1,0:T(8,128)S(1)}, f32[2,16,128]{2,1,0:T(8,128)S(1)}, u32[]{:S(2)}, u32[]{:S(2)}) %collective-permute-start.23) | collective-permute-done | bytes 16416 | tf_op jit(solution)/shard_map/ppermute | solution.py:22
  189.6 2.8 collective-permute-start.24
  193.7 6.8 %collective-permute-done.25 = f32[8,2,128]{2,1,0:T(2,128)S(1)} collective-permute-done((f32[8,2,128]{2,1,0:T(2,128)S(1)}, f32[8,2,128]{2,1,0:T(2,128)S(1)}, u32[]{:S(2)}, u32[]{:S(2)}) %collective-permute-start.25) | collective-permute-done | bytes 8224 | tf_op jit(solution)/shard_map/ppermute | solution.py:22
  200.8 3.1 collective-permute-start.26
  205.8 7.3 %collective-permute-done.27 = f32[2,16,128]{2,1,0:T(8,128)S(1)} collective-permute-done((f32[2,16,128]{2,1,0:T(8,128)S(1)}, f32[2,16,128]{2,1,0:T(8,128)S(1)}, u32[]{:S(2)}, u32[]{:S(2)}) %collective-permute-start.27) | collective-permute-done | bytes 16416 | tf_op jit(solution)/shard_map/ppermute | solution.py:22
  213.1 6.6 %collective-permute-start.28 = (f32[8,2,128]{2,1,0:T(2,128)S(1)}, f32[8,2,128]{2,1,0:T(2,128)S(1)}, u32[]{:S(2)}, u32[]{:S(2)}) collective-permute-start(f32[8,2,128]{2,1,0:T(2,128)S(1)} %get-tuple-element.32), channel_id=1, source_target_pairs={{0,1},{1,2},{2,3},{4,5},{5,6},{6,7},{8,9},{9,10},{10,11},{12,13},{... | collective-permute-start | bytes 24584 | tf_op jit(solution)/shard_map/ppermute | solution.py:19
  221.1 6.1 %collective-permute-done.29 = f32[8,2,128]{2,1,0:T(2,128)S(1)} collective-permute-done((f32[8,2,128]{2,1,0:T(2,128)S(1)}, f32[8,2,128]{2,1,0:T(2,128)S(1)}, u32[]{:S(2)}, u32[]{:S(2)}) %collective-permute-start.29) | collective-permute-done | bytes 8224 | tf_op jit(solution)/shard_map/ppermute | solution.py:22
  227.6 3.3 collective-permute-start.31
  232.9 7.2 %collective-permute-done.30 = f32[1,16,128]{2,1,0:T(8,128)S(1)} collective-permute-done((f32[1,16,128]{2,1,0:T(8,128)S(1)}, f32[1,16,128]{2,1,0:T(8,128)S(1)}, u32[]{:S(2)}, u32[]{:S(2)}) %collective-permute-start.30) | collective-permute-done | bytes 8224 | tf_op jit(solution)/shard_map/ppermute | solution.py:22
  241.4 7.0 %collective-permute-start.33 = (f32[6,1,128]{2,1,0:T(1,128)S(1)}, f32[6,1,128]{2,1,0:T(1,128)S(1)}, u32[]{:S(2)}, u32[]{:S(2)}) collective-permute-start(f32[6,1,128]{2,1,0:T(1,128)S(1)} %get-tuple-element.41), channel_id=1, source_target_pairs={{0,1},{1,2},{2,3},{4,5},{5,6},{6,7},{8,9},{9,10},{10,11},{12,13},{... | collective-permute-start | bytes 9224 | tf_op jit(solution)/shard_map/ppermute | solution.py:19
  249.9 2.8 reshape.122
  254.3 14.8 %all_to_all.15 = f32[4,1,1024]{2,1,0:T(1,128)S(1)} all-to-all(f32[4,1,1024]{2,1,0:T(1,128)S(1)} %reshape.129), channel_id=1, replica_groups=mesh['slab'=192,'cross'=4] {'cross'}, dimensions={0} | all-to-all | bytes 32768 | tf_op jit(solution)/shard_map/all_to_all | solution.py:29
  270.7 4.8 %collective-permute-start.35 = (f32[1,32,64]{2,1,0:T(8,128)S(1)}, f32[1,32,64]{2,1,0:T(8,128)S(1)}, u32[]{:S(2)}, u32[]{:S(2)}) collective-permute-start(f32[1,32,64]{2,1,0:T(8,128)S(1)} %get-tuple-element.57), channel_id=1, source_target_pairs={{0,4},{4,8},{8,12},{12,16},{16,20},{20,24},{24,28},{28,32},{32,36}... | collective-permute-start | bytes 24584 | tf_op jit(solution)/shard_map/ppermute | solution.py:19
  277.5 7.3 %collective-permute-done.34 = f32[1,32,64]{2,1,0:T(8,128)S(1)} collective-permute-done((f32[1,32,64]{2,1,0:T(8,128)S(1)}, f32[1,32,64]{2,1,0:T(8,128)S(1)}, u32[]{:S(2)}, u32[]{:S(2)}) %collective-permute-start.34) | collective-permute-done | bytes 8224 | tf_op jit(solution)/shard_map/ppermute | solution.py:22
  286.9 2.4 collective-permute-start.36
  289.3 6.9 %collective-permute-done.36 = f32[1,32,64]{2,1,0:T(8,128)S(1)} collective-permute-done((f32[1,32,64]{2,1,0:T(8,128)S(1)}, f32[1,32,64]{2,1,0:T(8,128)S(1)}, u32[]{:S(2)}, u32[]{:S(2)}) %collective-permute-start.36) | collective-permute-done | bytes 8224 | tf_op jit(solution)/shard_map/ppermute | solution.py:22
  298.3 2.6 collective-permute-start.38
  300.9 6.7 %collective-permute-done.38 = f32[1,32,64]{2,1,0:T(8,128)S(1)} collective-permute-done((f32[1,32,64]{2,1,0:T(8,128)S(1)}, f32[1,32,64]{2,1,0:T(8,128)S(1)}, u32[]{:S(2)}, u32[]{:S(2)}) %collective-permute-start.38) | collective-permute-done | bytes 8224 | tf_op jit(solution)/shard_map/ppermute | solution.py:22
  311.9 2.4 collective-permute-start.41
  314.3 6.9 %collective-permute-done.41 = f32[2,16,128]{2,1,0:T(8,128)S(1)} collective-permute-done((f32[2,16,128]{2,1,0:T(8,128)S(1)}, f32[2,16,128]{2,1,0:T(8,128)S(1)}, u32[]{:S(2)}, u32[]{:S(2)}) %collective-permute-start.41) | collective-permute-done | bytes 16416 | tf_op jit(solution)/shard_map/ppermute | solution.py:22
  321.2 2.8 collective-permute-start.42
  325.5 6.7 %collective-permute-done.43 = f32[8,2,128]{2,1,0:T(2,128)S(1)} collective-permute-done((f32[8,2,128]{2,1,0:T(2,128)S(1)}, f32[8,2,128]{2,1,0:T(2,128)S(1)}, u32[]{:S(2)}, u32[]{:S(2)}) %collective-permute-start.43) | collective-permute-done | bytes 8224 | tf_op jit(solution)/shard_map/ppermute | solution.py:22
  333.3 3.1 collective-permute-start.44
  338.3 7.3 %collective-permute-done.45 = f32[2,16,128]{2,1,0:T(8,128)S(1)} collective-permute-done((f32[2,16,128]{2,1,0:T(8,128)S(1)}, f32[2,16,128]{2,1,0:T(8,128)S(1)}, u32[]{:S(2)}, u32[]{:S(2)}) %collective-permute-start.45) | collective-permute-done | bytes 16416 | tf_op jit(solution)/shard_map/ppermute | solution.py:22
  345.7 6.6 %collective-permute-start.46 = (f32[8,2,128]{2,1,0:T(2,128)S(1)}, f32[8,2,128]{2,1,0:T(2,128)S(1)}, u32[]{:S(2)}, u32[]{:S(2)}) collective-permute-start(f32[8,2,128]{2,1,0:T(2,128)S(1)} %get-tuple-element.28), channel_id=1, source_target_pairs={{0,1},{1,2},{2,3},{4,5},{5,6},{6,7},{8,9},{9,10},{10,11},{12,13},{... | collective-permute-start | bytes 24584 | tf_op jit(solution)/shard_map/ppermute | solution.py:19
  353.7 6.1 %collective-permute-done.47 = f32[8,2,128]{2,1,0:T(2,128)S(1)} collective-permute-done((f32[8,2,128]{2,1,0:T(2,128)S(1)}, f32[8,2,128]{2,1,0:T(2,128)S(1)}, u32[]{:S(2)}, u32[]{:S(2)}) %collective-permute-start.47) | collective-permute-done | bytes 8224 | tf_op jit(solution)/shard_map/ppermute | solution.py:22
  (224 shorter events, 73.0 us)
Async XLA Ops:
  0.6 42.9 %collective-permute-start.5 = (f32[2,16,128]{2,1,0:T(8,128)S(1)}, f32[2,16,128]{2,1,0:T(8,128)S(1)}, u32[]{:S(2)}, u32[]{:S(2)}) collective-permute-start(f32[2,16,128]{2,1,0:T(8,128)S(1)} %broadcast.205), channel_id=1, source_target_pairs={{4,0},{8,4},{12,8},{16,12},{20,16},{24,20},{28,24},{32,28},{36,32}... | collective-permute-start | bytes 49160 | tf_op jit(solution)/shard_map/ppermute | solution.py:22
  3.2 42.3 %collective-permute-start.4 = (f32[2,16,128]{2,1,0:T(8,128)S(1)}, f32[2,16,128]{2,1,0:T(8,128)S(1)}, u32[]{:S(2)}, u32[]{:S(2)}) collective-permute-start(f32[2,16,128]{2,1,0:T(8,128)S(1)} %broadcast.205), channel_id=1, source_target_pairs={{0,4},{4,8},{8,12},{12,16},{16,20},{20,24},{24,28},{28,32},{32,36}... | collective-permute-start | bytes 49160 | tf_op jit(solution)/shard_map/ppermute | solution.py:19
  10.4 41.5 %collective-permute-start.11 = (f32[1,32,64]{2,1,0:T(8,128)S(1)}, f32[1,32,64]{2,1,0:T(8,128)S(1)}, u32[]{:S(2)}, u32[]{:S(2)}) collective-permute-start(f32[1,32,64]{2,1,0:T(8,128)S(1)} %broadcast.216), channel_id=1, source_target_pairs={{0,4},{4,8},{8,12},{12,16},{16,20},{20,24},{24,28},{28,32},{32,36}... | collective-permute-start | bytes 24584 | tf_op jit(solution)/shard_map/ppermute | solution.py:19
  12.4 40.9 %collective-permute-start.10 = (f32[1,32,64]{2,1,0:T(8,128)S(1)}, f32[1,32,64]{2,1,0:T(8,128)S(1)}, u32[]{:S(2)}, u32[]{:S(2)}) collective-permute-start(f32[1,32,64]{2,1,0:T(8,128)S(1)} %broadcast.216), channel_id=1, source_target_pairs={{4,0},{8,4},{12,8},{16,12},{20,16},{24,20},{28,24},{32,28},{36,32}... | collective-permute-start | bytes 24584 | tf_op jit(solution)/shard_map/ppermute | solution.py:22
  17.3 43.5 %collective-permute-start = (f32[14,2,16,128]{3,2,1,0:T(8,128)}, f32[14,2,16,128]{3,2,1,0:T(8,128)S(1)}, u32[]{:S(2)}, u32[]{:S(2)}) collective-permute-start(f32[14,2,16,128]{3,2,1,0:T(8,128)} %get-tuple-element.15), channel_id=1, source_target_pairs={{0,4},{4,8},{8,12},{12,16},{16,20},{20,24},{24,28},{28,32},{32,36}... | collective-permute-start | bytes 688136 | tf_op jit(solution)/shard_map/ppermute | solution.py:19
  27.7 31.6 %all-to-all-start = ((f32[4,1,1024]{2,1,0:T(1,128)}), f32[4,1,1024]{2,1,0:T(1,128)S(1)}, u32[]{:S(2)}, u32[]{:S(2)}) async-start(f32[4,1,1024]{2,1,0:T(1,128)} %reshape.125), calls=%async_computation | async-start | bytes 32768 | tf_op jit(solution)/shard_map/all_to_all | solution.py:29
  43.6 17.2 %collective-permute-start.1 = (f32[14,2,16,128]{3,2,1,0:T(8,128)S(1)}, f32[14,2,16,128]{3,2,1,0:T(8,128)S(1)}, u32[]{:S(2)}, u32[]{:S(2)}) collective-permute-start(f32[14,2,16,128]{3,2,1,0:T(8,128)S(1)} %get-tuple-element.16), channel_id=1, source_target_pairs={{4,0},{8,4},{12,8},{16,12},{20,16},{24,20},{28,24},{32,28},{36,32}... | collective-permute-start | bytes 688136 | tf_op jit(solution)/shard_map/ppermute | solution.py:22
  45.5 8.4 %collective-permute-start.6 = (f32[8,2,128]{2,1,0:T(2,128)S(1)}, f32[8,2,128]{2,1,0:T(2,128)S(1)}, u32[]{:S(2)}, u32[]{:S(2)}) collective-permute-start(f32[8,2,128]{2,1,0:T(2,128)S(1)} %get-tuple-element.38), channel_id=1, source_target_pairs={{0,1},{1,2},{2,3},{4,5},{5,6},{6,7},{8,9},{9,10},{10,11},{12,13},{... | collective-permute-start | bytes 24584 | tf_op jit(solution)/shard_map/ppermute | solution.py:19
  51.9 7.4 %collective-permute-start.7 = (f32[8,2,128]{2,1,0:T(2,128)S(1)}, f32[8,2,128]{2,1,0:T(2,128)S(1)}, u32[]{:S(2)}, u32[]{:S(2)}) collective-permute-start(f32[8,2,128]{2,1,0:T(2,128)S(1)} %get-tuple-element.39), channel_id=1, source_target_pairs={{1,0},{2,1},{3,2},{5,4},{6,5},{7,6},{9,8},{10,9},{11,10},{13,12},{... | collective-permute-start | bytes 24584 | tf_op jit(solution)/shard_map/ppermute | solution.py:22
  61.0 21.0 %collective-permute-start.2 = (f32[14,8,2,128]{3,2,1,0:T(2,128)S(1)}, f32[14,8,2,128]{3,2,1,0:T(2,128)S(1)}, u32[]{:S(2)}, u32[]{:S(2)}) collective-permute-start(f32[14,8,2,128]{3,2,1,0:T(2,128)S(1)} %get-tuple-element.13), channel_id=1, source_target_pairs={{0,1},{1,2},{2,3},{4,5},{5,6},{6,7},{8,9},{9,10},{10,11},{12,13},{... | collective-permute-start | bytes 344072 | tf_op jit(solution)/shard_map/ppermute | solution.py:19
  65.3 16.7 %collective-permute-start.3 = (f32[14,8,2,128]{3,2,1,0:T(2,128)S(1)}, f32[14,8,2,128]{3,2,1,0:T(2,128)S(1)}, u32[]{:S(2)}, u32[]{:S(2)}) collective-permute-start(f32[14,8,2,128]{3,2,1,0:T(2,128)S(1)} %get-tuple-element.14), channel_id=1, source_target_pairs={{1,0},{2,1},{3,2},{5,4},{6,5},{7,6},{9,8},{10,9},{11,10},{13,12},{... | collective-permute-start | bytes 344072 | tf_op jit(solution)/shard_map/ppermute | solution.py:22
  66.6 27.8 %collective-permute-start.8 = (f32[1,32,64]{2,1,0:T(8,128)S(1)}, f32[1,32,64]{2,1,0:T(8,128)S(1)}, u32[]{:S(2)}, u32[]{:S(2)}) collective-permute-start(f32[1,32,64]{2,1,0:T(8,128)S(1)} %get-tuple-element.78), channel_id=1, source_target_pairs={{0,4},{4,8},{8,12},{12,16},{16,20},{20,24},{24,28},{28,32},{32,36}... | collective-permute-start | bytes 24584 | tf_op jit(solution)/shard_map/ppermute | solution.py:19
  79.4 15.0 %collective-permute-start.9 = (f32[1,32,64]{2,1,0:T(8,128)S(1)}, f32[1,32,64]{2,1,0:T(8,128)S(1)}, u32[]{:S(2)}, u32[]{:S(2)}) collective-permute-start(f32[1,32,64]{2,1,0:T(8,128)S(1)} %get-tuple-element.79), channel_id=1, source_target_pairs={{4,0},{8,4},{12,8},{16,12},{20,16},{24,20},{28,24},{32,28},{36,32}... | collective-permute-start | bytes 24584 | tf_op jit(solution)/shard_map/ppermute | solution.py:22
  84.6 9.9 %collective-permute-start.13 = (f32[1,16,128]{2,1,0:T(8,128)S(1)}, f32[1,16,128]{2,1,0:T(8,128)S(1)}, u32[]{:S(2)}, u32[]{:S(2)}) collective-permute-start(f32[1,16,128]{2,1,0:T(8,128)S(1)} %get-tuple-element.84), channel_id=1, source_target_pairs={{0,4},{4,8},{8,12},{12,16},{16,20},{20,24},{24,28},{28,32},{32,36}... | collective-permute-start | bytes 24584 | tf_op jit(solution)/shard_map/ppermute | solution.py:19
  92.5 9.2 %collective-permute-start.12 = (f32[1,16,128]{2,1,0:T(8,128)S(1)}, f32[1,16,128]{2,1,0:T(8,128)S(1)}, u32[]{:S(2)}, u32[]{:S(2)}) collective-permute-start(f32[1,16,128]{2,1,0:T(8,128)S(1)} %get-tuple-element.85), channel_id=1, source_target_pairs={{4,0},{8,4},{12,8},{16,12},{20,16},{24,20},{28,24},{32,28},{36,32}... | collective-permute-start | bytes 24584 | tf_op jit(solution)/shard_map/ppermute | solution.py:22
  101.6 9.8 %collective-permute-start.14 = (f32[6,1,128]{2,1,0:T(1,128)S(1)}, f32[6,1,128]{2,1,0:T(1,128)S(1)}, u32[]{:S(2)}, u32[]{:S(2)}) collective-permute-start(f32[6,1,128]{2,1,0:T(1,128)S(1)} %get-tuple-element.42), channel_id=1, source_target_pairs={{1,0},{2,1},{3,2},{5,4},{6,5},{7,6},{9,8},{10,9},{11,10},{13,12},{... | collective-permute-start | bytes 9224 | tf_op jit(solution)/shard_map/ppermute | solution.py:22
  102.9 8.6 %collective-permute-start.15 = (f32[6,1,128]{2,1,0:T(1,128)S(1)}, f32[6,1,128]{2,1,0:T(1,128)S(1)}, u32[]{:S(2)}, u32[]{:S(2)}) collective-permute-start(f32[6,1,128]{2,1,0:T(1,128)S(1)} %get-tuple-element.43), channel_id=1, source_target_pairs={{0,1},{1,2},{2,3},{4,5},{5,6},{6,7},{8,9},{9,10},{10,11},{12,13},{... | collective-permute-start | bytes 9224 | tf_op jit(solution)/shard_map/ppermute | solution.py:19
  117.4 17.8 %all-to-all-start.1 = ((f32[4,1,1024]{2,1,0:T(1,128)}), f32[4,1,1024]{2,1,0:T(1,128)S(1)}, u32[]{:S(2)}, u32[]{:S(2)}) async-start(f32[4,1,1024]{2,1,0:T(1,128)} %reshape.127), calls=%async_computation.1 | async-start | bytes 32768 | tf_op jit(solution)/shard_map/all_to_all | solution.py:29
  137.6 7.6 %collective-permute-start.17 = (f32[1,32,64]{2,1,0:T(8,128)S(1)}, f32[1,32,64]{2,1,0:T(8,128)S(1)}, u32[]{:S(2)}, u32[]{:S(2)}) collective-permute-start(f32[1,32,64]{2,1,0:T(8,128)S(1)} %get-tuple-element.74), channel_id=1, source_target_pairs={{0,4},{4,8},{8,12},{12,16},{16,20},{20,24},{24,28},{28,32},{32,36}... | collective-permute-start | bytes 24584 | tf_op jit(solution)/shard_map/ppermute | solution.py:19
  143.2 9.3 %collective-permute-start.16 = (f32[1,32,64]{2,1,0:T(8,128)S(1)}, f32[1,32,64]{2,1,0:T(8,128)S(1)}, u32[]{:S(2)}, u32[]{:S(2)}) collective-permute-start(f32[1,32,64]{2,1,0:T(8,128)S(1)} %get-tuple-element.75), channel_id=1, source_target_pairs={{4,0},{8,4},{12,8},{16,12},{20,16},{24,20},{28,24},{32,28},{36,32}... | collective-permute-start | bytes 24584 | tf_op jit(solution)/shard_map/ppermute | solution.py:22
  152.7 4.3 %collective-permute-start.19 = (f32[1,32,64]{2,1,0:T(8,128)S(1)}, f32[1,32,64]{2,1,0:T(8,128)S(1)}, u32[]{:S(2)}, u32[]{:S(2)}) collective-permute-start(f32[1,32,64]{2,1,0:T(8,128)S(1)} %get-tuple-element.72), channel_id=1, source_target_pairs={{0,4},{4,8},{8,12},{12,16},{16,20},{20,24},{24,28},{28,32},{32,36}... | collective-permute-start | bytes 24584 | tf_op jit(solution)/shard_map/ppermute | solution.py:19
  154.6 9.3 %collective-permute-start.18 = (f32[1,32,64]{2,1,0:T(8,128)S(1)}, f32[1,32,64]{2,1,0:T(8,128)S(1)}, u32[]{:S(2)}, u32[]{:S(2)}) collective-permute-start(f32[1,32,64]{2,1,0:T(8,128)S(1)} %get-tuple-element.73), channel_id=1, source_target_pairs={{4,0},{8,4},{12,8},{16,12},{20,16},{24,20},{28,24},{32,28},{36,32}... | collective-permute-start | bytes 24584 | tf_op jit(solution)/shard_map/ppermute | solution.py:22
  164.0 4.4 %collective-permute-start.21 = (f32[1,32,64]{2,1,0:T(8,128)S(1)}, f32[1,32,64]{2,1,0:T(8,128)S(1)}, u32[]{:S(2)}, u32[]{:S(2)}) collective-permute-start(f32[1,32,64]{2,1,0:T(8,128)S(1)} %get-tuple-element.70), channel_id=1, source_target_pairs={{0,4},{4,8},{8,12},{12,16},{16,20},{20,24},{24,28},{28,32},{32,36}... | collective-permute-start | bytes 24584 | tf_op jit(solution)/shard_map/ppermute | solution.py:19
  166.0 9.3 %collective-permute-start.20 = (f32[1,32,64]{2,1,0:T(8,128)S(1)}, f32[1,32,64]{2,1,0:T(8,128)S(1)}, u32[]{:S(2)}, u32[]{:S(2)}) collective-permute-start(f32[1,32,64]{2,1,0:T(8,128)S(1)} %get-tuple-element.71), channel_id=1, source_target_pairs={{4,0},{8,4},{12,8},{16,12},{20,16},{24,20},{28,24},{32,28},{36,32}... | collective-permute-start | bytes 24584 | tf_op jit(solution)/shard_map/ppermute | solution.py:22
  178.4 4.3 %collective-permute-start.22 = (f32[2,16,128]{2,1,0:T(8,128)S(1)}, f32[2,16,128]{2,1,0:T(8,128)S(1)}, u32[]{:S(2)}, u32[]{:S(2)}) collective-permute-start(f32[2,16,128]{2,1,0:T(8,128)S(1)} %get-tuple-element.63), channel_id=1, source_target_pairs={{0,4},{4,8},{8,12},{12,16},{16,20},{20,24},{24,28},{28,32},{32,36}... | collective-permute-start | bytes 49160 | tf_op jit(solution)/shard_map/ppermute | solution.py:19
  180.3 9.3 %collective-permute-start.23 = (f32[2,16,128]{2,1,0:T(8,128)S(1)}, f32[2,16,128]{2,1,0:T(8,128)S(1)}, u32[]{:S(2)}, u32[]{:S(2)}) collective-permute-start(f32[2,16,128]{2,1,0:T(8,128)S(1)} %get-tuple-element.64), channel_id=1, source_target_pairs={{4,0},{8,4},{12,8},{16,12},{20,16},{24,20},{28,24},{32,28},{36,32}... | collective-permute-start | bytes 49160 | tf_op jit(solution)/shard_map/ppermute | solution.py:22
  192.4 8.1 %collective-permute-start.25 = (f32[8,2,128]{2,1,0:T(2,128)S(1)}, f32[8,2,128]{2,1,0:T(2,128)S(1)}, u32[]{:S(2)}, u32[]{:S(2)}) collective-permute-start(f32[8,2,128]{2,1,0:T(2,128)S(1)} %get-tuple-element.35), channel_id=1, source_target_pairs={{1,0},{2,1},{3,2},{5,4},{6,5},{7,6},{9,8},{10,9},{11,10},{13,12},{... | collective-permute-start | bytes 24584 | tf_op jit(solution)/shard_map/ppermute | solution.py:22
  200.8 5.0 %collective-permute-start.26 = (f32[2,16,128]{2,1,0:T(8,128)S(1)}, f32[2,16,128]{2,1,0:T(8,128)S(1)}, u32[]{:S(2)}, u32[]{:S(2)}) collective-permute-start(f32[2,16,128]{2,1,0:T(8,128)S(1)} %get-tuple-element.61), channel_id=1, source_target_pairs={{0,4},{4,8},{8,12},{12,16},{16,20},{20,24},{24,28},{28,32},{32,36}... | collective-permute-start | bytes 49160 | tf_op jit(solution)/shard_map/ppermute | solution.py:19
  203.9 9.3 %collective-permute-start.27 = (f32[2,16,128]{2,1,0:T(8,128)S(1)}, f32[2,16,128]{2,1,0:T(8,128)S(1)}, u32[]{:S(2)}, u32[]{:S(2)}) collective-permute-start(f32[2,16,128]{2,1,0:T(8,128)S(1)} %get-tuple-element.62), channel_id=1, source_target_pairs={{4,0},{8,4},{12,8},{16,12},{20,16},{24,20},{28,24},{32,28},{36,32}... | collective-permute-start | bytes 49160 | tf_op jit(solution)/shard_map/ppermute | solution.py:22
  213.1 8.0 %collective-permute-start.28 = (f32[8,2,128]{2,1,0:T(2,128)S(1)}, f32[8,2,128]{2,1,0:T(2,128)S(1)}, u32[]{:S(2)}, u32[]{:S(2)}) collective-permute-start(f32[8,2,128]{2,1,0:T(2,128)S(1)} %get-tuple-element.32), channel_id=1, source_target_pairs={{0,1},{1,2},{2,3},{4,5},{5,6},{6,7},{8,9},{9,10},{10,11},{12,13},{... | collective-permute-start | bytes 24584 | tf_op jit(solution)/shard_map/ppermute | solution.py:19
  219.8 7.4 %collective-permute-start.29 = (f32[8,2,128]{2,1,0:T(2,128)S(1)}, f32[8,2,128]{2,1,0:T(2,128)S(1)}, u32[]{:S(2)}, u32[]{:S(2)}) collective-permute-start(f32[8,2,128]{2,1,0:T(2,128)S(1)} %get-tuple-element.33), channel_id=1, source_target_pairs={{1,0},{2,1},{3,2},{5,4},{6,5},{7,6},{9,8},{10,9},{11,10},{13,12},{... | collective-permute-start | bytes 24584 | tf_op jit(solution)/shard_map/ppermute | solution.py:22
  227.6 5.3 %collective-permute-start.31 = (f32[1,16,128]{2,1,0:T(8,128)S(1)}, f32[1,16,128]{2,1,0:T(8,128)S(1)}, u32[]{:S(2)}, u32[]{:S(2)}) collective-permute-start(f32[1,16,128]{2,1,0:T(8,128)S(1)} %get-tuple-element.59), channel_id=1, source_target_pairs={{0,4},{4,8},{8,12},{12,16},{16,20},{20,24},{24,28},{28,32},{32,36}... | collective-permute-start | bytes 24584 | tf_op jit(solution)/shard_map/ppermute | solution.py:19
  230.9 9.2 %collective-permute-start.30 = (f32[1,16,128]{2,1,0:T(8,128)S(1)}, f32[1,16,128]{2,1,0:T(8,128)S(1)}, u32[]{:S(2)}, u32[]{:S(2)}) collective-permute-start(f32[1,16,128]{2,1,0:T(8,128)S(1)} %get-tuple-element.60), channel_id=1, source_target_pairs={{4,0},{8,4},{12,8},{16,12},{20,16},{24,20},{28,24},{32,28},{36,32}... | collective-permute-start | bytes 24584 | tf_op jit(solution)/shard_map/ppermute | solution.py:22
  240.1 8.3 %collective-permute-start.32 = (f32[6,1,128]{2,1,0:T(1,128)S(1)}, f32[6,1,128]{2,1,0:T(1,128)S(1)}, u32[]{:S(2)}, u32[]{:S(2)}) collective-permute-start(f32[6,1,128]{2,1,0:T(1,128)S(1)} %get-tuple-element.40), channel_id=1, source_target_pairs={{1,0},{2,1},{3,2},{5,4},{6,5},{7,6},{9,8},{10,9},{11,10},{13,12},{... | collective-permute-start | bytes 9224 | tf_op jit(solution)/shard_map/ppermute | solution.py:22
  241.4 7.7 %collective-permute-start.33 = (f32[6,1,128]{2,1,0:T(1,128)S(1)}, f32[6,1,128]{2,1,0:T(1,128)S(1)}, u32[]{:S(2)}, u32[]{:S(2)}) collective-permute-start(f32[6,1,128]{2,1,0:T(1,128)S(1)} %get-tuple-element.41), channel_id=1, source_target_pairs={{0,1},{1,2},{2,3},{4,5},{5,6},{6,7},{8,9},{9,10},{10,11},{12,13},{... | collective-permute-start | bytes 9224 | tf_op jit(solution)/shard_map/ppermute | solution.py:19
  270.7 6.7 %collective-permute-start.35 = (f32[1,32,64]{2,1,0:T(8,128)S(1)}, f32[1,32,64]{2,1,0:T(8,128)S(1)}, u32[]{:S(2)}, u32[]{:S(2)}) collective-permute-start(f32[1,32,64]{2,1,0:T(8,128)S(1)} %get-tuple-element.57), channel_id=1, source_target_pairs={{0,4},{4,8},{8,12},{12,16},{16,20},{20,24},{24,28},{28,32},{32,36}... | collective-permute-start | bytes 24584 | tf_op jit(solution)/shard_map/ppermute | solution.py:19
  275.5 9.3 %collective-permute-start.34 = (f32[1,32,64]{2,1,0:T(8,128)S(1)}, f32[1,32,64]{2,1,0:T(8,128)S(1)}, u32[]{:S(2)}, u32[]{:S(2)}) collective-permute-start(f32[1,32,64]{2,1,0:T(8,128)S(1)} %get-tuple-element.58), channel_id=1, source_target_pairs={{4,0},{8,4},{12,8},{16,12},{20,16},{24,20},{28,24},{32,28},{36,32}... | collective-permute-start | bytes 24584 | tf_op jit(solution)/shard_map/ppermute | solution.py:22
  285.0 4.3 %collective-permute-start.37 = (f32[1,32,64]{2,1,0:T(8,128)S(1)}, f32[1,32,64]{2,1,0:T(8,128)S(1)}, u32[]{:S(2)}, u32[]{:S(2)}) collective-permute-start(f32[1,32,64]{2,1,0:T(8,128)S(1)} %get-tuple-element.55), channel_id=1, source_target_pairs={{0,4},{4,8},{8,12},{12,16},{16,20},{20,24},{24,28},{28,32},{32,36}... | collective-permute-start | bytes 24584 | tf_op jit(solution)/shard_map/ppermute | solution.py:19
  286.9 9.3 %collective-permute-start.36 = (f32[1,32,64]{2,1,0:T(8,128)S(1)}, f32[1,32,64]{2,1,0:T(8,128)S(1)}, u32[]{:S(2)}, u32[]{:S(2)}) collective-permute-start(f32[1,32,64]{2,1,0:T(8,128)S(1)} %get-tuple-element.56), channel_id=1, source_target_pairs={{4,0},{8,4},{12,8},{16,12},{20,16},{24,20},{28,24},{32,28},{36,32}... | collective-permute-start | bytes 24584 | tf_op jit(solution)/shard_map/ppermute | solution.py:22
  296.3 4.5 %collective-permute-start.39 = (f32[1,32,64]{2,1,0:T(8,128)S(1)}, f32[1,32,64]{2,1,0:T(8,128)S(1)}, u32[]{:S(2)}, u32[]{:S(2)}) collective-permute-start(f32[1,32,64]{2,1,0:T(8,128)S(1)} %get-tuple-element.53), channel_id=1, source_target_pairs={{0,4},{4,8},{8,12},{12,16},{16,20},{20,24},{24,28},{28,32},{32,36}... | collective-permute-start | bytes 24584 | tf_op jit(solution)/shard_map/ppermute | solution.py:19
  298.3 9.3 %collective-permute-start.38 = (f32[1,32,64]{2,1,0:T(8,128)S(1)}, f32[1,32,64]{2,1,0:T(8,128)S(1)}, u32[]{:S(2)}, u32[]{:S(2)}) collective-permute-start(f32[1,32,64]{2,1,0:T(8,128)S(1)} %get-tuple-element.54), channel_id=1, source_target_pairs={{4,0},{8,4},{12,8},{16,12},{20,16},{24,20},{28,24},{32,28},{36,32}... | collective-permute-start | bytes 24584 | tf_op jit(solution)/shard_map/ppermute | solution.py:22
  310.0 4.3 %collective-permute-start.40 = (f32[2,16,128]{2,1,0:T(8,128)S(1)}, f32[2,16,128]{2,1,0:T(8,128)S(1)}, u32[]{:S(2)}, u32[]{:S(2)}) collective-permute-start(f32[2,16,128]{2,1,0:T(8,128)S(1)} %get-tuple-element.48), channel_id=1, source_target_pairs={{0,4},{4,8},{8,12},{12,16},{16,20},{20,24},{24,28},{28,32},{32,36}... | collective-permute-start | bytes 49160 | tf_op jit(solution)/shard_map/ppermute | solution.py:19
  311.9 9.3 %collective-permute-start.41 = (f32[2,16,128]{2,1,0:T(8,128)S(1)}, f32[2,16,128]{2,1,0:T(8,128)S(1)}, u32[]{:S(2)}, u32[]{:S(2)}) collective-permute-start(f32[2,16,128]{2,1,0:T(8,128)S(1)} %get-tuple-element.49), channel_id=1, source_target_pairs={{4,0},{8,4},{12,8},{16,12},{20,16},{24,20},{28,24},{32,28},{36,32}... | collective-permute-start | bytes 49160 | tf_op jit(solution)/shard_map/ppermute | solution.py:22
  324.0 8.1 %collective-permute-start.43 = (f32[8,2,128]{2,1,0:T(2,128)S(1)}, f32[8,2,128]{2,1,0:T(2,128)S(1)}, u32[]{:S(2)}, u32[]{:S(2)}) collective-permute-start(f32[8,2,128]{2,1,0:T(2,128)S(1)} %get-tuple-element.31), channel_id=1, source_target_pairs={{1,0},{2,1},{3,2},{5,4},{6,5},{7,6},{9,8},{10,9},{11,10},{13,12},{... | collective-permute-start | bytes 24584 | tf_op jit(solution)/shard_map/ppermute | solution.py:22
  333.3 5.0 %collective-permute-start.44 = (f32[2,16,128]{2,1,0:T(8,128)S(1)}, f32[2,16,128]{2,1,0:T(8,128)S(1)}, u32[]{:S(2)}, u32[]{:S(2)}) collective-permute-start(f32[2,16,128]{2,1,0:T(8,128)S(1)} %get-tuple-element.46), channel_id=1, source_target_pairs={{0,4},{4,8},{8,12},{12,16},{16,20},{20,24},{24,28},{28,32},{32,36}... | collective-permute-start | bytes 49160 | tf_op jit(solution)/shard_map/ppermute | solution.py:19
  336.4 9.3 %collective-permute-start.45 = (f32[2,16,128]{2,1,0:T(8,128)S(1)}, f32[2,16,128]{2,1,0:T(8,128)S(1)}, u32[]{:S(2)}, u32[]{:S(2)}) collective-permute-start(f32[2,16,128]{2,1,0:T(8,128)S(1)} %get-tuple-element.47), channel_id=1, source_target_pairs={{4,0},{8,4},{12,8},{16,12},{20,16},{24,20},{28,24},{32,28},{36,32}... | collective-permute-start | bytes 49160 | tf_op jit(solution)/shard_map/ppermute | solution.py:22
  345.7 8.0 %collective-permute-start.46 = (f32[8,2,128]{2,1,0:T(2,128)S(1)}, f32[8,2,128]{2,1,0:T(2,128)S(1)}, u32[]{:S(2)}, u32[]{:S(2)}) collective-permute-start(f32[8,2,128]{2,1,0:T(2,128)S(1)} %get-tuple-element.28), channel_id=1, source_target_pairs={{0,1},{1,2},{2,3},{4,5},{5,6},{6,7},{8,9},{9,10},{10,11},{12,13},{... | collective-permute-start | bytes 24584 | tf_op jit(solution)/shard_map/ppermute | solution.py:19
  352.3 7.4 %collective-permute-start.47 = (f32[8,2,128]{2,1,0:T(2,128)S(1)}, f32[8,2,128]{2,1,0:T(2,128)S(1)}, u32[]{:S(2)}, u32[]{:S(2)}) collective-permute-start(f32[8,2,128]{2,1,0:T(2,128)S(1)} %get-tuple-element.29), channel_id=1, source_target_pairs={{1,0},{2,1},{3,2},{5,4},{6,5},{7,6},{9,8},{10,9},{11,10},{13,12},{... | collective-permute-start | bytes 24584 | tf_op jit(solution)/shard_map/ppermute | solution.py:22
  (24 other events, 370.2 us)
where the time goes:
time: 365 us; the launch traced here: 363 us
  starting transfers between devices  183 us (50%)
  waiting for transfers between devices  125 us (34%)
  other arithmetic  21.4 us (6%)
  local copies, waits for them, and re-layouts  17 us (5%)
  blocking collectives  14.8 us (4%)
    ppermute x24, waiting for transfers between devices, with_halo(): lax.ppermute(lax.slice_in_dim(block, 0, width, axis=dim), axis, backward)  116 us
    ppermute x24, starting transfers between devices, with_halo(): lax.ppermute(lax.slice_in_dim(block, block.shape[dim] - width, None, axis...  113 us
    ppermute x24, starting transfers between devices, with_halo(): lax.ppermute(lax.slice_in_dim(block, 0, width, axis=dim), axis, backward)  45.3 us
    all_to_all x2, starting transfers between devices, sent_to_all(): return lax.all_to_all(copies, axis, split_axis=0, concat_axis=0, tiled=True)  24.5 us
    all_to_all x1, blocking collectives, sent_to_all(): return lax.all_to_all(copies, axis, split_axis=0, concat_axis=0, tiled=True)  14.8 us
    all_to_all x2, waiting for transfers between devices, sent_to_all(): return lax.all_to_all(copies, axis, split_axis=0, concat_axis=0, tiled=True)  8.27 us
    reshape x3, local copies, waits for them, and re-layouts, restrict(): field.reshape(cells_x // 2, 2, cells_y // 2, 2, cells_z // 2, 2)  7.75 us
  transfers between devices with their start and end apart: 50, of which 20 were waited for; matrix products, arithmetic and copies ran while one was open for 3% of the time, Pallas kernels for 0%

commit v1 on v0

v1 whole, which is shorter than its diff:
```python
import functools

import jax
import jax.numpy as jnp
from jax import lax
from jax.experimental import pallas as pl
from jax.experimental.pallas import tpu as pltpu
from jax.sharding import PartitionSpec as P

INTERPRET = False
ROWS = 64
LANES = 128
BLOCK = 16
SPECIES = 9
EDGE = 160
damping = 0.8
time_step = 0.25


class Place:
    def __init__(self, counter, constant):
        self.counter = counter
        self.constant = constant

    def __add__(self, other):
        return Place(self.counter, self.constant + other)

    def __sub__(self, other):
        return Place(self.counter, self.constant - other)

    def __rmul__(self, factor):
        return Place(self.counter * factor, self.constant * factor)

    def index(self, shift=None):
        start = self.counter if shift is None else self.counter + shift
        return start + self.constant if self.constant else start


def loop(low, high, body):
    def step(i, carry):
        body(Place(i, low))
        return carry

    lax.fori_loop(0, high - low, step, 0)


def rows_of(shape):
    return lax.broadcasted_iota(jnp.int32, shape, 0)


def lanes_of(shape):
    return lax.broadcasted_iota(jnp.int32, shape, 1)


PLANE = (ROWS, LANES)


def roll_rows(x, by):
    return pltpu.roll(x, by % x.shape[0], 0)


def roll_lanes(x, by):
    return pltpu.roll(x, by % x.shape[1], 1)


class Weights:
    def __init__(self, ref, step):
        self.ref = ref
        self.step = step

    def fill(self, low, high, mobile, target, inside, scale):
        s = self.step
        row, lane = rows_of(PLANE), lanes_of(PLANE)
        y_low, y_high = row >= s, row < ROWS - s
        z_low, z_high = lane >= s, lane < LANES - s

        def body(i):
            m = mobile(i)
            x_m, x_p = mobile(i - 1), mobile(i + 1)
            y_m = jnp.where(y_low, roll_rows(m, s), 0.0)
            y_p = jnp.where(y_high, roll_rows(m, -s), 0.0)
            z_m = jnp.where(z_low, roll_lanes(m, s), 0.0)
            z_p = jnp.where(z_high, roll_lanes(m, -s), 0.0)
            diagonal = 3.0 * m + 0.5 * ((x_m + x_p) + (y_m + y_p) + (z_m + z_p))
            valid = inside(i)
            scaled = (damping * valid) / (diagonal + (1.0 - valid))
            half = 0.5 * scaled
            k = (i - low).index()
            self.ref[0, k] = (m + x_m) * half
            self.ref[1, k] = (m + x_p) * half
            self.ref[2, k] = jnp.where(y_low, (m + y_m) * half, 0.0)
            self.ref[3, k] = jnp.where(y_high, (m + y_p) * half, 0.0)
            self.ref[4, k] = jnp.where(z_low, (m + z_m) * half, 0.0)
            self.ref[5, k] = jnp.where(z_high, (m + z_p) * half, 0.0)
            self.ref[6, k] = target(i) * scaled * scale
            self.ref[7, k] = diagonal * (1.0 / damping)

        self.low = low
        loop(low, high, body)

    def change(self, field, i):
        s = self.step
        k = (i - self.low).index()
        p = field(i)
        total = self.ref[0, k] * field(i - 1) + self.ref[1, k] * field(i + 1)
        total = total + (self.ref[2, k] * roll_rows(p, s) + self.ref[3, k] * roll_rows(p, -s))
        total = total + (self.ref[4, k] * roll_lanes(p, s) + self.ref[5, k] * roll_lanes(p, -s))
        return p, (total - self.ref[6, k]) - damping * p


def at(ref, origin):
    return lambda i: ref[(i - origin).index()]


def sweep(weights, source, source_low, result, result_low, low, high):
    def body(i):
        p, change = weights.change(at(source, source_low), i)
        result[(i - result_low).index()] = p + change

    loop(low, high, body)


def first_sweep(weights, result, result_low, low, high):
    def body(i):
        result[(i - result_low).index()] = -weights.ref[6, (i - weights.low).index()]

    loop(low, high, body)


def pair_sum(q):
    row, lane = rows_of(PLANE), lanes_of(PLANE)
    q = q + jnp.where(lane % 2 == 0, roll_lanes(q, -1), roll_lanes(q, 1))
    return q + jnp.where(row % 2 == 0, roll_rows(q, -1), roll_rows(q, 1))


def packed(a, b, c, d):
    row, lane = rows_of(PLANE), lanes_of(PLANE)
    even = lane % 2 == 0
    return jnp.where(row % 2 == 0, jnp.where(even, a, b), jnp.where(even, c, d))


def unpacked(v):
    row, lane = rows_of(PLANE), lanes_of(PLANE)
    even, upper = lane % 2 == 0, row % 2 == 0
    first = jnp.where(even, v, roll_lanes(v, 1))
    second = jnp.where(even, roll_lanes(v, -1), v)

    def low_row(x):
        return jnp.where(upper, x, roll_rows(x, 1))

    def high_row(x):
        return jnp.where(upper, roll_rows(x, -1), x)

    return low_row(first), low_row(second), high_row(first), high_row(second)


def residual_planes(weights, field_ref, field_low, result, result_low, low, high):
    def body(i):
        field = at(field_ref, field_low)
        total = 0.0
        for half in range(2):
            _, change = weights.change(field, 2 * i + half)
            total = total - change * weights.ref[7, (2 * i + half - weights.low).index()]
        result[(i - result_low).index()] = 0.125 * pair_sum(total)

    loop(low, high, body)


def inside_of(first, count):
    def inside(i):
        place = i.index(first)
        return jnp.where((place >= 0) & (place < count), 1.0, 0.0)

    return inside


def bounded(place, k, count):
    return jnp.minimum(jnp.maximum(place[k], 0), count - 1)


def prepare(velocity, density, source, species, out):
    lane = lanes_of((BLOCK, LANES))
    row = rows_of((BLOCK, LANES))
    for x in range(4):
        out[BLOCK * x : BLOCK * (x + 1)] = 1.0 / density[x]
        u_p = velocity[0, x + 1] if x < 3 else 0.0
        u_m = velocity[0, x - 1] if x > 0 else 0.0
        v, w = velocity[1, x], velocity[2, x]
        v_p = jnp.where(row < BLOCK - 1, roll_rows(v, -1), 0.0)
        v_m = jnp.where(row > 0, roll_rows(v, 1), 0.0)
        w_p = jnp.where(lane < LANES - 1, roll_lanes(w, -1), 0.0)
        w_m = jnp.where(lane > 0, roll_lanes(w, 1), 0.0)
        moved = 0.5 * ((u_p - u_m) + (v_p - v_m) + (w_p - w_m))
        out[64 + BLOCK * x : 64 + BLOCK * (x + 1)] = moved - source[x]
        for s in range(SPECIES):
            r = EDGE + 4 * s + x
            out[r : r + 1] = species[s, x, 0:1]
            out[r + 36 : r + 37] = species[s, x, BLOCK - 1 : BLOCK]
        r = EDGE + 72 + x
        out[r : r + 1] = velocity[1, x, 0:1]
        out[r + 4 : r + 5] = velocity[1, x, BLOCK - 1 : BLOCK]
    out[128:144] = velocity[0, 0]
    out[144:160] = velocity[0, 3]


def assemble(place, gathered, mobile, target, edge, sent):
    north = place[0] == 0
    row = rows_of((BLOCK, LANES))
    for c in range(4):
        rows = slice(BLOCK * c, BLOCK * (c + 1))
        for k in range(2):
            block = 2 * c + k
            for x in range(4):
                mobile[4 * k + x, rows] = gathered[block, BLOCK * x : BLOCK * (x + 1)]
                t = gathered[block, 64 + BLOCK * x : 64 + BLOCK * (x + 1)]
                r = EDGE + 72 + x
                if c > 0:
                    t = t - jnp.where(row == 0, 0.5 * gathered[block - 2, r + 4 : r + 5], 0.0)
                if c < 3:
                    t = t + jnp.where(row == BLOCK - 1, 0.5 * gathered[block + 2, r : r + 1], 0.0)
                if k == 0 and x == 3:
                    t = t + 0.5 * gathered[block + 1, 128:144]
                if k == 1 and x == 0:
                    t = t - 0.5 * gathered[block - 1, 144:160]
                target[4 * k + x, rows] = t
        edge[0, rows] = gathered[2 * c, 128:144]
        edge[1, rows] = gathered[2 * c + 1, 144:160]
    one, two = jnp.where(north, 0, 1), jnp.where(north, 0, 2)
    for i in range(7):
        sent[i] = mobile[one + i]
    for i in range(6):
        sent[7 + i] = target[two + i]
    sent[13] = edge[one]


def first_cycle(
    n_chips, place, mobile, target, edge, got, swapped, species,
    mobile_w, target_w, pressure, residual, coarse, sent, rim,
    weights_ref, field,
):
    north, chip = place[0] == 0, bounded(place, 2, n_chips)

    def sides(i):
        a, b = got[i], swapped[i]
        return jnp.where(north, a, b), jnp.where(north, b, a)

    def copy_mobile(i):
        left, right = sides(i.index())
        mobile_w[i.index()] = left
        mobile_w[(i + 15).index()] = right

    loop(0, 7, copy_mobile)

    def copy_block(i):
        mobile_w[(i + 7).index()] = mobile[i.index()]
        target_w[(i + 6).index()] = target[i.index()]

    loop(0, 8, copy_block)

    def copy_target(i):
        left, right = sides((i + 7).index())
        target_w[i.index()] = left
        target_w[(i + 14).index()] = right

    loop(0, 6, copy_target)
    left, right = sides(13)
    target_w[5] = target_w[5] + 0.5 * edge[0]
    target_w[6] = target_w[6] - 0.5 * left
    target_w[13] = target_w[13] + 0.5 * right
    target_w[14] = target_w[14] - 0.5 * edge[1]

    weights = Weights(weights_ref, 1)
    weights.fill(-6, 14, at(mobile_w, -7), at(target_w, -6), inside_of(8 * chip, 8 * n_chips), 1.0)
    first_sweep(weights, field, -6, -6, 14)
    sweep(weights, field, -6, pressure, -5, -5, 13)
    residual_planes(weights, pressure, -5, residual, -2, -2, 6)

    def restrict(i):
        first, second = mobile_w[(2 * i + 1).index()], mobile_w[(2 * i + 2).index()]
        coarse[i.index()] = 0.125 * pair_sum(first + second)

    loop(0, 10, restrict)
    r = jnp.where(north, 4, 0)
    sent[0:64] = packed(residual[r], residual[r + 1], residual[r + 2], residual[r + 3])
    m = jnp.where(north, 6, 0)
    sent[64:128] = packed(coarse[m], coarse[m + 1], coarse[m + 2], coarse[m + 3])
    for s in range(SPECIES):
        sent[128 + BLOCK * s : 144 + BLOCK * s] = species[s, jnp.where(north, 0, 3)]
        rim[BLOCK * s : BLOCK * (s + 1)] = species[s, jnp.where(north, 3, 0)]


def coarse_sweeps(weights, one, two, low, high, origin):
    first_sweep(weights, one, origin, low, high)
    sweep(weights, one, origin, two, origin, low + 1, high - 1)
    sweep(weights, two, origin, one, origin, low + 2, high - 2)
    sweep(weights, one, origin, two, origin, low + 3, high - 3)


def second_cycle(
    n_chips, place, mobile_w, target_w, pressure, residual, coarse, got, swapped,
    pressure_new, residual_new, coarse_w, sent, sent_far,
    weights_ref, coarse_ref, residual_w, one, two, field, other,
):
    north, chip = place[0] == 0, bounded(place, 2, n_chips)

    def sides(low):
        a, b = got[low : low + 64], swapped[low : low + 64]
        return unpacked(jnp.where(north, a, b)), unpacked(jnp.where(north, b, a))

    left, right = sides(0)
    for i in range(4):
        residual_w[i] = left[i]
        residual_w[12 + i] = right[i]
    left, right = sides(64)
    for i in range(4):
        coarse_w[i] = left[i]
        coarse_w[14 + i] = right[i]

    def copy_residual(i):
        residual_w[(i + 4).index()] = residual[i.index()]

    def copy_coarse(i):
        coarse_w[(i + 4).index()] = coarse[i.index()]

    loop(0, 8, copy_residual)
    loop(0, 10, copy_coarse)

    coarse_weights = Weights(coarse_ref, 2)
    coarse_weights.fill(
        -6, 10, at(coarse_w, -7), at(residual_w, -6), inside_of(4 * chip, 4 * n_chips), 4.0
    )
    coarse_sweeps(coarse_weights, one, two, -6, 10, -6)

    def prolong(i):
        correction = two[(i + 3).index()]
        for half in range(2):
            k = (2 * i + half).index()
            field[k] = field[k] + correction

    def copy_pressure(i):
        field[(i + 1).index()] = pressure[i.index()]

    field[0] = jnp.zeros(PLANE, jnp.float32)
    field[19] = jnp.zeros(PLANE, jnp.float32)
    loop(0, 18, copy_pressure)
    loop(0, 10, prolong)

    weights = Weights(weights_ref, 1)
    weights.fill(-4, 12, at(mobile_w, -7), at(target_w, -6), inside_of(8 * chip, 8 * n_chips), 1.0)
    sweep(weights, field, -6, other, -6, -4, 12)
    sweep(weights, other, -6, field, -6, -3, 11)
    sweep(weights, field, -6, other, -6, -2, 10)
    sweep(weights, other, -6, pressure_new, -1, -1, 9)
    residual_planes(weights, pressure_new, -1, residual_new, 0, 0, 4)
    for i in range(3):
        sent[i] = pressure_new[jnp.where(north, 2, 5) + i]
    sent[3] = packed(residual_new[0], residual_new[1], residual_new[2], residual_new[3])
    sent_far[...] = residual_new[jnp.where(north, 0, 3)]


def finish(
    n_chips, place, mobile_w, target_w, pressure, residual, coarse_w, got, far, swapped,
    gathered, velocity, species, near_rims, swapped_rims,
    velocity_out, pressure_out, species_out,
    weights_ref, coarse_ref, residual_w, pressure_w, one, two, field, other, mobile_pad, final_pad,
):
    north, cross, chip = place[0] == 0, bounded(place, 1, 4), bounded(place, 2, n_chips)
    core = jnp.where(north, 0, 1)
    a, b = got[3], swapped[...]
    left, right = unpacked(jnp.where(north, a, b)), unpacked(jnp.where(north, b, a))
    for i in range(4):
        residual_w[1 + i] = left[i]
        residual_w[5 + i] = residual[i]
        residual_w[9 + i] = right[i]
    residual_w[0] = far[...]
    residual_w[13] = far[...]
    for i in range(3):
        pressure_w[i] = got[i]
        pressure_w[13 + i] = got[i]

    def copy_pressure(i):
        pressure_w[(i + 3).index()] = pressure[i.index()]

    loop(0, 10, copy_pressure)

    shift, coarse_shift = jnp.where(north, 0, 4), jnp.where(north, 0, 2)
    coarse_weights = Weights(coarse_ref, 2)
    coarse_weights.fill(
        -5,
        7,
        lambda i: coarse_w[(i + 7).index(coarse_shift)],
        lambda i: residual_w[(i + 5).index(coarse_shift)],
        inside_of(4 * chip + coarse_shift, 4 * n_chips),
        4.0,
    )
    coarse_sweeps(coarse_weights, one, two, -5, 7, -5)

    def prolong(i):
        correction = two[(i + 3).index()]
        for half in range(2):
            k = 2 * i + half
            field[k.index()] = pressure_w[k.index(shift)] + correction

    loop(0, 6, prolong)

    def mobile(i):
        return mobile_w[(i + 7).index(shift)]

    weights = Weights(weights_ref, 1)
    weights.fill(
        -3,
        7,
        mobile,
        lambda i: target_w[(i + 6).index(shift)],
        inside_of(8 * chip + shift, 8 * n_chips),
        1.0,
    )
    sweep(weights, field, -4, other, -4, -3, 7)

    nothing = jnp.zeros((8, LANES), jnp.float32)

    def last(i):
        p, change = weights.change(at(other, -4), i)
        k = (i + 2).index()
        final_pad[k, 0:8] = nothing
        final_pad[k, 8:72] = p + change
        final_pad[k, 72:80] = nothing

    loop(-2, 6, last)

    def pad_mobile(i):
        k = i.index()
        mobile_pad[k, 0:8] = nothing
        mobile_pad[k, 8:72] = mobile(i)
        mobile_pad[k, 72:80] = nothing

    loop(0, 4, pad_mobile)

    start = pl.multiple_of(cross * BLOCK, BLOCK)
    own = pl.ds(start + 8, BLOCK)
    own_in = pl.ds(start, BLOCK)
    row, lane = rows_of((BLOCK, LANES)), lanes_of((BLOCK, LANES))

    partner = gathered[2 * cross + jnp.where(north, 1, 0)]
    beside = jnp.where(north, partner[128:144], partner[144:160])

    outer = near_rims[SPECIES * BLOCK : (SPECIES + 1) * BLOCK]
    u_low = jnp.where(north, outer, beside)
    u_high = jnp.where(north, beside, outer)

    def u_out(x):
        if x < 0:
            u = u_low
        elif x > 3:
            u = u_high
        else:
            u = velocity[0, x]
        slope = 0.5 * (final_pad[x + 3, own] - final_pad[x + 1, own])
        return u - mobile_w[x + 7 + shift, own_in] * slope

    u = [u_out(x) for x in range(-1, 5)]
    below = gathered[2 * jnp.maximum(cross - 1, 0) + core, EDGE:240]
    above = gathered[2 * jnp.minimum(cross + 1, 3) + core, EDGE:240]
    has_below = jnp.where(cross > 0, 1.0, 0.0)
    has_above = jnp.where(cross < 3, 1.0, 0.0)
    wide = pl.ds(start, 32)
    for x in range(4):
        p = final_pad[x + 2, wide]
        m = mobile_pad[x, wide]
        p_own = p[8:24]
        v = velocity[1, x] - m[8:24] * (0.5 * (p[9:25] - p[7:23]))
        v_low = has_below * below[76 + x : 77 + x] - m[7:8] * (0.5 * (p[8:9] - p[6:7]))
        v_high = has_above * above[72 + x : 73 + x] - m[24:25] * (0.5 * (p[25:26] - p[23:24]))
        p_zp = jnp.where(lane < LANES - 1, roll_lanes(p_own, -1), 0.0)
        p_zm = jnp.where(lane > 0, roll_lanes(p_own, 1), 0.0)
        w = velocity[2, x] - m[8:24] * (0.5 * (p_zp - p_zm))
        velocity_out[0, x] = u[x + 1]
        velocity_out[1, x] = v
        velocity_out[2, x] = w
        pressure_out[x] = p_own

        flow_xm, flow_xp = 0.5 * (u[x] + u[x + 1]), 0.5 * (u[x + 1] + u[x + 2])
        v_m = jnp.where(row == 0, v_low, roll_rows(v, 1))
        v_p = jnp.where(row == BLOCK - 1, v_high, roll_rows(v, -1))
        flow_ym, flow_yp = 0.5 * (v_m + v), 0.5 * (v + v_p)
        w_m = jnp.where(lane > 0, roll_lanes(w, 1), 0.0)
        w_p = jnp.where(lane < LANES - 1, roll_lanes(w, -1), 0.0)
        flow_zm, flow_zp = 0.5 * (w_m + w), 0.5 * (w + w_p)

        def leaves(high, low):
            return jnp.maximum(high, 0.0) - jnp.minimum(low, 0.0)

        keep = 1.0 - time_step * (
            leaves(flow_xp, flow_xm) + leaves(flow_yp, flow_ym) + leaves(flow_zp, flow_zm)
        )
        from_xm, from_xp = (
            time_step * jnp.maximum(flow_xm, 0.0),
            -time_step * jnp.minimum(flow_xp, 0.0),
        )
        from_ym, from_yp = (
            time_step * jnp.maximum(flow_ym, 0.0),
            -time_step * jnp.minimum(flow_yp, 0.0),
        )
        from_zm = jnp.where(lane > 0, time_step * jnp.maximum(flow_zm, 0.0), 0.0)
        from_zp = jnp.where(lane < LANES - 1, -time_step * jnp.minimum(flow_zp, 0.0), 0.0)
        for s in range(SPECIES):
            c = species[s, x]
            rim = slice(BLOCK * s, BLOCK * (s + 1))
            if x > 0:
                c_xm = species[s, x - 1]
            else:
                c_xm = jnp.where(north, near_rims[rim], swapped_rims[rim])
            if x < 3:
                c_xp = species[s, x + 1]
            else:
                c_xp = jnp.where(north, swapped_rims[rim], near_rims[rim])
            r = 4 * s + x
            c_ym = jnp.where(row == 0, has_below * below[36 + r : 37 + r], roll_rows(c, 1))
            c_yp = jnp.where(row == BLOCK - 1, has_above * above[r : r + 1], roll_rows(c, -1))
            total = keep * c + (from_xm * c_xm + from_xp * c_xp)
            total = total + (from_ym * c_ym + from_yp * c_yp)
            total = total + (from_zm * roll_lanes(c, 1) + from_zp * roll_lanes(c, -1))
            species_out[s, x] = total


def call(kernel, outs, scratch, *operands, scalars=True, flops=1000000):
    specs = [pl.BlockSpec(memory_space=pltpu.VMEM) for _ in operands]
    if scalars:
        specs[0] = pl.BlockSpec(memory_space=pltpu.SMEM)
    single = len(outs) == 1
    shapes = [jax.ShapeDtypeStruct(shape, jnp.float32) for shape in outs]
    return pl.pallas_call(
        kernel,
        out_shape=shapes[0] if single else shapes,
        in_specs=specs,
        out_specs=pl.BlockSpec(memory_space=pltpu.VMEM)
        if single
        else [pl.BlockSpec(memory_space=pltpu.VMEM) for _ in outs],
        scratch_shapes=[pltpu.VMEM(shape, jnp.float32) for shape in scratch],
        cost_estimate=pl.CostEstimate(flops=flops, bytes_accessed=1000000, transcendentals=0),
        interpret=INTERPRET,
    )(*operands)


def local(n_chips, velocity, density, source, species):
    slab, cross = lax.axis_index("slab"), lax.axis_index("cross")
    core, chip = slab % 2, slab // 2
    place = jnp.stack([core, cross, chip]).astype(jnp.int32)
    groups = [[(2 * j + k) * 4 + c for c in range(4) for k in range(2)] for j in range(n_chips)]

    def beside(distance):
        pairs = []
        for j in range(n_chips - distance):
            left, right = 2 * j + 1, 2 * (j + distance)
            pairs += [(left, right), (right, left)]
        return pairs

    within = [pair for j in range(n_chips) for pair in ((2 * j, 2 * j + 1), (2 * j + 1, 2 * j))]

    def plane(n):
        return (n, ROWS, LANES)

    own = call(prepare, [(240, LANES)], [], velocity, density, source, species, scalars=False)
    gathered = lax.all_gather(own, ("slab", "cross"), axis_index_groups=groups)
    mobile, target, edge, sent = call(
        assemble, [plane(8), plane(8), plane(2), plane(14)], [], place, gathered
    )
    got = lax.ppermute(sent, "slab", beside(1))
    swapped = lax.ppermute(got, "slab", within)
    edge_rows = lax.dynamic_slice_in_dim(got[13], cross * BLOCK, BLOCK, 0)
    mobile_w, target_w, pressure, residual, coarse, sent, rim = call(
        functools.partial(first_cycle, n_chips),
        [plane(22), plane(20), plane(18), plane(8), plane(10), (272, LANES), (144, LANES)],
        [(8, *plane(20)), plane(20)],
        place, mobile, target, edge, got, swapped, species,
    )
    got = lax.ppermute(sent, "slab", beside(1))
    swapped = lax.ppermute(jnp.concatenate([got[:128], rim], 0), "slab", within)
    near_rims = jnp.concatenate([got[128:], edge_rows], 0)
    swapped_rims = swapped[128:]
    pressure, residual, coarse_w, sent, sent_far = call(
        functools.partial(second_cycle, n_chips),
        [plane(10), plane(4), plane(18), plane(4), PLANE],
        [(8, *plane(16)), (8, *plane(16)), plane(16), plane(16), plane(16), plane(20), plane(20)],
        place, mobile_w, target_w, pressure, residual, coarse, got, swapped,
    )
    got = lax.ppermute(sent, "slab", beside(1))
    far = lax.ppermute(sent_far, "slab", beside(2))
    swapped = lax.ppermute(got[3], "slab", within)
    return call(
        functools.partial(finish, n_chips),
        [velocity.shape, density.shape, species.shape],
        [
            (8, *plane(10)), (8, *plane(12)), plane(14), plane(16), plane(12), plane(12), plane(12),
            plane(12), (4, 80, LANES), (8, 80, LANES),
        ],
        place, mobile_w, target_w, pressure, residual, coarse_w, got, far, swapped,
        gathered, velocity, species, near_rims, swapped_rims,
    )


def solution(mesh):
    n_chips = mesh.shape["slab"] // 2
    block = P("slab", "cross", None)
    stack = P(None, "slab", "cross", None)
    return jax.shard_map(
        lambda *arrays: tuple(local(n_chips, *arrays)),
        mesh=mesh,
        in_specs=(stack, block, block, stack),
        out_specs=(stack, block, stack),
        check_vma=False,
    )
```

time: 365 us -> 126 us (0.35)
  the two profiles are of different devices: /device:TPU:127 before, /device:TPU:256 now
where the time goes in v1:
time: 126 us
  Pallas kernels  38.8 us (31%)
  starting transfers between devices  36.6 us (29%)
  blocking collectives  26 us (21%)
  waiting for transfers between devices  17.6 us (14%)
  local copies, waits for them, and re-layouts  4.84 us (4%)
    pallas_call x5, Pallas kernels, call(): pl.pallas_call(kernel, out_shape=shapes[0] if single else shapes, in_spec...  38.8 us
    ppermute x3, starting transfers between devices, local(): got = lax.ppermute(sent, 'slab', beside(1))  27.7 us
    all_gather x1, blocking collectives, local(): gathered = lax.all_gather(own, ('slab', 'cross'), axis_index_groups=groups)  26 us
    ppermute x3, waiting for transfers between devices, local(): got = lax.ppermute(sent, 'slab', beside(1))  9.3 us
    ppermute x1, waiting for transfers between devices, local(): far = lax.ppermute(sent_far, 'slab', beside(2))  5.18 us
    unnamed x20, local copies, waits for them, and re-layouts  3.42 us
    ppermute x1, starting transfers between devices, local(): far = lax.ppermute(sent_far, 'slab', beside(2))  3.11 us
  transfers between devices with their start and end apart: 7, of which 5 were waited for; matrix products, arithmetic and copies ran while one was open for 2% of the time, Pallas kernels for 0%

profile of v1, /device:TPU:256, one launch (start us, length us, event | category | flops | bytes accessed | tf_op | source)
XLA Modules:
  0.0 125.8 jit_solution(13156696127682192920)
XLA Ops:
  0.7 1.8 %shard_map.67 = f32[240,128]{1,0:T(8,128)} custom-call(f32[3,4,16,128]{3,2,1,0:T(8,128)} %velocity.3, f32[4,16,128]{2,1,0:T(8,128)} %density.1, f32[4,16,128]{2,1,0:T(8,128)} %source.1, f32[9,4,16,128]{3,2,1,0:T(8,128)} %species.5), custom_call_target="tpu_custom_call" | custom-call | flops 1000000 | bytes 1000000 | tf_op jit(solution)/shard_map/pallas_call | solution.py:532
  2.4 26.0 %all-gather = f32[1920,128]{1,0:T(8,128)} all-gather(f32[240,128]{1,0:T(8,128)} %shard_map.67), channel_id=2, replica_groups={{0,4,1,5,2,6,3,7},{8,12,9,13,10,14,11,15},{16,20,17,21,18,22,19,23},{24..., dimensions={0}, use_global_device_ids=true | all-gather | bytes 1105920 | tf_op jit(solution)/shard_map/all_gather | solution.py:564
  28.5 0.6 pad_add_fusion.place
  29.1 2.3 %shard_map.68 = (f32[8,64,128]{2,1,0:T(8,128)}, f32[8,64,128]{2,1,0:T(8,128)}, f32[2,64,128]{2,1,0:T(8,128)}, f32[14,64,128]{2,1,0:T(8,128)}) custom-call(s32[3]{0:T(128)} %pad_add_fusion.place, f32[8,240,128]{2,1,0:T(8,128)} %bitcast.8), custom_call_target="tpu_custom_call" | custom-call | flops 1000000 | bytes 1000000 | tf_op jit(solution)/shard_map/pallas_call | solution.py:532
  31.3 9.5 %collective-permute-start = (f32[14,64,128]{2,1,0:T(8,128)}, f32[14,64,128]{2,1,0:T(8,128)S(1)}, u32[]{:S(2)}, u32[]{:S(2)}) collective-permute-start(f32[14,64,128]{2,1,0:T(8,128)} %get-tuple-element.22), channel_id=1, source_target_pairs={{4,8},{8,4},{12,16},{16,12},{20,24},{24,20},{28,32},{32,28},{36,40... | collective-permute-start | bytes 1376264 | tf_op jit(solution)/shard_map/ppermute | solution.py:568
  40.8 6.4 %collective-permute-done.got = f32[14,64,128]{2,1,0:T(8,128)S(1)} collective-permute-done((f32[14,64,128]{2,1,0:T(8,128)}, f32[14,64,128]{2,1,0:T(8,128)S(1)}, u32[]{:S(2)}, u32[]{:S(2)}) %collective-permute-start) | collective-permute-done | bytes 458784 | tf_op jit(solution)/shard_map/ppermute | solution.py:568
  47.2 0.0 copy-start.1
  47.2 1.9 %collective-permute-start.1 = (f32[14,64,128]{2,1,0:T(8,128)S(1)}, f32[14,64,128]{2,1,0:T(8,128)S(1)}, u32[]{:S(2)}, u32[]{:S(2)}) collective-permute-start(f32[14,64,128]{2,1,0:T(8,128)S(1)} %collective-permute-done.got), channel_id=1, source_target_pairs={{0,4},{4,0},{8,12},{12,8},{16,20},{20,16},{24,28},{28,24},{32,36},... | collective-permute-start | bytes 1376264 | tf_op jit(solution)/shard_map/ppermute | solution.py:569
  49.1 1.8 %collective-permute-done.1.swapped = f32[14,64,128]{2,1,0:T(8,128)S(1)} collective-permute-done((f32[14,64,128]{2,1,0:T(8,128)S(1)}, f32[14,64,128]{2,1,0:T(8,128)S(1)}, u32[]{:S(2)}, u32[]{:S(2)}) %collective-permute-start.1) | collective-permute-done | bytes 458784 | tf_op jit(solution)/shard_map/ppermute | solution.py:569
  50.9 0.0 copy-start.2
  50.9 0.0 copy-done.1
  50.9 0.8 copy-done.2
  51.6 9.4 %shard_map.69 = (f32[22,64,128]{2,1,0:T(8,128)}, f32[20,64,128]{2,1,0:T(8,128)}, f32[18,64,128]{2,1,0:T(8,128)}, f32[8,64,128]{2,1,0:T(8,128)}, f32[10,64,128]{2...) custom-call(s32[3]{0:T(128)} %pad_add_fusion.place, f32[8,64,128]{2,1,0:T(8,128)} %get-tuple-element.19.mobile, ...), custom_call_target="tpu_custom_call" | custom-call | flops 1000000 | bytes 1000000 | tf_op jit(solution)/shard_map/pallas_call | solution.py:532
  61.1 0.0 copy-start.6
  61.1 9.2 %collective-permute-start.2 = (f32[272,128]{1,0:T(8,128)}, f32[272,128]{1,0:T(8,128)S(1)}, u32[]{:S(2)}, u32[]{:S(2)}) collective-permute-start(f32[272,128]{1,0:T(8,128)} %get-tuple-element.28), channel_id=1, source_target_pairs={{4,8},{8,4},{12,16},{16,12},{20,24},{24,20},{28,32},{32,28},{36,40... | collective-permute-start | bytes 417800 | tf_op jit(solution)/shard_map/ppermute | solution.py:577
  70.3 2.9 %collective-permute-done.2.got = f32[272,128]{1,0:T(8,128)S(1)} collective-permute-done((f32[272,128]{1,0:T(8,128)}, f32[272,128]{1,0:T(8,128)S(1)}, u32[]{:S(2)}, u32[]{:S(2)}) %collective-permute-start.2) | collective-permute-done | bytes 139296 | tf_op jit(solution)/shard_map/ppermute | solution.py:577
  73.2 0.0 copy-start
  73.2 0.0 copy-done.6
  73.3 0.6 copy-done
  73.9 1.9 %collective-permute-start.3 = (f32[272,128]{1,0:T(8,128)S(1)}, f32[272,128]{1,0:T(8,128)S(1)}, u32[]{:S(2)}, u32[]{:S(2)}) collective-permute-start(f32[272,128]{1,0:T(8,128)S(1)} %pad_maximum_fusion), channel_id=1, source_target_pairs={{0,4},{4,0},{8,12},{12,8},{16,20},{20,16},{24,28},{28,24},{32,36},... | collective-permute-start | bytes 417800 | tf_op jit(solution)/shard_map/ppermute | solution.py:578
  75.8 1.3 %collective-permute-done.3.swapped = f32[272,128]{1,0:T(8,128)S(1)} collective-permute-done((f32[272,128]{1,0:T(8,128)S(1)}, f32[272,128]{1,0:T(8,128)S(1)}, u32[]{:S(2)}, u32[]{:S(2)}) %collective-permute-start.3) | collective-permute-done | bytes 139296 | tf_op jit(solution)/shard_map/ppermute | solution.py:578
  77.1 0.0 copy-start.3
  77.1 0.7 copy-done.3
  77.8 15.5 %shard_map.70 = (f32[10,64,128]{2,1,0:T(8,128)}, f32[4,64,128]{2,1,0:T(8,128)}, f32[18,64,128]{2,1,0:T(8,128)}, f32[4,64,128]{2,1,0:T(8,128)}, f32[64,128]{1,0:T(8,128)}) custom-call(s32[3]{0:T(128)} %pad_add_fusion.place, f32[22,64,128]{2,1,0:T(8,128)} %get-tuple-element.23.mobile_w, f32[20,64,128]{2,1,0:T(8,128)} %get-tuple-element.24.target_w, ...), custom_call_target="tpu_custom_call" | custom-call | flops 1000000 | bytes 1000000 | tf_op jit(solution)/shard_map/pallas_call | solution.py:532
  93.3 9.1 %collective-permute-start.4 = (f32[4,64,128]{2,1,0:T(8,128)}, f32[4,64,128]{2,1,0:T(8,128)S(1)}, u32[]{:S(2)}, u32[]{:S(2)}) collective-permute-start(f32[4,64,128]{2,1,0:T(8,128)} %get-tuple-element.33), channel_id=1, source_target_pairs={{4,8},{8,4},{12,16},{16,12},{20,24},{24,20},{28,32},{32,28},{36,40... | collective-permute-start | bytes 393224 | tf_op jit(solution)/shard_map/ppermute | solution.py:587
  102.3 0.8 slice.23
  103.1 0.0 copy-start.9
  103.1 0.0 slice-start
  103.1 0.0 copy-start.4
  103.1 0.7 copy-done.9
  103.9 3.1 %collective-permute-start.5 = (f32[64,128]{1,0:T(8,128)S(1)}, f32[64,128]{1,0:T(8,128)S(1)}, u32[]{:S(2)}, u32[]{:S(2)}) collective-permute-start(f32[64,128]{1,0:T(8,128)S(1)} %copy-done.9), channel_id=1, source_target_pairs={{4,16},{16,4},{12,24},{24,12},{20,32},{32,20},{28,40},{40,28},{36,... | collective-permute-start | bytes 98312 | tf_op jit(solution)/shard_map/ppermute | solution.py:588
  107.0 0.0 collective-permute-done.4.got
  107.0 0.0 copy-start.5
  107.0 1.9 %collective-permute-start.6 = (f32[64,128]{1,0:T(8,128)S(1)}, f32[64,128]{1,0:T(8,128)S(1)}, u32[]{:S(2)}, u32[]{:S(2)}) collective-permute-start(f32[64,128]{1,0:T(8,128)S(1)} %slice_bitcast_fusion), channel_id=1, source_target_pairs={{0,4},{4,0},{8,12},{12,8},{16,20},{20,16},{24,28},{28,24},{32,36},... | collective-permute-start | bytes 98312 | tf_op jit(solution)/shard_map/ppermute | solution.py:589
  108.9 0.0 slice-done
  109.0 0.6 pad_maximum_fusion.1.near_rims
  109.6 0.0 copy-done.4
  109.6 0.6 slice.24.swapped_rims
  110.2 0.0 copy-done.5
  110.2 5.2 %collective-permute-done.5.far = f32[64,128]{1,0:T(8,128)S(1)} collective-permute-done((f32[64,128]{1,0:T(8,128)S(1)}, f32[64,128]{1,0:T(8,128)S(1)}, u32[]{:S(2)}, u32[]{:S(2)}) %collective-permute-start.5) | collective-permute-done | bytes 32800 | tf_op jit(solution)/shard_map/ppermute | solution.py:588
  115.4 0.0 copy-start.7
  115.4 0.0 collective-permute-done.6.swapped
  115.4 0.0 copy-start.8
  115.4 0.6 copy-done.7
  116.0 0.0 copy-done.8
  116.0 9.8 %shard_map.71 = (f32[3,4,16,128]{3,2,1,0:T(8,128)}, f32[4,16,128]{2,1,0:T(8,128)}, f32[9,4,16,128]{3,2,1,0:T(8,128)}) custom-call(s32[3]{0:T(128)} %pad_add_fusion.place, f32[22,64,128]{2,1,0:T(8,128)} %get-tuple-element.23.mobile_w, f32[20,64,128]{2,1,0:T(8,128)} %get-tuple-element.24.target_w, f32[10,64,128]{2,1,0:T(8,128)} %get-tuple-element.30.pressure, ...), custom_call_target="tpu_custom_call" | custom-call | flops 1000000 | bytes 1000000 | tf_op jit(solution)/shard_map/pallas_call | solution.py:532
  (4 shorter events, 0.0 us)
Async XLA Ops:
  31.3 15.8 %collective-permute-start = (f32[14,64,128]{2,1,0:T(8,128)}, f32[14,64,128]{2,1,0:T(8,128)S(1)}, u32[]{:S(2)}, u32[]{:S(2)}) collective-permute-start(f32[14,64,128]{2,1,0:T(8,128)} %get-tuple-element.22), channel_id=1, source_target_pairs={{4,8},{8,4},{12,16},{16,12},{20,24},{24,20},{28,32},{32,28},{36,40... | collective-permute-start | bytes 1376264 | tf_op jit(solution)/shard_map/ppermute | solution.py:568
  47.2 3.7 %copy-start.1 = (f32[14,64,128]{2,1,0:T(8,128)}, f32[14,64,128]{2,1,0:T(8,128)S(1)}, u32[]{:S(2)}) copy-start(f32[14,64,128]{2,1,0:T(8,128)S(1)} %collective-permute-done.got) | copy-start | bytes 1376260
  47.2 3.7 %collective-permute-start.1 = (f32[14,64,128]{2,1,0:T(8,128)S(1)}, f32[14,64,128]{2,1,0:T(8,128)S(1)}, u32[]{:S(2)}, u32[]{:S(2)}) collective-permute-start(f32[14,64,128]{2,1,0:T(8,128)S(1)} %collective-permute-done.got), channel_id=1, source_target_pairs={{0,4},{4,0},{8,12},{12,8},{16,20},{20,16},{24,28},{28,24},{32,36},... | collective-permute-start | bytes 1376264 | tf_op jit(solution)/shard_map/ppermute | solution.py:569
  50.9 0.8 copy-start.2
  61.1 12.1 %copy-start.6 = (f32[144,128]{1,0:T(8,128)S(1)}, f32[144,128]{1,0:T(8,128)}, u32[]{:S(2)}) copy-start(f32[144,128]{1,0:T(8,128)} %get-tuple-element.29) | copy-start | bytes 221188
  61.1 12.1 %collective-permute-start.2 = (f32[272,128]{1,0:T(8,128)}, f32[272,128]{1,0:T(8,128)S(1)}, u32[]{:S(2)}, u32[]{:S(2)}) collective-permute-start(f32[272,128]{1,0:T(8,128)} %get-tuple-element.28), channel_id=1, source_target_pairs={{4,8},{8,4},{12,16},{16,12},{20,24},{24,20},{28,32},{32,28},{36,40... | collective-permute-start | bytes 417800 | tf_op jit(solution)/shard_map/ppermute | solution.py:577
  73.2 0.7 copy-start
  73.9 3.2 %collective-permute-start.3 = (f32[272,128]{1,0:T(8,128)S(1)}, f32[272,128]{1,0:T(8,128)S(1)}, u32[]{:S(2)}, u32[]{:S(2)}) collective-permute-start(f32[272,128]{1,0:T(8,128)S(1)} %pad_maximum_fusion), channel_id=1, source_target_pairs={{0,4},{4,0},{8,12},{12,8},{16,20},{20,16},{24,28},{28,24},{32,36},... | collective-permute-start | bytes 417800 | tf_op jit(solution)/shard_map/ppermute | solution.py:578
  77.1 0.7 copy-start.3
  93.3 13.7 %collective-permute-start.4 = (f32[4,64,128]{2,1,0:T(8,128)}, f32[4,64,128]{2,1,0:T(8,128)S(1)}, u32[]{:S(2)}, u32[]{:S(2)}) collective-permute-start(f32[4,64,128]{2,1,0:T(8,128)} %get-tuple-element.33), channel_id=1, source_target_pairs={{4,8},{8,4},{12,16},{16,12},{20,24},{24,20},{28,32},{32,28},{36,40... | collective-permute-start | bytes 393224 | tf_op jit(solution)/shard_map/ppermute | solution.py:587
  103.1 0.8 copy-start.9
  103.1 5.8 %slice-start = ((f32[272,128]{1,0:T(8,128)}), f32[144,128]{1,0:T(8,128)S(1)}, s32[]{:S(2)}) async-start(f32[272,128]{1,0:T(8,128)} %copy-done), calls=%async_computation | async-start | bytes 147456 | tf_op jit(solution)/shard_map/slice | solution.py:579
  103.1 6.5 %copy-start.4 = (f32[272,128]{1,0:T(8,128)S(1)}, f32[272,128]{1,0:T(8,128)}, u32[]{:S(2)}) copy-start(f32[272,128]{1,0:T(8,128)} %copy-done.3) | copy-start | bytes 417796
  103.9 11.6 %collective-permute-start.5 = (f32[64,128]{1,0:T(8,128)S(1)}, f32[64,128]{1,0:T(8,128)S(1)}, u32[]{:S(2)}, u32[]{:S(2)}) collective-permute-start(f32[64,128]{1,0:T(8,128)S(1)} %copy-done.9), channel_id=1, source_target_pairs={{4,16},{16,4},{12,24},{24,12},{20,32},{32,20},{28,40},{40,28},{36,... | collective-permute-start | bytes 98312 | tf_op jit(solution)/shard_map/ppermute | solution.py:588
  107.0 3.2 %copy-start.5 = (f32[4,64,128]{2,1,0:T(8,128)}, f32[4,64,128]{2,1,0:T(8,128)S(1)}, u32[]{:S(2)}) copy-start(f32[4,64,128]{2,1,0:T(8,128)S(1)} %collective-permute-done.4.got) | copy-start | bytes 393220
  107.0 8.4 %collective-permute-start.6 = (f32[64,128]{1,0:T(8,128)S(1)}, f32[64,128]{1,0:T(8,128)S(1)}, u32[]{:S(2)}, u32[]{:S(2)}) collective-permute-start(f32[64,128]{1,0:T(8,128)S(1)} %slice_bitcast_fusion), channel_id=1, source_target_pairs={{0,4},{4,0},{8,12},{12,8},{16,20},{20,16},{24,28},{28,24},{32,36},... | collective-permute-start | bytes 98312 | tf_op jit(solution)/shard_map/ppermute | solution.py:589
  115.4 0.6 copy-start.7
  115.4 0.6 copy-start.8

commit v2 on v1

v2 whole, which is shorter than its diff:
```python
import functools

import jax
import jax.numpy as jnp
from jax import lax
from jax.experimental import pallas as pl
from jax.experimental.pallas import tpu as pltpu
from jax.sharding import PartitionSpec as P

INTERPRET = False
ROWS = 64
LANES = 128
BLOCK = 16
SPECIES = 9
EDGE = 160
damping = 0.8
time_step = 0.25


class Place:
    def __init__(self, counter, constant):
        self.counter = counter
        self.constant = constant

    def __add__(self, other):
        return Place(self.counter, self.constant + other)

    def __sub__(self, other):
        return Place(self.counter, self.constant - other)

    def __rmul__(self, factor):
        return Place(self.counter * factor, self.constant * factor)

    def index(self, shift=None):
        start = self.counter if shift is None else self.counter + shift
        return start + self.constant


def loop(low, high, body):
    count = high - low
    some = next(u for u in (4, 5, 6, 3, 7, 2, 1) if count % u == 0)

    def several(start):
        for u in range(some):
            body(Place(start, low + u))

    def step(i, carry):
        several(i * some)
        return carry

    if count == some:
        several(0)
    else:
        lax.fori_loop(0, count // some, step, 0)


def rows_of(shape):
    return lax.broadcasted_iota(jnp.int32, shape, 0)


def lanes_of(shape):
    return lax.broadcasted_iota(jnp.int32, shape, 1)


PLANE = (ROWS, LANES)


def roll_rows(x, by):
    return pltpu.roll(x, by % x.shape[0], 0)


def roll_lanes(x, by):
    return pltpu.roll(x, by % x.shape[1], 1)


PAD = 8
PADDED = (ROWS + 2 * PAD, LANES)


class Field:
    def __init__(self, ref, low, shift=None):
        self.ref = ref
        self.low = low
        self.shift = shift

    def __call__(self, i, rows=0):
        k = (i - self.low).index(self.shift)
        return self.ref[k, PAD + rows : PAD + rows + ROWS]

    def put(self, i, value):
        self.ref[(i - self.low).index(), PAD : PAD + ROWS] = value


def clear_pads(ref):
    nothing = jnp.zeros((PAD, LANES), jnp.float32)
    for k in range(ref.shape[0]):
        ref[k, 0:PAD] = nothing
        ref[k, PAD + ROWS :] = nothing


class Weights:
    def __init__(self, ref, step):
        self.ref = ref
        self.step = step

    def fill(self, low, high, mobile, target, inside, scale):
        s = self.step
        lane = lanes_of(PLANE)
        z_low, z_high = lane >= s, lane < LANES - s

        def body(i):
            m = mobile(i)
            x_m, x_p = mobile(i - 1), mobile(i + 1)
            y_m, y_p = mobile(i, -s), mobile(i, s)
            z_m = jnp.where(z_low, roll_lanes(m, s), 0.0)
            z_p = jnp.where(z_high, roll_lanes(m, -s), 0.0)
            diagonal = 3.0 * m + 0.5 * ((x_m + x_p) + (y_m + y_p) + (z_m + z_p))
            valid = inside(i)
            scaled = (damping * valid) / (diagonal + (1.0 - valid))
            half = 0.5 * scaled
            k = (i - low).index()
            self.ref[0, k] = (m + x_m) * half
            self.ref[1, k] = (m + x_p) * half
            self.ref[2, k] = (m + y_m) * half
            self.ref[3, k] = (m + y_p) * half
            self.ref[4, k] = jnp.where(z_low, (m + z_m) * half, 0.0)
            self.ref[5, k] = jnp.where(z_high, (m + z_p) * half, 0.0)
            self.ref[6, k] = target(i) * (scaled * scale)
            self.ref[7, k] = diagonal * (1.0 / damping)

        self.low = low
        loop(low, high, body)

    def change(self, field, i):
        s = self.step
        k = (i - self.low).index()
        p = field(i)
        total = self.ref[0, k] * field(i - 1) + self.ref[1, k] * field(i + 1)
        total = total + (self.ref[2, k] * field(i, -s) + self.ref[3, k] * field(i, s))
        total = total + (self.ref[4, k] * roll_lanes(p, s) + self.ref[5, k] * roll_lanes(p, -s))
        return p, (total - self.ref[6, k]) - damping * p


def at(ref, origin, shift=None):
    return lambda i: ref[(i - origin).index(shift)]


def sweep(weights, source, result, low, high):
    def body(i):
        p, change = weights.change(source, i)
        result.put(i, p + change)

    loop(low, high, body)


def first_sweep(weights, result, low, high):
    def body(i):
        result.put(i, -weights.ref[6, (i - weights.low).index()])

    loop(low, high, body)


def pair_sum(q):
    row, lane = rows_of(PLANE), lanes_of(PLANE)
    q = q + jnp.where(lane % 2 == 0, roll_lanes(q, -1), roll_lanes(q, 1))
    return q + jnp.where(row % 2 == 0, roll_rows(q, -1), roll_rows(q, 1))


def packed(a, b, c, d):
    row, lane = rows_of(PLANE), lanes_of(PLANE)
    even = lane % 2 == 0
    return jnp.where(row % 2 == 0, jnp.where(even, a, b), jnp.where(even, c, d))


def unpacked(v):
    row, lane = rows_of(PLANE), lanes_of(PLANE)
    even, upper = lane % 2 == 0, row % 2 == 0
    first = jnp.where(even, v, roll_lanes(v, 1))
    second = jnp.where(even, roll_lanes(v, -1), v)

    def low_row(x):
        return jnp.where(upper, x, roll_rows(x, 1))

    def high_row(x):
        return jnp.where(upper, roll_rows(x, -1), x)

    return low_row(first), low_row(second), high_row(first), high_row(second)


def residual_planes(weights, field, result, result_low, low, high):
    def body(i):
        total = 0.0
        for half in range(2):
            _, change = weights.change(field, 2 * i + half)
            total = total - change * weights.ref[7, (2 * i + half - weights.low).index()]
        result[(i - result_low).index()] = 0.125 * pair_sum(total)

    loop(low, high, body)


def inside_of(first, count):
    def inside(i):
        place = i.index(first)
        return jnp.where((place >= 0) & (place < count), 1.0, 0.0)

    return inside


def whereabouts(n_chips):
    slab, cross = lax.axis_index("slab"), lax.axis_index("cross")
    chip = jnp.minimum(jnp.maximum(slab // 2, 0), n_chips - 1)
    return slab % 2 == 0, jnp.minimum(jnp.maximum(cross, 0), 3), chip


def prepare(velocity, density, source, species, out):
    lane = lanes_of((BLOCK, LANES))
    row = rows_of((BLOCK, LANES))
    for x in range(4):
        out[BLOCK * x : BLOCK * (x + 1)] = 1.0 / density[x]
        u_p = velocity[0, x + 1] if x < 3 else 0.0
        u_m = velocity[0, x - 1] if x > 0 else 0.0
        v, w = velocity[1, x], velocity[2, x]
        v_p = jnp.where(row < BLOCK - 1, roll_rows(v, -1), 0.0)
        v_m = jnp.where(row > 0, roll_rows(v, 1), 0.0)
        w_p = jnp.where(lane < LANES - 1, roll_lanes(w, -1), 0.0)
        w_m = jnp.where(lane > 0, roll_lanes(w, 1), 0.0)
        moved = 0.5 * ((u_p - u_m) + (v_p - v_m) + (w_p - w_m))
        out[64 + BLOCK * x : 64 + BLOCK * (x + 1)] = moved - source[x]
        for s in range(SPECIES):
            r = EDGE + 4 * s + x
            out[r : r + 1] = species[s, x, 0:1]
            out[r + 36 : r + 37] = species[s, x, BLOCK - 1 : BLOCK]
        r = EDGE + 72 + x
        out[r : r + 1] = velocity[1, x, 0:1]
        out[r + 4 : r + 5] = velocity[1, x, BLOCK - 1 : BLOCK]
    out[128:144] = velocity[0, 0]
    out[144:160] = velocity[0, 3]


def assemble(n_chips, gathered, mobile, target, edge, sent):
    north, _, _ = whereabouts(n_chips)
    row = rows_of((BLOCK, LANES))
    for c in range(4):
        rows = slice(BLOCK * c, BLOCK * (c + 1))
        for k in range(2):
            block = 2 * c + k
            for x in range(4):
                mobile[4 * k + x, rows] = gathered[block, BLOCK * x : BLOCK * (x + 1)]
                t = gathered[block, 64 + BLOCK * x : 64 + BLOCK * (x + 1)]
                r = EDGE + 72 + x
                if c > 0:
                    t = t - jnp.where(row == 0, 0.5 * gathered[block - 2, r + 4 : r + 5], 0.0)
                if c < 3:
                    t = t + jnp.where(row == BLOCK - 1, 0.5 * gathered[block + 2, r : r + 1], 0.0)
                if k == 0 and x == 3:
                    t = t + 0.5 * gathered[block + 1, 128:144]
                if k == 1 and x == 0:
                    t = t - 0.5 * gathered[block - 1, 144:160]
                target[4 * k + x, rows] = t
        edge[0, rows] = gathered[2 * c, 128:144]
        edge[1, rows] = gathered[2 * c + 1, 144:160]
    one, two = jnp.where(north, 0, 1), jnp.where(north, 0, 2)
    for i in range(7):
        sent[i] = mobile[one + i]
    for i in range(6):
        sent[7 + i] = target[two + i]
    sent[13] = edge[one]


def first_cycle(
    n_chips, mobile, target, edge, got, swapped, species,
    mobile_ref, target_w, pressure_ref, residual, coarse, outer, sent, rim,
    weights_ref, field_ref,
):
    north, _, chip = whereabouts(n_chips)
    clear_pads(mobile_ref)
    clear_pads(field_ref)
    clear_pads(pressure_ref)
    mobile_w, pressure = Field(mobile_ref, -7), Field(pressure_ref, -6)
    field = Field(field_ref, -6)

    def sides(i):
        a, b = got[i], swapped[i]
        return jnp.where(north, a, b), jnp.where(north, b, a)

    def copy_mobile(i):
        left, right = sides((i + 7).index())
        mobile_w.put(i, left)
        mobile_w.put(i + 15, right)

    loop(-7, 0, copy_mobile)

    def copy_block(i):
        mobile_w.put(i, mobile[i.index()])
        target_w[(i + 6).index()] = target[i.index()]

    loop(0, 8, copy_block)

    def copy_target(i):
        left, right = sides((i + 7).index())
        target_w[i.index()] = left
        target_w[(i + 14).index()] = right

    loop(0, 6, copy_target)
    left, right = sides(13)
    target_w[5] = target_w[5] + 0.5 * edge[0]
    target_w[6] = target_w[6] - 0.5 * left
    target_w[13] = target_w[13] + 0.5 * right
    target_w[14] = target_w[14] - 0.5 * edge[1]
    outer[...] = got[13]

    weights = Weights(weights_ref, 1)
    weights.fill(-6, 14, mobile_w, at(target_w, -6), inside_of(8 * chip, 8 * n_chips), 1.0)
    first_sweep(weights, field, -6, 14)
    sweep(weights, field, pressure, -5, 13)
    residual_planes(weights, pressure, residual, -2, -2, 6)

    def restrict(i):
        pair = mobile_w(2 * i) + mobile_w(2 * i + 1)
        coarse[(i + 3).index()] = 0.125 * pair_sum(pair)

    loop(-3, 7, restrict)
    r = jnp.where(north, 4, 0)
    sent[0:64] = packed(residual[r], residual[r + 1], residual[r + 2], residual[r + 3])
    m = jnp.where(north, 6, 0)
    sent[64:128] = packed(coarse[m], coarse[m + 1], coarse[m + 2], coarse[m + 3])
    near, beside = jnp.where(north, 0, 3), jnp.where(north, 3, 0)
    for s in range(SPECIES):
        sent[128 + BLOCK * s : 144 + BLOCK * s] = species[s, near]
        rim[BLOCK * s : BLOCK * (s + 1)] = species[s, beside]


def coarse_sweeps(weights, one, two, low, high):
    first_sweep(weights, one, low, high)
    sweep(weights, one, two, low + 1, high - 1)
    sweep(weights, two, one, low + 2, high - 2)
    sweep(weights, one, two, low + 3, high - 3)


def second_cycle(
    n_chips, mobile_ref, target_w, pressure_ref, residual, coarse, got, swapped,
    pressure_new_ref, residual_new, coarse_ref, sent, sent_far,
    weights_ref, coarse_weights_ref, residual_w, one_ref, two_ref, field_ref, other_ref,
):
    north, _, chip = whereabouts(n_chips)
    for ref in (pressure_new_ref, coarse_ref, one_ref, two_ref, field_ref, other_ref):
        clear_pads(ref)
    coarse_w, one, two = Field(coarse_ref, -7), Field(one_ref, -6), Field(two_ref, -6)
    field, other = Field(field_ref, -6), Field(other_ref, -6)
    pressure, pressure_new = Field(pressure_ref, -6), Field(pressure_new_ref, -1)

    def sides(low):
        a, b = got[low : low + 64], swapped[low : low + 64]
        return unpacked(jnp.where(north, a, b)), unpacked(jnp.where(north, b, a))

    left, right = sides(0)
    for i in range(4):
        residual_w[i] = left[i]
        residual_w[12 + i] = right[i]
    left, right = sides(64)
    for i in range(4):
        coarse_w.put(Place(0, i - 7), left[i])
        coarse_w.put(Place(0, i + 7), right[i])

    def copy_residual(i):
        residual_w[(i + 4).index()] = residual[i.index()]

    def copy_coarse(i):
        coarse_w.put(i - 3, coarse[i.index()])

    loop(0, 8, copy_residual)
    loop(0, 10, copy_coarse)

    coarse_weights = Weights(coarse_weights_ref, 2)
    coarse_weights.fill(
        -6, 10, coarse_w, at(residual_w, -6), inside_of(4 * chip, 4 * n_chips), 4.0
    )
    coarse_sweeps(coarse_weights, one, two, -6, 10)

    def prolong(i):
        correction = two(i)
        for half in range(2):
            k = 2 * i + half
            field.put(k, pressure(k) + correction)

    loop(-3, 7, prolong)

    weights = Weights(weights_ref, 1)
    weights.fill(
        -4, 12, Field(mobile_ref, -7), at(target_w, -6), inside_of(8 * chip, 8 * n_chips), 1.0
    )
    sweep(weights, field, other, -4, 12)
    sweep(weights, other, field, -3, 11)
    sweep(weights, field, other, -2, 10)
    sweep(weights, other, pressure_new, -1, 9)
    residual_planes(weights, pressure_new, residual_new, 0, 0, 4)
    first = jnp.where(north, 2, 5)
    for i in range(3):
        sent[i] = pressure_new_ref[first + i, PAD : PAD + ROWS]
    sent[3] = packed(residual_new[0], residual_new[1], residual_new[2], residual_new[3])
    sent_far[...] = residual_new[jnp.where(north, 0, 3)]


def finish(
    n_chips, mobile_ref, target_w, pressure, residual, coarse_ref, got, far, swapped,
    gathered, velocity, species, outer, near_rims, swapped_rims,
    velocity_out, pressure_out, species_out,
    weights_ref, coarse_weights_ref, residual_w, pressure_w, one_ref, two_ref, field_ref,
    other_ref, final_pad,
):
    north, cross, chip = whereabouts(n_chips)
    core = jnp.where(north, 0, 1)
    for ref in (one_ref, two_ref, field_ref, other_ref, final_pad):
        clear_pads(ref)
    one, two = Field(one_ref, -5), Field(two_ref, -5)
    field, other, final = Field(field_ref, -4), Field(other_ref, -4), Field(final_pad, -2)
    a, b = got[3], swapped[3]
    left, right = unpacked(jnp.where(north, a, b)), unpacked(jnp.where(north, b, a))
    for i in range(4):
        residual_w[1 + i] = left[i]
        residual_w[5 + i] = residual[i]
        residual_w[9 + i] = right[i]
    residual_w[0] = far[...]
    residual_w[13] = far[...]
    for i in range(3):
        pressure_w[i] = got[i]
        pressure_w[13 + i] = got[i]
    known = Field(pressure, -1)

    def copy_pressure(i):
        pressure_w[(i + 4).index()] = known(i)

    loop(-1, 9, copy_pressure)

    shift, coarse_shift = jnp.where(north, 0, 4), jnp.where(north, 0, 2)
    coarse_weights = Weights(coarse_weights_ref, 2)
    coarse_weights.fill(
        -5,
        7,
        Field(coarse_ref, -7, coarse_shift),
        at(residual_w, -5, coarse_shift),
        inside_of(4 * chip + coarse_shift, 4 * n_chips),
        4.0,
    )
    coarse_sweeps(coarse_weights, one, two, -5, 7)

    def prolong(i):
        correction = two(i)
        for half in range(2):
            k = 2 * i + half
            field.put(k, pressure_w[(k + 4).index(shift)] + correction)

    loop(-2, 4, prolong)

    weights = Weights(weights_ref, 1)
    weights.fill(
        -3,
        7,
        Field(mobile_ref, -7, shift),
        at(target_w, -6, shift),
        inside_of(8 * chip + shift, 8 * n_chips),
        1.0,
    )
    sweep(weights, field, other, -3, 7)
    sweep(weights, other, final, -2, 6)

    start = pl.multiple_of(cross * BLOCK, BLOCK)
    own = pl.ds(start + 8, BLOCK)
    row, lane = rows_of((BLOCK, LANES)), lanes_of((BLOCK, LANES))

    partner = gathered[2 * cross + jnp.where(north, 1, 0)]
    beside = jnp.where(north, partner[128:144], partner[144:160])

    beyond = outer[pl.ds(start, BLOCK)]
    u_low = jnp.where(north, beyond, beside)
    u_high = jnp.where(north, beside, beyond)

    def u_out(x):
        if x < 0:
            u = u_low
        elif x > 3:
            u = u_high
        else:
            u = velocity[0, x]
        slope = 0.5 * (final_pad[x + 3, own] - final_pad[x + 1, own])
        return u - mobile_ref[shift + (x + 7), own] * slope

    u = [u_out(x) for x in range(-1, 5)]
    below = gathered[2 * jnp.maximum(cross - 1, 0) + core, EDGE:240]
    above = gathered[2 * jnp.minimum(cross + 1, 3) + core, EDGE:240]
    has_below = jnp.where(cross > 0, 1.0, 0.0)
    has_above = jnp.where(cross < 3, 1.0, 0.0)
    wide = pl.ds(start, 32)
    for x in range(4):
        p = final_pad[x + 2, wide]
        m = mobile_ref[shift + (x + 7), wide]
        p_own = p[8:24]
        v = velocity[1, x] - m[8:24] * (0.5 * (p[9:25] - p[7:23]))
        v_low = has_below * below[76 + x : 77 + x] - m[7:8] * (0.5 * (p[8:9] - p[6:7]))
        v_high = has_above * above[72 + x : 73 + x] - m[24:25] * (0.5 * (p[25:26] - p[23:24]))
        p_zp = jnp.where(lane < LANES - 1, roll_lanes(p_own, -1), 0.0)
        p_zm = jnp.where(lane > 0, roll_lanes(p_own, 1), 0.0)
        w = velocity[2, x] - m[8:24] * (0.5 * (p_zp - p_zm))
        velocity_out[0, x] = u[x + 1]
        velocity_out[1, x] = v
        velocity_out[2, x] = w
        pressure_out[x] = p_own

        flow_xm, flow_xp = 0.5 * (u[x] + u[x + 1]), 0.5 * (u[x + 1] + u[x + 2])
        v_m = jnp.where(row == 0, v_low, roll_rows(v, 1))
        v_p = jnp.where(row == BLOCK - 1, v_high, roll_rows(v, -1))
        flow_ym, flow_yp = 0.5 * (v_m + v), 0.5 * (v + v_p)
        w_m = jnp.where(lane > 0, roll_lanes(w, 1), 0.0)
        w_p = jnp.where(lane < LANES - 1, roll_lanes(w, -1), 0.0)
        flow_zm, flow_zp = 0.5 * (w_m + w), 0.5 * (w + w_p)

        def leaves(high, low):
            return jnp.maximum(high, 0.0) - jnp.minimum(low, 0.0)

        keep = 1.0 - time_step * (
            leaves(flow_xp, flow_xm) + leaves(flow_yp, flow_ym) + leaves(flow_zp, flow_zm)
        )
        from_xm, from_xp = (
            time_step * jnp.maximum(flow_xm, 0.0),
            -time_step * jnp.minimum(flow_xp, 0.0),
        )
        from_ym, from_yp = (
            time_step * jnp.maximum(flow_ym, 0.0),
            -time_step * jnp.minimum(flow_yp, 0.0),
        )
        from_zm = jnp.where(lane > 0, time_step * jnp.maximum(flow_zm, 0.0), 0.0)
        from_zp = jnp.where(lane < LANES - 1, -time_step * jnp.minimum(flow_zp, 0.0), 0.0)
        for s in range(SPECIES):
            c = species[s, x]
            rim = slice(128 + BLOCK * s, 144 + BLOCK * s)
            if x > 0:
                c_xm = species[s, x - 1]
            else:
                c_xm = jnp.where(north, near_rims[rim], swapped_rims[rim])
            if x < 3:
                c_xp = species[s, x + 1]
            else:
                c_xp = jnp.where(north, swapped_rims[rim], near_rims[rim])
            r = 4 * s + x
            c_ym = jnp.where(row == 0, has_below * below[36 + r : 37 + r], roll_rows(c, 1))
            c_yp = jnp.where(row == BLOCK - 1, has_above * above[r : r + 1], roll_rows(c, -1))
            total = keep * c + (from_xm * c_xm + from_xp * c_xp)
            total = total + (from_ym * c_ym + from_yp * c_yp)
            total = total + (from_zm * roll_lanes(c, 1) + from_zp * roll_lanes(c, -1))
            species_out[s, x] = total


def call(kernel, outs, scratch, *operands):
    vmem = pl.BlockSpec(memory_space=pltpu.VMEM)
    shapes = [jax.ShapeDtypeStruct(shape, jnp.float32) for shape in outs]
    return pl.pallas_call(
        kernel,
        out_shape=shapes,
        in_specs=[vmem for _ in operands],
        out_specs=[vmem for _ in outs],
        scratch_shapes=[pltpu.VMEM(shape, jnp.float32) for shape in scratch],
        cost_estimate=pl.CostEstimate(flops=1000000, bytes_accessed=1000000, transcendentals=0),
        compiler_params=pltpu.CompilerParams(vmem_limit_bytes=24 * 2**20),
        interpret=INTERPRET,
    )(*operands)


def local(n_chips, velocity, density, source, species):
    groups = [[(2 * j + k) * 4 + c for c in range(4) for k in range(2)] for j in range(n_chips)]

    def beside(distance):
        pairs = []
        for j in range(n_chips - distance):
            left, right = 2 * j + 1, 2 * (j + distance)
            pairs += [(left, right), (right, left)]
        return pairs

    within = [pair for j in range(n_chips) for pair in ((2 * j, 2 * j + 1), (2 * j + 1, 2 * j))]

    def plane(n):
        return (n, ROWS, LANES)

    def padded(n):
        return (n, *PADDED)

    def bind(kernel):
        return functools.partial(kernel, n_chips)

    (own,) = call(prepare, [(240, LANES)], [], velocity, density, source, species)
    gathered = lax.all_gather(own, ("slab", "cross"), axis_index_groups=groups)
    mobile, target, edge, sent = call(
        bind(assemble), [plane(8), plane(8), plane(2), plane(14)], [], gathered
    )
    got = lax.ppermute(sent, "slab", beside(1))
    swapped = lax.ppermute(got, "slab", within)
    mobile_w, target_w, pressure, residual, coarse, outer, sent, rim = call(
        bind(first_cycle),
        [
            padded(22), plane(20), padded(20), plane(8), plane(10), PLANE, (272, LANES),
            (144, LANES),
        ],
        [(8, *plane(20)), padded(20)],
        mobile, target, edge, got, swapped, species,
    )
    near = lax.ppermute(sent, "slab", beside(1))
    far_side = lax.ppermute(jnp.concatenate([near[:128], rim], 0), "slab", within)
    pressure, residual, coarse_w, sent, sent_far = call(
        bind(second_cycle),
        [padded(10), plane(4), padded(18), plane(4), PLANE],
        [
            (8, *plane(16)), (8, *plane(16)), plane(16), padded(16), padded(16), padded(20),
            padded(20),
        ],
        mobile_w, target_w, pressure, residual, coarse, near, far_side,
    )
    got = lax.ppermute(sent, "slab", beside(1))
    far = lax.ppermute(sent_far, "slab", beside(2))
    swapped = lax.ppermute(got, "slab", within)
    return call(
        bind(finish),
        [velocity.shape, density.shape, species.shape],
        [
            (8, *plane(10)), (8, *plane(12)), plane(14), plane(16), padded(12), padded(12),
            padded(12), padded(12), padded(8),
        ],
        mobile_w, target_w, pressure, residual, coarse_w, got, far, swapped,
        gathered, velocity, species, outer, near, far_side,
    )


def solution(mesh):
    n_chips = mesh.shape["slab"] // 2
    block = P("slab", "cross", None)
    stack = P(None, "slab", "cross", None)
    return jax.shard_map(
        lambda *arrays: tuple(local(n_chips, *arrays)),
        mesh=mesh,
        in_specs=(stack, block, block, stack),
        out_specs=(stack, block, stack),
        check_vma=False,
    )
```

time: 126 us -> 105 us (0.83)
  the two profiles are of different devices: /device:TPU:256 before, /device:TPU:255 now
where the time goes in v2:
time: 105 us
  waiting for transfers between devices  45.7 us (44%)
  blocking collectives  28.9 us (28%)
  starting transfers between devices  13.4 us (13%)
  Pallas kernels  12.5 us (12%)
  local copies, waits for them, and re-layouts  3.37 us (3%)
    all_gather x1, blocking collectives, local(): gathered = lax.all_gather(own, ('slab', 'cross'), axis_index_groups=groups)  28.9 us
    ppermute x2, waiting for transfers between devices, local(): got = lax.ppermute(sent, 'slab', beside(1))  23.1 us
    pallas_call x5, Pallas kernels, call(): pl.pallas_call(kernel, out_shape=shapes, in_specs=[vmem for _ in operands...  12.5 us
    ppermute x1, waiting for transfers between devices, local(): near = lax.ppermute(sent, 'slab', beside(1))  9.88 us
    ppermute x1, waiting for transfers between devices, local(): far = lax.ppermute(sent_far, 'slab', beside(2))  9.63 us
    ppermute x2, starting transfers between devices, local(): got = lax.ppermute(sent, 'slab', beside(1))  3.84 us
    ppermute x2, starting transfers between devices, local(): swapped = lax.ppermute(got, 'slab', within)  3.82 us
    unnamed x10, local copies, waits for them, and re-layouts  3.37 us
  transfers between devices with their start and end apart: 7, of which 6 were waited for; matrix products, arithmetic and copies ran while one was open for 0% of the time, Pallas kernels for 0%

profile of v2, /device:TPU:255, one launch (start us, length us, event | category | flops | bytes accessed | tf_op | source)
XLA Modules:
  0.0 104.6 jit_solution(9458439568288199246)
XLA Ops:
  0.6 0.0 copy-start
  0.6 1.0 copy-done
  1.6 0.0 copy-start.2
  1.6 0.9 copy-done.2
  2.5 0.0 copy-start.3
  2.5 0.8 copy-done.3
  3.2 0.0 copy-start.4
  3.2 0.8 copy-done.4
  4.0 0.1 shard_map.67
  4.1 28.9 %all-gather = f32[1920,128]{1,0:T(8,128)S(1)} all-gather(f32[240,128]{1,0:T(8,128)S(1)} %shard_map.67), channel_id=2, replica_groups={{0,4,1,5,2,6,3,7},{8,12,9,13,10,14,11,15},{16,20,17,21,18,22,19,23},{24..., dimensions={0}, use_global_device_ids=true | all-gather | bytes 1105920 | tf_op jit(solution)/shard_map/all_gather | solution.py:590
  33.0 0.0 copy-start.1
  33.0 0.1 shard_map.68
  33.1 1.9 %collective-permute-start = (f32[14,64,128]{2,1,0:T(8,128)S(1)}, f32[14,64,128]{2,1,0:T(8,128)S(1)}, u32[]{:S(2)}, u32[]{:S(2)}) collective-permute-start(f32[14,64,128]{2,1,0:T(8,128)S(1)} %get-tuple-element.23), channel_id=1, source_target_pairs={{4,8},{8,4},{12,16},{16,12},{20,24},{24,20},{28,32},{32,28},{36,40... | collective-permute-start | bytes 1376264 | tf_op jit(solution)/shard_map/ppermute | solution.py:594
  35.0 13.3 %collective-permute-done.got = f32[14,64,128]{2,1,0:T(8,128)S(1)} collective-permute-done((f32[14,64,128]{2,1,0:T(8,128)S(1)}, f32[14,64,128]{2,1,0:T(8,128)S(1)}, u32[]{:S(2)}, u32[]{:S(2)}) %collective-permute-start) | collective-permute-done | bytes 458784 | tf_op jit(solution)/shard_map/ppermute | solution.py:594
  48.3 1.9 %collective-permute-start.1 = (f32[14,64,128]{2,1,0:T(8,128)S(1)}, f32[14,64,128]{2,1,0:T(8,128)S(1)}, u32[]{:S(2)}, u32[]{:S(2)}) collective-permute-start(f32[14,64,128]{2,1,0:T(8,128)S(1)} %collective-permute-done.got), channel_id=1, source_target_pairs={{0,4},{4,0},{8,12},{12,8},{16,20},{20,16},{24,28},{28,24},{32,36},... | collective-permute-start | bytes 1376264 | tf_op jit(solution)/shard_map/ppermute | solution.py:595
  50.2 1.8 %collective-permute-done.1.swapped = f32[14,64,128]{2,1,0:T(8,128)S(1)} collective-permute-done((f32[14,64,128]{2,1,0:T(8,128)S(1)}, f32[14,64,128]{2,1,0:T(8,128)S(1)}, u32[]{:S(2)}, u32[]{:S(2)}) %collective-permute-start.1) | collective-permute-done | bytes 458784 | tf_op jit(solution)/shard_map/ppermute | solution.py:595
  52.0 0.0 copy-done.1
  52.0 3.0 %shard_map.69 = (f32[22,80,128]{2,1,0:T(8,128)S(1)}, f32[20,64,128]{2,1,0:T(8,128)S(1)}, f32[20,80,128]{2,1,0:T(8,128)S(1)}, f32[8,64,128]{2,1,0:T(8,128)S(1)}, ...) custom-call(f32[8,64,128]{2,1,0:T(8,128)S(1)} %get-tuple-element.20.mobile,, ...), custom_call_target="tpu_custom_call" | custom-call | flops 1000000 | bytes 1000000 | tf_op jit(solution)/shard_map/pallas_call | solution.py:556
  55.0 1.9 %collective-permute-start.2 = (f32[272,128]{1,0:T(8,128)S(1)}, f32[272,128]{1,0:T(8,128)S(1)}, u32[]{:S(2)}, u32[]{:S(2)}) collective-permute-start(f32[272,128]{1,0:T(8,128)S(1)} %get-tuple-element.29), channel_id=1, source_target_pairs={{4,8},{8,4},{12,16},{16,12},{20,24},{24,20},{28,32},{32,28},{36,40... | collective-permute-start | bytes 417800 | tf_op jit(solution)/shard_map/ppermute | solution.py:605
  56.9 9.9 %collective-permute-done.2.got.near_rims = f32[272,128]{1,0:T(8,128)S(1)} collective-permute-done((f32[272,128]{1,0:T(8,128)S(1)}, f32[272,128]{1,0:T(8,128)S(1)}, u32[]{:S(2)}, u32[]{:S(2)}) %collective-permute-start.2) | collective-permute-done | bytes 139296 | tf_op jit(solution)/shard_map/ppermute | solution.py:605
  66.8 1.9 %collective-permute-start.3 = (f32[272,128]{1,0:T(8,128)S(1)}, f32[272,128]{1,0:T(8,128)S(1)}, u32[]{:S(2)}, u32[]{:S(2)}) collective-permute-start(f32[272,128]{1,0:T(8,128)S(1)} %pad_maximum_fusion), channel_id=1, source_target_pairs={{0,4},{4,0},{8,12},{12,8},{16,20},{20,16},{24,28},{28,24},{32,36},... | collective-permute-start | bytes 417800 | tf_op jit(solution)/shard_map/ppermute | solution.py:606
  68.8 1.3 %collective-permute-done.3.swapped.swapped_rims = f32[272,128]{1,0:T(8,128)S(1)} collective-permute-done((f32[272,128]{1,0:T(8,128)S(1)}, f32[272,128]{1,0:T(8,128)S(1)}, u32[]{:S(2)}, u32[]{:S(2)}) %collective-permute-start.3) | collective-permute-done | bytes 139296 | tf_op jit(solution)/shard_map/ppermute | solution.py:606
  70.1 5.4 %shard_map.70 = (f32[10,80,128]{2,1,0:T(8,128)S(1)}, f32[4,64,128]{2,1,0:T(8,128)S(1)}, f32[18,80,128]{2,1,0:T(8,128)S(1)}, f32[4,64,128]{2,1,0:T(8,128)S(1)}, f32[64,128]{1,0:T(8,128)S(1)}) custom-call(f32[22,80,128]{2,1,0:T(8,128)S(1)} %get-tuple-element.24.mobile_ref, f32[20,64,128]{2,1,0:T(8,128)S(1)} %get-tuple-element.25.target_w, ...), custom_call_target="tpu_custom_call" | custom-call | flops 1000000 | bytes 1000000 | tf_op jit(solution)/shard_map/pallas_call | solution.py:556
  75.5 1.9 %collective-permute-start.4 = (f32[4,64,128]{2,1,0:T(8,128)S(1)}, f32[4,64,128]{2,1,0:T(8,128)S(1)}, u32[]{:S(2)}, u32[]{:S(2)}) collective-permute-start(f32[4,64,128]{2,1,0:T(8,128)S(1)} %get-tuple-element.34), channel_id=1, source_target_pairs={{4,8},{8,4},{12,16},{16,12},{20,24},{24,20},{28,32},{32,28},{36,40... | collective-permute-start | bytes 393224 | tf_op jit(solution)/shard_map/ppermute | solution.py:616
  77.5 9.8 %collective-permute-done.4.got = f32[4,64,128]{2,1,0:T(8,128)S(1)} collective-permute-done((f32[4,64,128]{2,1,0:T(8,128)S(1)}, f32[4,64,128]{2,1,0:T(8,128)S(1)}, u32[]{:S(2)}, u32[]{:S(2)}) %collective-permute-start.4) | collective-permute-done | bytes 131104 | tf_op jit(solution)/shard_map/ppermute | solution.py:616
  87.2 1.9 %collective-permute-start.6 = (f32[4,64,128]{2,1,0:T(8,128)S(1)}, f32[4,64,128]{2,1,0:T(8,128)S(1)}, u32[]{:S(2)}, u32[]{:S(2)}) collective-permute-start(f32[4,64,128]{2,1,0:T(8,128)S(1)} %collective-permute-done.4.got), channel_id=1, source_target_pairs={{0,4},{4,0},{8,12},{12,8},{16,20},{20,16},{24,28},{28,24},{32,36},... | collective-permute-start | bytes 393224 | tf_op jit(solution)/shard_map/ppermute | solution.py:618
  89.2 1.9 %collective-permute-start.5 = (f32[64,128]{1,0:T(8,128)S(1)}, f32[64,128]{1,0:T(8,128)S(1)}, u32[]{:S(2)}, u32[]{:S(2)}) collective-permute-start(f32[64,128]{1,0:T(8,128)S(1)} %get-tuple-element.35), channel_id=1, source_target_pairs={{4,16},{16,4},{12,24},{24,12},{20,32},{32,20},{28,40},{40,28},{36,... | collective-permute-start | bytes 98312 | tf_op jit(solution)/shard_map/ppermute | solution.py:617
  91.1 9.6 %collective-permute-done.5.far = f32[64,128]{1,0:T(8,128)S(1)} collective-permute-done((f32[64,128]{1,0:T(8,128)S(1)}, f32[64,128]{1,0:T(8,128)S(1)}, u32[]{:S(2)}, u32[]{:S(2)}) %collective-permute-start.5) | collective-permute-done | bytes 32800 | tf_op jit(solution)/shard_map/ppermute | solution.py:617
  100.7 0.0 collective-permute-done.6.swapped
  100.7 3.9 %shard_map.71 = (f32[3,4,16,128]{3,2,1,0:T(8,128)}, f32[4,16,128]{2,1,0:T(8,128)}, f32[9,4,16,128]{3,2,1,0:T(8,128)}) custom-call(f32[22,80,128]{2,1,0:T(8,128)S(1)} %get-tuple-element.24.mobile_ref, f32[20,64,128]{2,1,0:T(8,128)S(1)} %get-tuple-element.25.target_w, f32[10,80,128]{2,1,0:T(8,128)S(1)} %get-tuple-element.31.pressure, ...), custom_call_target="tpu_custom_call" | custom-call | flops 1000000 | bytes 1000000 | tf_op jit(solution)/shard_map/pallas_call | solution.py:556
  (2 shorter events, 0.0 us)
Async XLA Ops:
  0.6 1.0 copy-start
  1.6 0.9 copy-start.2
  2.5 0.8 copy-start.3
  3.2 0.8 copy-start.4
  33.0 19.0 %copy-start.1 = (f32[9,4,16,128]{3,2,1,0:T(8,128)S(1)}, f32[9,4,16,128]{3,2,1,0:T(8,128)}, u32[]{:S(2)}) copy-start(f32[9,4,16,128]{3,2,1,0:T(8,128)} %species.5) | copy-start | bytes 884740
  33.1 15.2 %collective-permute-start = (f32[14,64,128]{2,1,0:T(8,128)S(1)}, f32[14,64,128]{2,1,0:T(8,128)S(1)}, u32[]{:S(2)}, u32[]{:S(2)}) collective-permute-start(f32[14,64,128]{2,1,0:T(8,128)S(1)} %get-tuple-element.23), channel_id=1, source_target_pairs={{4,8},{8,4},{12,16},{16,12},{20,24},{24,20},{28,32},{32,28},{36,40... | collective-permute-start | bytes 1376264 | tf_op jit(solution)/shard_map/ppermute | solution.py:594
  48.3 3.7 %collective-permute-start.1 = (f32[14,64,128]{2,1,0:T(8,128)S(1)}, f32[14,64,128]{2,1,0:T(8,128)S(1)}, u32[]{:S(2)}, u32[]{:S(2)}) collective-permute-start(f32[14,64,128]{2,1,0:T(8,128)S(1)} %collective-permute-done.got), channel_id=1, source_target_pairs={{0,4},{4,0},{8,12},{12,8},{16,20},{20,16},{24,28},{28,24},{32,36},... | collective-permute-start | bytes 1376264 | tf_op jit(solution)/shard_map/ppermute | solution.py:595
  55.0 11.8 %collective-permute-start.2 = (f32[272,128]{1,0:T(8,128)S(1)}, f32[272,128]{1,0:T(8,128)S(1)}, u32[]{:S(2)}, u32[]{:S(2)}) collective-permute-start(f32[272,128]{1,0:T(8,128)S(1)} %get-tuple-element.29), channel_id=1, source_target_pairs={{4,8},{8,4},{12,16},{16,12},{20,24},{24,20},{28,32},{32,28},{36,40... | collective-permute-start | bytes 417800 | tf_op jit(solution)/shard_map/ppermute | solution.py:605
  66.8 3.3 %collective-permute-start.3 = (f32[272,128]{1,0:T(8,128)S(1)}, f32[272,128]{1,0:T(8,128)S(1)}, u32[]{:S(2)}, u32[]{:S(2)}) collective-permute-start(f32[272,128]{1,0:T(8,128)S(1)} %pad_maximum_fusion), channel_id=1, source_target_pairs={{0,4},{4,0},{8,12},{12,8},{16,20},{20,16},{24,28},{28,24},{32,36},... | collective-permute-start | bytes 417800 | tf_op jit(solution)/shard_map/ppermute | solution.py:606
  75.5 11.7 %collective-permute-start.4 = (f32[4,64,128]{2,1,0:T(8,128)S(1)}, f32[4,64,128]{2,1,0:T(8,128)S(1)}, u32[]{:S(2)}, u32[]{:S(2)}) collective-permute-start(f32[4,64,128]{2,1,0:T(8,128)S(1)} %get-tuple-element.34), channel_id=1, source_target_pairs={{4,8},{8,4},{12,16},{16,12},{20,24},{24,20},{28,32},{32,28},{36,40... | collective-permute-start | bytes 393224 | tf_op jit(solution)/shard_map/ppermute | solution.py:616
  87.2 13.5 %collective-permute-start.6 = (f32[4,64,128]{2,1,0:T(8,128)S(1)}, f32[4,64,128]{2,1,0:T(8,128)S(1)}, u32[]{:S(2)}, u32[]{:S(2)}) collective-permute-start(f32[4,64,128]{2,1,0:T(8,128)S(1)} %collective-permute-done.4.got), channel_id=1, source_target_pairs={{0,4},{4,0},{8,12},{12,8},{16,20},{20,16},{24,28},{28,24},{32,36},... | collective-permute-start | bytes 393224 | tf_op jit(solution)/shard_map/ppermute | solution.py:618
  89.2 11.6 %collective-permute-start.5 = (f32[64,128]{1,0:T(8,128)S(1)}, f32[64,128]{1,0:T(8,128)S(1)}, u32[]{:S(2)}, u32[]{:S(2)}) collective-permute-start(f32[64,128]{1,0:T(8,128)S(1)} %get-tuple-element.35), channel_id=1, source_target_pairs={{4,16},{16,4},{12,24},{24,12},{20,32},{32,20},{28,40},{40,28},{36,... | collective-permute-start | bytes 98312 | tf_op jit(solution)/shard_map/ppermute | solution.py:617

commit v3 on v2

--- a/solution.py
+++ b/solution.py
@@ -7,12 +7,15 @@
 from jax.experimental.pallas import tpu as pltpu
 from jax.sharding import PartitionSpec as P
 
+
 INTERPRET = False
+HBM = pltpu.HBM
 ROWS = 64
 LANES = 128
 BLOCK = 16
 SPECIES = 9
 EDGE = 160
+OWN = EDGE + 8
 damping = 0.8
 time_step = 0.25
 
@@ -99,11 +102,17 @@
 
 
 class Weights:
-    def __init__(self, ref, step):
+    def __init__(self, ref, step, low, shift=None, constant=None):
         self.ref = ref
         self.step = step
-
-    def fill(self, low, high, mobile, target, inside, scale):
+        self.low = low
+        self.shift = shift
+        self.constant = constant
+
+    def place(self, i):
+        return (i - self.low).index(self.shift)
+
+    def fill(self, low, high, mobile, target, inside):
         s = self.step
         lane = lanes_of(PLANE)
         z_low, z_high = lane >= s, lane < LANES - s
@@ -118,27 +127,35 @@
             valid = inside(i)
             scaled = (damping * valid) / (diagonal + (1.0 - valid))
             half = 0.5 * scaled
-            k = (i - low).index()
+            k = self.place(i)
             self.ref[0, k] = (m + x_m) * half
             self.ref[1, k] = (m + x_p) * half
             self.ref[2, k] = (m + y_m) * half
             self.ref[3, k] = (m + y_p) * half
             self.ref[4, k] = jnp.where(z_low, (m + z_m) * half, 0.0)
             self.ref[5, k] = jnp.where(z_high, (m + z_p) * half, 0.0)
-            self.ref[6, k] = target(i) * (scaled * scale)
-            self.ref[7, k] = diagonal * (1.0 / damping)
-
-        self.low = low
+            if s == 1:
+                self.ref[6, k] = target(i) * scaled
+                self.ref[7, k] = diagonal * (1.0 / damping)
+            else:
+                self.ref[6, k] = target(i) * (4.0 * scaled)
+                self.ref[7, k] = 4.0 * scaled
+
         loop(low, high, body)
+
+    def side(self, i):
+        if self.constant is not None:
+            return self.constant(i)
+        return self.ref[6, self.place(i)]
 
     def change(self, field, i):
         s = self.step
-        k = (i - self.low).index()
+        k = self.place(i)
         p = field(i)
         total = self.ref[0, k] * field(i - 1) + self.ref[1, k] * field(i + 1)
         total = total + (self.ref[2, k] * field(i, -s) + self.ref[3, k] * field(i, s))
         total = total + (self.ref[4, k] * roll_lanes(p, s) + self.ref[5, k] * roll_lanes(p, -s))
-        return p, (total - self.ref[6, k]) - damping * p
+        return p, (total - self.side(i)) - damping * p
 
 
 def at(ref, origin, shift=None):
@@ -155,7 +172,7 @@
 
 def first_sweep(weights, result, low, high):
     def body(i):
-        result.put(i, -weights.ref[6, (i - weights.low).index()])
+        result.put(i, -weights.side(i))
 
     loop(low, high, body)
 
@@ -192,7 +209,7 @@
         total = 0.0
         for half in range(2):
             _, change = weights.change(field, 2 * i + half)
-            total = total - change * weights.ref[7, (2 * i + half - weights.low).index()]
+            total = total - change * weights.ref[7, weights.place(2 * i + half)]
         result[(i - result_low).index()] = 0.125 * pair_sum(total)
 
     loop(low, high, body)
@@ -212,11 +229,23 @@
     return slab % 2 == 0, jnp.minimum(jnp.maximum(cross, 0), 3), chip
 
 
-def prepare(velocity, density, source, species, out):
+def prepare(velocity_in, density_in, source_in, out, velocity, density, source, semaphore):
+    copies = [
+        pltpu.make_async_copy(there, here, semaphore.at[k])
+        for k, (there, here) in enumerate(
+            [(density_in, density), (velocity_in, velocity), (source_in, source)]
+        )
+    ]
+    for copy in copies:
+        copy.start()
     lane = lanes_of((BLOCK, LANES))
     row = rows_of((BLOCK, LANES))
+    copies[0].wait()
     for x in range(4):
         out[BLOCK * x : BLOCK * (x + 1)] = 1.0 / density[x]
+    copies[1].wait()
+    copies[2].wait()
+    for x in range(4):
         u_p = velocity[0, x + 1] if x < 3 else 0.0
         u_m = velocity[0, x - 1] if x > 0 else 0.0
         v, w = velocity[1, x], velocity[2, x]
@@ -226,11 +255,7 @@
         w_m = jnp.where(lane > 0, roll_lanes(w, 1), 0.0)
         moved = 0.5 * ((u_p - u_m) + (v_p - v_m) + (w_p - w_m))
         out[64 + BLOCK * x : 64 + BLOCK * (x + 1)] = moved - source[x]
-        for s in range(SPECIES):
-            r = EDGE + 4 * s + x
-            out[r : r + 1] = species[s, x, 0:1]
-            out[r + 36 : r + 37] = species[s, x, BLOCK - 1 : BLOCK]
-        r = EDGE + 72 + x
+        r = EDGE + x
         out[r : r + 1] = velocity[1, x, 0:1]
         out[r + 4 : r + 5] = velocity[1, x, BLOCK - 1 : BLOCK]
     out[128:144] = velocity[0, 0]
@@ -247,7 +272,7 @@
             for x in range(4):
                 mobile[4 * k + x, rows] = gathered[block, BLOCK * x : BLOCK * (x + 1)]
                 t = gathered[block, 64 + BLOCK * x : 64 + BLOCK * (x + 1)]
-                r = EDGE + 72 + x
+                r = EDGE + x
                 if c > 0:
                     t = t - jnp.where(row == 0, 0.5 * gathered[block - 2, r + 4 : r + 5], 0.0)
                 if c < 3:
@@ -269,8 +294,8 @@
 
 def first_cycle(
     n_chips, mobile, target, edge, got, swapped, species,
-    mobile_ref, target_w, pressure_ref, residual, coarse, outer, sent, rim,
-    weights_ref, field_ref,
+    mobile_ref, weights_ref, pressure_ref, residual, coarse, outer, sent, rim, edge_low, edge_high,
+    target_w, field_ref,
 ):
     north, _, chip = whereabouts(n_chips)
     clear_pads(mobile_ref)
@@ -309,8 +334,8 @@
     target_w[14] = target_w[14] - 0.5 * edge[1]
     outer[...] = got[13]
 
-    weights = Weights(weights_ref, 1)
-    weights.fill(-6, 14, mobile_w, at(target_w, -6), inside_of(8 * chip, 8 * n_chips), 1.0)
+    weights = Weights(weights_ref, 1, -6)
+    weights.fill(-6, 14, mobile_w, at(target_w, -6), inside_of(8 * chip, 8 * n_chips))
     first_sweep(weights, field, -6, 14)
     sweep(weights, field, pressure, -5, 13)
     residual_planes(weights, pressure, residual, -2, -2, 6)
@@ -328,6 +353,34 @@
     for s in range(SPECIES):
         sent[128 + BLOCK * s : 144 + BLOCK * s] = species[s, near]
         rim[BLOCK * s : BLOCK * (s + 1)] = species[s, beside]
+        for x in range(4):
+            r = 4 * s + x
+            edge_low[r : r + 1] = species[s, x, 0:1]
+            edge_high[r : r + 1] = species[s, x, BLOCK - 1 : BLOCK]
+    edge_low[36:40] = jnp.zeros((4, LANES), jnp.float32)
+    edge_high[36:40] = jnp.zeros((4, LANES), jnp.float32)
+
+
+def flow_rims(n_chips, gathered, outer, u_rims, v_rims):
+    north, cross, _ = whereabouts(n_chips)
+    core = jnp.where(north, 0, 1)
+    start = pl.multiple_of(cross * BLOCK, BLOCK)
+    partner = 2 * cross + jnp.where(north, 1, 0)
+    first, last = gathered[partner, 128:144], gathered[partner, 144:160]
+    beyond = outer[pl.ds(start, BLOCK)]
+    u_rims[0] = jnp.where(north, beyond, last)
+    u_rims[1] = jnp.where(north, first, beyond)
+    below = gathered[2 * jnp.maximum(cross - 1, 0) + core, EDGE:OWN]
+    above = gathered[2 * jnp.minimum(cross + 1, 3) + core, EDGE:OWN]
+    v_rims[0:4] = jnp.where(cross > 0, below[4:8], 0.0)
+    v_rims[4:8] = jnp.where(cross < 3, above[0:4], 0.0)
+
+
+def species_rims(n_chips, near, beside, rims):
+    north, _, _ = whereabouts(n_chips)
+    a, b = near[128:272], beside[128:272]
+    rims[0] = jnp.where(north, a, b)
+    rims[1] = jnp.where(north, b, a)
 
 
 def coarse_sweeps(weights, one, two, low, high):
@@ -338,9 +391,9 @@
 
 
 def second_cycle(
-    n_chips, mobile_ref, target_w, pressure_ref, residual, coarse, got, swapped,
-    pressure_new_ref, residual_new, coarse_ref, sent, sent_far,
-    weights_ref, coarse_weights_ref, residual_w, one_ref, two_ref, field_ref, other_ref,
+    n_chips, weights_ref, pressure_ref, residual, coarse, got, swapped,
+    pressure_new_ref, residual_new, coarse_weights_ref, sent, sent_far,
+    coarse_ref, residual_w, one_ref, two_ref, field_ref, other_ref,
 ):
     north, _, chip = whereabouts(n_chips)
     for ref in (pressure_new_ref, coarse_ref, one_ref, two_ref, field_ref, other_ref):
@@ -371,10 +424,8 @@
     loop(0, 8, copy_residual)
     loop(0, 10, copy_coarse)
 
-    coarse_weights = Weights(coarse_weights_ref, 2)
-    coarse_weights.fill(
-        -6, 10, coarse_w, at(residual_w, -6), inside_of(4 * chip, 4 * n_chips), 4.0
-    )
+    coarse_weights = Weights(coarse_weights_ref, 2, -6)
+    coarse_weights.fill(-6, 10, coarse_w, at(residual_w, -6), inside_of(4 * chip, 4 * n_chips))
     coarse_sweeps(coarse_weights, one, two, -6, 10)
 
     def prolong(i):
@@ -385,10 +436,7 @@
 
     loop(-3, 7, prolong)
 
-    weights = Weights(weights_ref, 1)
-    weights.fill(
-        -4, 12, Field(mobile_ref, -7), at(target_w, -6), inside_of(8 * chip, 8 * n_chips), 1.0
-    )
+    weights = Weights(weights_ref, 1, -6)
     sweep(weights, field, other, -4, 12)
     sweep(weights, other, field, -3, 11)
     sweep(weights, field, other, -2, 10)
@@ -402,14 +450,12 @@
 
 
 def finish(
-    n_chips, mobile_ref, target_w, pressure, residual, coarse_ref, got, far, swapped,
-    gathered, velocity, species, outer, near_rims, swapped_rims,
+    n_chips, mobile_ref, weights_ref, pressure, residual, coarse_weights_ref, got, far, swapped,
+    velocity, species, u_rims, v_rims, x_rims, y_low, y_high,
     velocity_out, pressure_out, species_out,
-    weights_ref, coarse_weights_ref, residual_w, pressure_w, one_ref, two_ref, field_ref,
-    other_ref, final_pad,
+    residual_w, pressure_w, one_ref, two_ref, field_ref, other_ref, final_pad,
 ):
-    north, cross, chip = whereabouts(n_chips)
-    core = jnp.where(north, 0, 1)
+    north, cross, _ = whereabouts(n_chips)
     for ref in (one_ref, two_ref, field_ref, other_ref, final_pad):
         clear_pads(ref)
     one, two = Field(one_ref, -5), Field(two_ref, -5)
@@ -433,15 +479,15 @@
     loop(-1, 9, copy_pressure)
 
     shift, coarse_shift = jnp.where(north, 0, 4), jnp.where(north, 0, 2)
-    coarse_weights = Weights(coarse_weights_ref, 2)
-    coarse_weights.fill(
-        -5,
-        7,
-        Field(coarse_ref, -7, coarse_shift),
-        at(residual_w, -5, coarse_shift),
-        inside_of(4 * chip + coarse_shift, 4 * n_chips),
-        4.0,
-    )
+    coarse_weights = Weights(coarse_weights_ref, 2, -6, coarse_shift, at(residual_w, -5))
+
+    def right_side(i):
+        k = (i + 5).index()
+        factor = coarse_weights_ref[7, coarse_weights.place(i)]
+        residual_w[k] = residual_w[(i + 5).index(coarse_shift)] * factor
+
+    for k in range(12):
+        right_side(Place(0, k - 5))
     coarse_sweeps(coarse_weights, one, two, -5, 7)
 
     def prolong(i):
@@ -452,15 +498,7 @@
 
     loop(-2, 4, prolong)
 
-    weights = Weights(weights_ref, 1)
-    weights.fill(
-        -3,
-        7,
-        Field(mobile_ref, -7, shift),
-        at(target_w, -6, shift),
-        inside_of(8 * chip + shift, 8 * n_chips),
-        1.0,
-    )
+    weights = Weights(weights_ref, 1, -6, shift)
     sweep(weights, field, other, -3, 7)
     sweep(weights, other, final, -2, 6)
 
@@ -468,36 +506,25 @@
     own = pl.ds(start + 8, BLOCK)
     row, lane = rows_of((BLOCK, LANES)), lanes_of((BLOCK, LANES))
 
-    partner = gathered[2 * cross + jnp.where(north, 1, 0)]
-    beside = jnp.where(north, partner[128:144], partner[144:160])
-
-    beyond = outer[pl.ds(start, BLOCK)]
-    u_low = jnp.where(north, beyond, beside)
-    u_high = jnp.where(north, beside, beyond)
-
     def u_out(x):
         if x < 0:
-            u = u_low
+            u = u_rims[0]
         elif x > 3:
-            u = u_high
+            u = u_rims[1]
         else:
             u = velocity[0, x]
         slope = 0.5 * (final_pad[x + 3, own] - final_pad[x + 1, own])
         return u - mobile_ref[shift + (x + 7), own] * slope
 
     u = [u_out(x) for x in range(-1, 5)]
-    below = gathered[2 * jnp.maximum(cross - 1, 0) + core, EDGE:240]
-    above = gathered[2 * jnp.minimum(cross + 1, 3) + core, EDGE:240]
-    has_below = jnp.where(cross > 0, 1.0, 0.0)
-    has_above = jnp.where(cross < 3, 1.0, 0.0)
     wide = pl.ds(start, 32)
     for x in range(4):
         p = final_pad[x + 2, wide]
         m = mobile_ref[shift + (x + 7), wide]
         p_own = p[8:24]
         v = velocity[1, x] - m[8:24] * (0.5 * (p[9:25] - p[7:23]))
-        v_low = has_below * below[76 + x : 77 + x] - m[7:8] * (0.5 * (p[8:9] - p[6:7]))
-        v_high = has_above * above[72 + x : 73 + x] - m[24:25] * (0.5 * (p[25:26] - p[23:24]))
+        v_low = v_rims[x : x + 1] - m[7:8] * (0.5 * (p[8:9] - p[6:7]))
+        v_high = v_rims[4 + x : 5 + x] - m[24:25] * (0.5 * (p[25:26] - p[23:24]))
         p_zp = jnp.where(lane < LANES - 1, roll_lanes(p_own, -1), 0.0)
         p_zm = jnp.where(lane > 0, roll_lanes(p_own, 1), 0.0)
         w = velocity[2, x] - m[8:24] * (0.5 * (p_zp - p_zm))
@@ -532,35 +559,38 @@
         from_zp = jnp.where(lane < LANES - 1, -time_step * jnp.minimum(flow_zp, 0.0), 0.0)
         for s in range(SPECIES):
             c = species[s, x]
-            rim = slice(128 + BLOCK * s, 144 + BLOCK * s)
+            rim = slice(BLOCK * s, BLOCK * (s + 1))
             if x > 0:
                 c_xm = species[s, x - 1]
             else:
-                c_xm = jnp.where(north, near_rims[rim], swapped_rims[rim])
+                c_xm = x_rims[0, rim]
             if x < 3:
                 c_xp = species[s, x + 1]
             else:
-                c_xp = jnp.where(north, swapped_rims[rim], near_rims[rim])
+                c_xp = x_rims[1, rim]
             r = 4 * s + x
-            c_ym = jnp.where(row == 0, has_below * below[36 + r : 37 + r], roll_rows(c, 1))
-            c_yp = jnp.where(row == BLOCK - 1, has_above * above[r : r + 1], roll_rows(c, -1))
+            c_ym = jnp.where(row == 0, y_low[r : r + 1], roll_rows(c, 1))
+            c_yp = jnp.where(row == BLOCK - 1, y_high[r : r + 1], roll_rows(c, -1))
             total = keep * c + (from_xm * c_xm + from_xp * c_xp)
             total = total + (from_ym * c_ym + from_yp * c_yp)
             total = total + (from_zm * roll_lanes(c, 1) + from_zp * roll_lanes(c, -1))
             species_out[s, x] = total
 
 
-def call(kernel, outs, scratch, *operands):
+def call(kernel, outs, scratch, *operands, where=pltpu.VMEM, semaphores=0, grant=24):
     vmem = pl.BlockSpec(memory_space=pltpu.VMEM)
     shapes = [jax.ShapeDtypeStruct(shape, jnp.float32) for shape in outs]
+    scratch = [pltpu.VMEM(shape, jnp.float32) for shape in scratch]
+    if semaphores:
+        scratch = [*scratch, pltpu.SemaphoreType.DMA((semaphores,))]
     return pl.pallas_call(
         kernel,
         out_shape=shapes,
-        in_specs=[vmem for _ in operands],
+        in_specs=[pl.BlockSpec(memory_space=where) for _ in operands],
         out_specs=[vmem for _ in outs],
-        scratch_shapes=[pltpu.VMEM(shape, jnp.float32) for shape in scratch],
+        scratch_shapes=scratch,
         cost_estimate=pl.CostEstimate(flops=1000000, bytes_accessed=1000000, transcendentals=0),
-        compiler_params=pltpu.CompilerParams(vmem_limit_bytes=24 * 2**20),
+        compiler_params=pltpu.CompilerParams(vmem_limit_bytes=grant * 2**20),
         interpret=INTERPRET,
     )(*operands)
 
@@ -576,6 +606,8 @@
         return pairs
 
     within = [pair for j in range(n_chips) for pair in ((2 * j, 2 * j + 1), (2 * j + 1, 2 * j))]
+    upward = [(c, c + 1) for c in range(3)]
+    downward = [(c + 1, c) for c in range(3)]
 
     def plane(n):
         return (n, ROWS, LANES)
@@ -586,45 +618,47 @@
     def bind(kernel):
         return functools.partial(kernel, n_chips)
 
-    (own,) = call(prepare, [(240, LANES)], [], velocity, density, source, species)
+    (own,) = call(
+        prepare, [(OWN, LANES)], [velocity.shape, density.shape, source.shape],
+        velocity, density, source,
+        where=HBM, semaphores=3, grant=63,
+    )
     gathered = lax.all_gather(own, ("slab", "cross"), axis_index_groups=groups)
     mobile, target, edge, sent = call(
         bind(assemble), [plane(8), plane(8), plane(2), plane(14)], [], gathered
     )
     got = lax.ppermute(sent, "slab", beside(1))
     swapped = lax.ppermute(got, "slab", within)
-    mobile_w, target_w, pressure, residual, coarse, outer, sent, rim = call(
+    mobile_w, weights, pressure, residual, coarse, outer, sent, rim, edge_low, edge_high = call(
         bind(first_cycle),
         [
-            padded(22), plane(20), padded(20), plane(8), plane(10), PLANE, (272, LANES),
-            (144, LANES),
+            padded(22), (8, *plane(20)), padded(20), plane(8), plane(10), PLANE, (272, LANES),
+            (144, LANES), (40, LANES), (40, LANES),
         ],
-        [(8, *plane(20)), padded(20)],
+        [plane(20), padded(20)],
         mobile, target, edge, got, swapped, species,
     )
     near = lax.ppermute(sent, "slab", beside(1))
-    far_side = lax.ppermute(jnp.concatenate([near[:128], rim], 0), "slab", within)
-    pressure, residual, coarse_w, sent, sent_far = call(
+    y_low = lax.ppermute(edge_high, "cross", upward)
+    y_high = lax.ppermute(edge_low, "cross", downward)
+    u_rims, v_rims = call(bind(flow_rims), [(2, BLOCK, LANES), (8, LANES)], [], gathered, outer)
+    opposite = lax.ppermute(jnp.concatenate([near[:128], rim], 0), "slab", within)
+    pressure, residual, coarse_weights, sent, sent_far = call(
         bind(second_cycle),
-        [padded(10), plane(4), padded(18), plane(4), PLANE],
-        [
-            (8, *plane(16)), (8, *plane(16)), plane(16), padded(16), padded(16), padded(20),
-            padded(20),
-        ],
-        mobile_w, target_w, pressure, residual, coarse, near, far_side,
+        [padded(10), plane(4), (8, *plane(16)), plane(4), PLANE],
+        [padded(18), plane(16), padded(16), padded(16), padded(20), padded(20)],
+        weights, pressure, residual, coarse, near, opposite,
     )
     got = lax.ppermute(sent, "slab", beside(1))
     far = lax.ppermute(sent_far, "slab", beside(2))
+    (x_rims,) = call(bind(species_rims), [(2, 144, LANES)], [], near, opposite)
     swapped = lax.ppermute(got, "slab", within)
     return call(
         bind(finish),
         [velocity.shape, density.shape, species.shape],
-        [
-            (8, *plane(10)), (8, *plane(12)), plane(14), plane(16), padded(12), padded(12),
-            padded(12), padded(12), padded(8),
-        ],
-        mobile_w, target_w, pressure, residual, coarse_w, got, far, swapped,
-        gathered, velocity, species, outer, near, far_side,
+        [plane(14), plane(16), padded(12), padded(12), padded(12), padded(12), padded(8)],
+        mobile_w, weights, pressure, residual, coarse_weights, got, far, swapped,
+        velocity, species, u_rims, v_rims, x_rims, y_low, y_high,
     )
 
 
@@ -632,8 +666,12 @@
     n_chips = mesh.shape["slab"] // 2
     block = P("slab", "cross", None)
     stack = P(None, "slab", "cross", None)
+
+    def step(*arrays):
+        return tuple(local(n_chips, *arrays))
+
     return jax.shard_map(
-        lambda *arrays: tuple(local(n_chips, *arrays)),
+        step,
         mesh=mesh,
         in_specs=(stack, block, block, stack),
         out_specs=(stack, block, stack),

time: 105 us -> 112 us (1.067)
  the two profiles are of different devices: /device:TPU:255 before, /device:TPU:72 now
where the time goes in v3:
time: 112 us; the launch traced here: 111 us
  starting transfers between devices  48 us (43%)
  blocking collectives  26.3 us (23%)
  waiting for transfers between devices  22.9 us (20%)
  Pallas kernels  12.5 us (11%)
    all_gather x1, blocking collectives, local(): gathered = lax.all_gather(own, ('slab', 'cross'), axis_index_groups=groups)  26.3 us
    ppermute x1, starting transfers between devices, local(): far = lax.ppermute(sent_far, 'slab', beside(2))  12.8 us
    pallas_call x7, Pallas kernels, call(): pl.pallas_call(kernel, out_shape=shapes, in_specs=[pl.BlockSpec(memory_sp...  12.5 us
    ppermute x1, starting transfers between devices, local(): y_low = lax.ppermute(edge_high, 'cross', upward)  11.3 us
    ppermute x2, starting transfers between devices, local(): got = lax.ppermute(sent, 'slab', beside(1))  10.2 us
    ppermute x2, waiting for transfers between devices, local(): got = lax.ppermute(sent, 'slab', beside(1))  10.1 us
    ppermute x1, waiting for transfers between devices, local(): y_high = lax.ppermute(edge_low, 'cross', downward)  7.22 us
    ppermute x1, starting transfers between devices, local(): near = lax.ppermute(sent, 'slab', beside(1))  6.35 us
  transfers between devices with their start and end apart: 9, of which 7 were waited for; matrix products, arithmetic and copies ran while one was open for 0% of the time, Pallas kernels for 0%

profile of v3, /device:TPU:72, one launch (start us, length us, event | category | flops | bytes accessed | tf_op | source)
XLA Modules:
  0.0 111.4 jit_solution(2738200280719058097)
XLA Ops:
  0.6 1.7 %shard_map.67 = f32[168,128]{1,0:T(8,128)} custom-call(f32[3,4,16,128]{3,2,1,0:T(8,128)} %velocity.1, f32[4,16,128]{2,1,0:T(8,128)} %density_in.1, f32[4,16,128]{2,1,0:T(8,128)} %source_in.1), custom_call_target="tpu_custom_call" | custom-call | flops 1000000 | bytes 1000000 | tf_op jit(solution)/shard_map/pallas_call | solution.py:586
  2.3 26.3 %all-gather = f32[1344,128]{1,0:T(8,128)S(1)} all-gather(f32[168,128]{1,0:T(8,128)} %shard_map.67), channel_id=2, replica_groups={{0,4,1,5,2,6,3,7},{8,12,9,13,10,14,11,15},{16,20,17,21,18,22,19,23},{24..., dimensions={0}, use_global_device_ids=true | all-gather | bytes 774144 | tf_op jit(solution)/shard_map/all_gather | solution.py:626
  28.6 0.0 copy-start.1
  28.6 0.1 shard_map.68
  28.7 2.3 %collective-permute-start = (f32[14,64,128]{2,1,0:T(8,128)S(1)}, f32[14,64,128]{2,1,0:T(8,128)S(1)}, u32[]{:S(2)}, u32[]{:S(2)}) collective-permute-start(f32[14,64,128]{2,1,0:T(8,128)S(1)} %get-tuple-element.27), channel_id=1, source_target_pairs={{4,8},{8,4},{12,16},{16,12},{20,24},{24,20},{28,32},{32,28},{36,40... | collective-permute-start | bytes 1376264 | tf_op jit(solution)/shard_map/ppermute | solution.py:630
  31.0 7.5 %collective-permute-done.got = f32[14,64,128]{2,1,0:T(8,128)S(1)} collective-permute-done((f32[14,64,128]{2,1,0:T(8,128)S(1)}, f32[14,64,128]{2,1,0:T(8,128)S(1)}, u32[]{:S(2)}, u32[]{:S(2)}) %collective-permute-start) | collective-permute-done | bytes 458784 | tf_op jit(solution)/shard_map/ppermute | solution.py:630
  38.5 2.2 %collective-permute-start.1 = (f32[14,64,128]{2,1,0:T(8,128)S(1)}, f32[14,64,128]{2,1,0:T(8,128)S(1)}, u32[]{:S(2)}, u32[]{:S(2)}) collective-permute-start(f32[14,64,128]{2,1,0:T(8,128)S(1)} %collective-permute-done.got), channel_id=1, source_target_pairs={{0,4},{4,0},{8,12},{12,8},{16,20},{20,16},{24,28},{28,24},{32,36},... | collective-permute-start | bytes 1376264 | tf_op jit(solution)/shard_map/ppermute | solution.py:631
  40.7 1.4 %collective-permute-done.1.swapped = f32[14,64,128]{2,1,0:T(8,128)S(1)} collective-permute-done((f32[14,64,128]{2,1,0:T(8,128)S(1)}, f32[14,64,128]{2,1,0:T(8,128)S(1)}, u32[]{:S(2)}, u32[]{:S(2)}) %collective-permute-start.1) | collective-permute-done | bytes 458784 | tf_op jit(solution)/shard_map/ppermute | solution.py:631
  42.2 0.0 copy-start
  42.2 1.0 copy-done
  43.1 3.0 %shard_map.69 = (f32[22,80,128]{2,1,0:T(8,128)S(1)}, f32[8,20,64,128]{3,2,1,0:T(8,128)S(1)}, f32[20,80,128]{2,1,0:T(8,128)S(1)}, f32[8,64,128]{2,1,0:T(8,128)S(1...) custom-call(f32[8,64,128]{2,1,0:T(8,128)S(1)} %get-tuple-element.24., ...), custom_call_target="tpu_custom_call" | custom-call | flops 1000000 | bytes 1000000 | tf_op jit(solution)/shard_map/pallas_call | solution.py:586
  46.1 6.3 %collective-permute-start.2 = (f32[272,128]{1,0:T(8,128)S(1)}, f32[272,128]{1,0:T(8,128)S(1)}, u32[]{:S(2)}, u32[]{:S(2)}) collective-permute-start(f32[272,128]{1,0:T(8,128)S(1)} %get-tuple-element.33), channel_id=1, source_target_pairs={{4,8},{8,4},{12,16},{16,12},{20,24},{24,20},{28,32},{32,28},{36,40... | collective-permute-start | bytes 417800 | tf_op jit(solution)/shard_map/ppermute | solution.py:641
  52.5 2.7 %collective-permute-done.2.got.near = f32[272,128]{1,0:T(8,128)S(1)} collective-permute-done((f32[272,128]{1,0:T(8,128)S(1)}, f32[272,128]{1,0:T(8,128)S(1)}, u32[]{:S(2)}, u32[]{:S(2)}) %collective-permute-start.2) | collective-permute-done | bytes 139296 | tf_op jit(solution)/shard_map/ppermute | solution.py:641
  55.2 1.9 %collective-permute-start.3 = (f32[272,128]{1,0:T(8,128)S(1)}, f32[272,128]{1,0:T(8,128)S(1)}, u32[]{:S(2)}, u32[]{:S(2)}) collective-permute-start(f32[272,128]{1,0:T(8,128)S(1)} %pad_maximum_fusion), channel_id=1, source_target_pairs={{0,4},{4,0},{8,12},{12,8},{16,20},{20,16},{24,28},{28,24},{32,36},... | collective-permute-start | bytes 417800 | tf_op jit(solution)/shard_map/ppermute | solution.py:645
  57.1 1.3 %collective-permute-done.3.swapped.beside = f32[272,128]{1,0:T(8,128)S(1)} collective-permute-done((f32[272,128]{1,0:T(8,128)S(1)}, f32[272,128]{1,0:T(8,128)S(1)}, u32[]{:S(2)}, u32[]{:S(2)}) %collective-permute-start.3) | collective-permute-done | bytes 139296 | tf_op jit(solution)/shard_map/ppermute | solution.py:645
  58.5 4.8 %shard_map.70 = (f32[10,80,128]{2,1,0:T(8,128)S(1)}, f32[4,64,128]{2,1,0:T(8,128)S(1)}, f32[8,16,64,128]{3,2,1,0:T(8,128)S(1)}, f32[4,64,128]{2,1,0:T(8,128)S(1)}, f32[64,128]{1,0:T(8,128)S(1)}) custom-call(f32[8,20,64,128]{3,2,1,0:T(8,128)S(1)} %get-tuple-element.29.weights_ref, f32[20,80,128]{2,1,0:T(8,128)S(1)} %get-tuple-element.30.pressure_ref, ...), custom_call_target="tpu_custom_call" | custom-call | flops 1000000 | bytes 1000000 | tf_op jit(solution)/shard_map/pallas_call | solution.py:586
  63.2 7.9 %collective-permute-start.4 = (f32[4,64,128]{2,1,0:T(8,128)S(1)}, f32[4,64,128]{2,1,0:T(8,128)S(1)}, u32[]{:S(2)}, u32[]{:S(2)}) collective-permute-start(f32[4,64,128]{2,1,0:T(8,128)S(1)} %get-tuple-element.38), channel_id=1, source_target_pairs={{4,8},{8,4},{12,16},{16,12},{20,24},{24,20},{28,32},{32,28},{36,40... | collective-permute-start | bytes 393224 | tf_op jit(solution)/shard_map/ppermute | solution.py:652
  71.1 2.6 %collective-permute-done.4.got = f32[4,64,128]{2,1,0:T(8,128)S(1)} collective-permute-done((f32[4,64,128]{2,1,0:T(8,128)S(1)}, f32[4,64,128]{2,1,0:T(8,128)S(1)}, u32[]{:S(2)}, u32[]{:S(2)}) %collective-permute-start.4) | collective-permute-done | bytes 131104 | tf_op jit(solution)/shard_map/ppermute | solution.py:652
  73.7 1.9 %collective-permute-start.6 = (f32[4,64,128]{2,1,0:T(8,128)S(1)}, f32[4,64,128]{2,1,0:T(8,128)S(1)}, u32[]{:S(2)}, u32[]{:S(2)}) collective-permute-start(f32[4,64,128]{2,1,0:T(8,128)S(1)} %collective-permute-done.4.got), channel_id=1, source_target_pairs={{0,4},{4,0},{8,12},{12,8},{16,20},{20,16},{24,28},{28,24},{32,36},... | collective-permute-start | bytes 393224 | tf_op jit(solution)/shard_map/ppermute | solution.py:655
  75.7 12.8 %collective-permute-start.5 = (f32[64,128]{1,0:T(8,128)S(1)}, f32[64,128]{1,0:T(8,128)S(1)}, u32[]{:S(2)}, u32[]{:S(2)}) collective-permute-start(f32[64,128]{1,0:T(8,128)S(1)} %get-tuple-element.39), channel_id=1, source_target_pairs={{4,16},{16,4},{12,24},{24,12},{20,32},{32,20},{28,40},{40,28},{36,... | collective-permute-start | bytes 98312 | tf_op jit(solution)/shard_map/ppermute | solution.py:653
  88.5 11.3 %collective-permute-start.7 = (f32[40,128]{1,0:T(8,128)S(1)}, f32[40,128]{1,0:T(8,128)S(1)}, u32[]{:S(2)}, u32[]{:S(2)}) collective-permute-start(f32[40,128]{1,0:T(8,128)S(1)} %get-tuple-element.43), channel_id=1, source_target_pairs={{0,1},{1,2},{2,3},{4,5},{5,6},{6,7},{8,9},{9,10},{10,11},{12,13},{... | collective-permute-start | bytes 61448 | tf_op jit(solution)/shard_map/ppermute | solution.py:642
  99.8 1.3 %collective-permute-start.8 = (f32[40,128]{1,0:T(8,128)S(1)}, f32[40,128]{1,0:T(8,128)S(1)}, u32[]{:S(2)}, u32[]{:S(2)}) collective-permute-start(f32[40,128]{1,0:T(8,128)S(1)} %get-tuple-element.44), channel_id=1, source_target_pairs={{1,0},{2,1},{3,2},{5,4},{6,5},{7,6},{9,8},{10,9},{11,10},{13,12},{... | collective-permute-start | bytes 61448 | tf_op jit(solution)/shard_map/ppermute | solution.py:643
  101.2 0.1 collective-permute-done.7.y_low
  101.3 7.2 %collective-permute-done.8.y_high = f32[40,128]{1,0:T(8,128)S(1)} collective-permute-done((f32[40,128]{1,0:T(8,128)S(1)}, f32[40,128]{1,0:T(8,128)S(1)}, u32[]{:S(2)}, u32[]{:S(2)}) %collective-permute-start.8) | collective-permute-done | bytes 20512 | tf_op jit(solution)/shard_map/ppermute | solution.py:643
  108.5 0.0 collective-permute-done.5.far
  108.5 0.0 collective-permute-done.6.swapped
  108.5 0.0 copy-done.1
  108.5 2.9 %shard_map.73 = (f32[3,4,16,128]{3,2,1,0:T(8,128)}, f32[4,16,128]{2,1,0:T(8,128)}, f32[9,4,16,128]{3,2,1,0:T(8,128)}) custom-call(f32[22,80,128]{2,1,0:T(8,128)S(1)} %get-tuple-element.28.mobile_ref, f32[8,20,64,128]{3,2,1,0:T(8,128)S(1)} %get-tuple-element.29.weights_ref, f32[10,80,128]{2,1,0:T(8,128)S(1)} %get-tuple-element.35.pressure, ...), custom_call_target="tpu_custom_call" | custom-call | flops 1000000 | bytes 1000000 | tf_op jit(solution)/shard_map/pallas_call | solution.py:586
  (4 shorter events, 0.1 us)
Async XLA Ops:
  28.6 79.9 %copy-start.1 = (f32[3,4,16,128]{3,2,1,0:T(8,128)S(1)}, f32[3,4,16,128]{3,2,1,0:T(8,128)}, u32[]{:S(2)}) copy-start(f32[3,4,16,128]{3,2,1,0:T(8,128)} %velocity.1) | copy-start | bytes 294916
  28.7 9.8 %collective-permute-start = (f32[14,64,128]{2,1,0:T(8,128)S(1)}, f32[14,64,128]{2,1,0:T(8,128)S(1)}, u32[]{:S(2)}, u32[]{:S(2)}) collective-permute-start(f32[14,64,128]{2,1,0:T(8,128)S(1)} %get-tuple-element.27), channel_id=1, source_target_pairs={{4,8},{8,4},{12,16},{16,12},{20,24},{24,20},{28,32},{32,28},{36,40... | collective-permute-start | bytes 1376264 | tf_op jit(solution)/shard_map/ppermute | solution.py:630
  38.5 3.7 %collective-permute-start.1 = (f32[14,64,128]{2,1,0:T(8,128)S(1)}, f32[14,64,128]{2,1,0:T(8,128)S(1)}, u32[]{:S(2)}, u32[]{:S(2)}) collective-permute-start(f32[14,64,128]{2,1,0:T(8,128)S(1)} %collective-permute-done.got), channel_id=1, source_target_pairs={{0,4},{4,0},{8,12},{12,8},{16,20},{20,16},{24,28},{28,24},{32,36},... | collective-permute-start | bytes 1376264 | tf_op jit(solution)/shard_map/ppermute | solution.py:631
  42.2 1.0 copy-start
  46.1 9.1 %collective-permute-start.2 = (f32[272,128]{1,0:T(8,128)S(1)}, f32[272,128]{1,0:T(8,128)S(1)}, u32[]{:S(2)}, u32[]{:S(2)}) collective-permute-start(f32[272,128]{1,0:T(8,128)S(1)} %get-tuple-element.33), channel_id=1, source_target_pairs={{4,8},{8,4},{12,16},{16,12},{20,24},{24,20},{28,32},{32,28},{36,40... | collective-permute-start | bytes 417800 | tf_op jit(solution)/shard_map/ppermute | solution.py:641
  55.2 3.3 %collective-permute-start.3 = (f32[272,128]{1,0:T(8,128)S(1)}, f32[272,128]{1,0:T(8,128)S(1)}, u32[]{:S(2)}, u32[]{:S(2)}) collective-permute-start(f32[272,128]{1,0:T(8,128)S(1)} %pad_maximum_fusion), channel_id=1, source_target_pairs={{0,4},{4,0},{8,12},{12,8},{16,20},{20,16},{24,28},{28,24},{32,36},... | collective-permute-start | bytes 417800 | tf_op jit(solution)/shard_map/ppermute | solution.py:645
  63.2 10.5 %collective-permute-start.4 = (f32[4,64,128]{2,1,0:T(8,128)S(1)}, f32[4,64,128]{2,1,0:T(8,128)S(1)}, u32[]{:S(2)}, u32[]{:S(2)}) collective-permute-start(f32[4,64,128]{2,1,0:T(8,128)S(1)} %get-tuple-element.38), channel_id=1, source_target_pairs={{4,8},{8,4},{12,16},{16,12},{20,24},{24,20},{28,32},{32,28},{36,40... | collective-permute-start | bytes 393224 | tf_op jit(solution)/shard_map/ppermute | solution.py:652
  73.7 34.8 %collective-permute-start.6 = (f32[4,64,128]{2,1,0:T(8,128)S(1)}, f32[4,64,128]{2,1,0:T(8,128)S(1)}, u32[]{:S(2)}, u32[]{:S(2)}) collective-permute-start(f32[4,64,128]{2,1,0:T(8,128)S(1)} %collective-permute-done.4.got), channel_id=1, source_target_pairs={{0,4},{4,0},{8,12},{12,8},{16,20},{20,16},{24,28},{28,24},{32,36},... | collective-permute-start | bytes 393224 | tf_op jit(solution)/shard_map/ppermute | solution.py:655
  75.7 32.8 %collective-permute-start.5 = (f32[64,128]{1,0:T(8,128)S(1)}, f32[64,128]{1,0:T(8,128)S(1)}, u32[]{:S(2)}, u32[]{:S(2)}) collective-permute-start(f32[64,128]{1,0:T(8,128)S(1)} %get-tuple-element.39), channel_id=1, source_target_pairs={{4,16},{16,4},{12,24},{24,12},{20,32},{32,20},{28,40},{40,28},{36,... | collective-permute-start | bytes 98312 | tf_op jit(solution)/shard_map/ppermute | solution.py:653
  88.5 12.8 %collective-permute-start.7 = (f32[40,128]{1,0:T(8,128)S(1)}, f32[40,128]{1,0:T(8,128)S(1)}, u32[]{:S(2)}, u32[]{:S(2)}) collective-permute-start(f32[40,128]{1,0:T(8,128)S(1)} %get-tuple-element.43), channel_id=1, source_target_pairs={{0,1},{1,2},{2,3},{4,5},{5,6},{6,7},{8,9},{9,10},{10,11},{12,13},{... | collective-permute-start | bytes 61448 | tf_op jit(solution)/shard_map/ppermute | solution.py:642
  99.8 8.7 %collective-permute-start.8 = (f32[40,128]{1,0:T(8,128)S(1)}, f32[40,128]{1,0:T(8,128)S(1)}, u32[]{:S(2)}, u32[]{:S(2)}) collective-permute-start(f32[40,128]{1,0:T(8,128)S(1)} %get-tuple-element.44), channel_id=1, source_target_pairs={{1,0},{2,1},{3,2},{5,4},{6,5},{7,6},{9,8},{10,9},{11,10},{13,12},{... | collective-permute-start | bytes 61448 | tf_op jit(solution)/shard_map/ppermute | solution.py:643

commit v4 on v3

--- a/solution.py
+++ b/solution.py
@@ -262,7 +262,7 @@
     out[144:160] = velocity[0, 3]
 
 
-def assemble(n_chips, gathered, mobile, target, edge, sent):
+def assemble(n_chips, gathered, sent, sent_far, edge):
     north, _, _ = whereabouts(n_chips)
     row = rows_of((BLOCK, LANES))
     for c in range(4):
@@ -270,7 +270,7 @@
         for k in range(2):
             block = 2 * c + k
             for x in range(4):
-                mobile[4 * k + x, rows] = gathered[block, BLOCK * x : BLOCK * (x + 1)]
+                sent[4 * k + x, rows] = gathered[block, BLOCK * x : BLOCK * (x + 1)]
                 t = gathered[block, 64 + BLOCK * x : 64 + BLOCK * (x + 1)]
                 r = EDGE + x
                 if c > 0:
@@ -281,106 +281,97 @@
                     t = t + 0.5 * gathered[block + 1, 128:144]
                 if k == 1 and x == 0:
                     t = t - 0.5 * gathered[block - 1, 144:160]
-                target[4 * k + x, rows] = t
+                sent[8 + 4 * k + x, rows] = t
         edge[0, rows] = gathered[2 * c, 128:144]
         edge[1, rows] = gathered[2 * c + 1, 144:160]
-    one, two = jnp.where(north, 0, 1), jnp.where(north, 0, 2)
-    for i in range(7):
-        sent[i] = mobile[one + i]
-    for i in range(6):
-        sent[7 + i] = target[two + i]
-    sent[13] = edge[one]
+    u = edge[jnp.where(north, 0, 1)]
+    sent[16] = u
+    sent_far[0] = sent[jnp.where(north, 0, 7)]
+    sent_far[1] = u
+
+
+def species_edges(n_chips, species, near, beside, edge_low, edge_high):
+    north, _, _ = whereabouts(n_chips)
+    outward, inward = jnp.where(north, 0, 3), jnp.where(north, 3, 0)
+    for s in range(SPECIES):
+        near[BLOCK * s : BLOCK * (s + 1)] = species[s, outward]
+        beside[BLOCK * s : BLOCK * (s + 1)] = species[s, inward]
+        for x in range(4):
+            r = 4 * s + x
+            edge_low[r : r + 1] = species[s, x, 0:1]
+            edge_high[r : r + 1] = species[s, x, BLOCK - 1 : BLOCK]
+    edge_low[36:40] = jnp.zeros((4, LANES), jnp.float32)
+    edge_high[36:40] = jnp.zeros((4, LANES), jnp.float32)
+
+
+def flow_rims(n_chips, gathered, u_beside, v_rims):
+    north, cross, _ = whereabouts(n_chips)
+    core = jnp.where(north, 0, 1)
+    partner = 2 * cross + jnp.where(north, 1, 0)
+    u_beside[...] = jnp.where(north, gathered[partner, 128:144], gathered[partner, 144:160])
+    below = gathered[2 * jnp.maximum(cross - 1, 0) + core, EDGE:OWN]
+    above = gathered[2 * jnp.minimum(cross + 1, 3) + core, EDGE:OWN]
+    v_rims[0:4] = jnp.where(cross > 0, below[4:8], 0.0)
+    v_rims[4:8] = jnp.where(cross < 3, above[0:4], 0.0)
 
 
 def first_cycle(
-    n_chips, mobile, target, edge, got, swapped, species,
-    mobile_ref, weights_ref, pressure_ref, residual, coarse, outer, sent, rim, edge_low, edge_high,
+    n_chips, own, edge, mine, swapped, species_near,
+    mobile_ref, weights_ref, pressure_ref, residual, coarse, outer, sent,
     target_w, field_ref,
 ):
     north, _, chip = whereabouts(n_chips)
     clear_pads(mobile_ref)
     clear_pads(field_ref)
     clear_pads(pressure_ref)
-    mobile_w, pressure = Field(mobile_ref, -7), Field(pressure_ref, -6)
-    field = Field(field_ref, -6)
-
-    def sides(i):
-        a, b = got[i], swapped[i]
+    mobile_w, pressure = Field(mobile_ref, -9), Field(pressure_ref, -8)
+    field = Field(field_ref, -8)
+
+    def sides(k):
+        a, b = mine[k], swapped[k]
         return jnp.where(north, a, b), jnp.where(north, b, a)
 
-    def copy_mobile(i):
-        left, right = sides((i + 7).index())
-        mobile_w.put(i, left)
-        mobile_w.put(i + 15, right)
-
-    loop(-7, 0, copy_mobile)
-
-    def copy_block(i):
-        mobile_w.put(i, mobile[i.index()])
-        target_w[(i + 6).index()] = target[i.index()]
-
-    loop(0, 8, copy_block)
-
-    def copy_target(i):
-        left, right = sides((i + 7).index())
-        target_w[i.index()] = left
-        target_w[(i + 14).index()] = right
-
-    loop(0, 6, copy_target)
-    left, right = sides(13)
-    target_w[5] = target_w[5] + 0.5 * edge[0]
-    target_w[6] = target_w[6] - 0.5 * left
-    target_w[13] = target_w[13] + 0.5 * right
-    target_w[14] = target_w[14] - 0.5 * edge[1]
-    outer[...] = got[13]
-
-    weights = Weights(weights_ref, 1, -6)
-    weights.fill(-6, 14, mobile_w, at(target_w, -6), inside_of(8 * chip, 8 * n_chips))
-    first_sweep(weights, field, -6, 14)
-    sweep(weights, field, pressure, -5, 13)
-    residual_planes(weights, pressure, residual, -2, -2, 6)
+    def copy(i):
+        k, later = i.index(), (i + 8).index()
+        left, right = sides(k)
+        mobile_w.put(i - 8, left)
+        mobile_w.put(i, own[k])
+        mobile_w.put(i + 8, right)
+        left, right = sides(later)
+        target_w[k] = left
+        target_w[later] = own[later]
+        target_w[(i + 16).index()] = right
+
+    loop(0, 8, copy)
+    left, right = sides(17)
+    mobile_w.put(Place(0, -9), left)
+    mobile_w.put(Place(0, 16), right)
+    left, right = sides(18)
+    target_w[0] = target_w[0] - 0.5 * left
+    target_w[23] = target_w[23] + 0.5 * right
+    left, right = sides(16)
+    target_w[7] = target_w[7] + 0.5 * edge[0]
+    target_w[8] = target_w[8] - 0.5 * left
+    target_w[15] = target_w[15] + 0.5 * right
+    target_w[16] = target_w[16] - 0.5 * edge[1]
+    outer[...] = mine[16]
+
+    weights = Weights(weights_ref, 1, -8)
+    weights.fill(-8, 16, mobile_w, at(target_w, -8), inside_of(8 * chip, 8 * n_chips))
+    first_sweep(weights, field, -8, 16)
+    sweep(weights, field, pressure, -7, 15)
+    residual_planes(weights, pressure, residual, -3, -3, 7)
 
     def restrict(i):
         pair = mobile_w(2 * i) + mobile_w(2 * i + 1)
-        coarse[(i + 3).index()] = 0.125 * pair_sum(pair)
-
-    loop(-3, 7, restrict)
-    r = jnp.where(north, 4, 0)
+        coarse[(i + 4).index()] = 0.125 * pair_sum(pair)
+
+    loop(-4, 8, restrict)
+    r = jnp.where(north, 6, 0)
     sent[0:64] = packed(residual[r], residual[r + 1], residual[r + 2], residual[r + 3])
-    m = jnp.where(north, 6, 0)
+    m = jnp.where(north, 8, 0)
     sent[64:128] = packed(coarse[m], coarse[m + 1], coarse[m + 2], coarse[m + 3])
-    near, beside = jnp.where(north, 0, 3), jnp.where(north, 3, 0)
-    for s in range(SPECIES):
-        sent[128 + BLOCK * s : 144 + BLOCK * s] = species[s, near]
-        rim[BLOCK * s : BLOCK * (s + 1)] = species[s, beside]
-        for x in range(4):
-            r = 4 * s + x
-            edge_low[r : r + 1] = species[s, x, 0:1]
-            edge_high[r : r + 1] = species[s, x, BLOCK - 1 : BLOCK]
-    edge_low[36:40] = jnp.zeros((4, LANES), jnp.float32)
-    edge_high[36:40] = jnp.zeros((4, LANES), jnp.float32)
-
-
-def flow_rims(n_chips, gathered, outer, u_rims, v_rims):
-    north, cross, _ = whereabouts(n_chips)
-    core = jnp.where(north, 0, 1)
-    start = pl.multiple_of(cross * BLOCK, BLOCK)
-    partner = 2 * cross + jnp.where(north, 1, 0)
-    first, last = gathered[partner, 128:144], gathered[partner, 144:160]
-    beyond = outer[pl.ds(start, BLOCK)]
-    u_rims[0] = jnp.where(north, beyond, last)
-    u_rims[1] = jnp.where(north, first, beyond)
-    below = gathered[2 * jnp.maximum(cross - 1, 0) + core, EDGE:OWN]
-    above = gathered[2 * jnp.minimum(cross + 1, 3) + core, EDGE:OWN]
-    v_rims[0:4] = jnp.where(cross > 0, below[4:8], 0.0)
-    v_rims[4:8] = jnp.where(cross < 3, above[0:4], 0.0)
-
-
-def species_rims(n_chips, near, beside, rims):
-    north, _, _ = whereabouts(n_chips)
-    a, b = near[128:272], beside[128:272]
-    rims[0] = jnp.where(north, a, b)
-    rims[1] = jnp.where(north, b, a)
+    sent[128:272] = species_near[...]
 
 
 def coarse_sweeps(weights, one, two, low, high):
@@ -390,43 +381,46 @@
     sweep(weights, one, two, low + 3, high - 3)
 
 
+def inner(n_chips, chip):
+    return chip > 0, chip < n_chips - 1
+
+
 def second_cycle(
-    n_chips, weights_ref, pressure_ref, residual, coarse, got, swapped,
-    pressure_new_ref, residual_new, coarse_weights_ref, sent, sent_far,
+    n_chips, weights_ref, pressure_ref, residual, coarse, got,
+    pressure_new_ref, residual_new, coarse_weights_ref, sent,
     coarse_ref, residual_w, one_ref, two_ref, field_ref, other_ref,
 ):
     north, _, chip = whereabouts(n_chips)
+    before, after = inner(n_chips, chip)
     for ref in (pressure_new_ref, coarse_ref, one_ref, two_ref, field_ref, other_ref):
         clear_pads(ref)
-    coarse_w, one, two = Field(coarse_ref, -7), Field(one_ref, -6), Field(two_ref, -6)
-    field, other = Field(field_ref, -6), Field(other_ref, -6)
-    pressure, pressure_new = Field(pressure_ref, -6), Field(pressure_new_ref, -1)
-
-    def sides(low):
-        a, b = got[low : low + 64], swapped[low : low + 64]
-        return unpacked(jnp.where(north, a, b)), unpacked(jnp.where(north, b, a))
-
-    left, right = sides(0)
+    coarse_w, one, two = Field(coarse_ref, -8), Field(one_ref, -7), Field(two_ref, -7)
+    field, other = Field(field_ref, -8), Field(other_ref, -8)
+    pressure, pressure_new = Field(pressure_ref, -8), Field(pressure_new_ref, -3)
+
+    left = unpacked(jnp.where(before, got[0, 0:64], 0.0))
+    right = unpacked(jnp.where(after, got[1, 272:336], 0.0))
     for i in range(4):
         residual_w[i] = left[i]
-        residual_w[12 + i] = right[i]
-    left, right = sides(64)
+        residual_w[14 + i] = right[i]
+    left = unpacked(jnp.where(before, got[0, 64:128], 0.0))
+    right = unpacked(jnp.where(after, got[1, 336:400], 0.0))
     for i in range(4):
-        coarse_w.put(Place(0, i - 7), left[i])
-        coarse_w.put(Place(0, i + 7), right[i])
+        coarse_w.put(Place(0, i - 8), left[i])
+        coarse_w.put(Place(0, i + 8), right[i])
 
     def copy_residual(i):
         residual_w[(i + 4).index()] = residual[i.index()]
 
     def copy_coarse(i):
-        coarse_w.put(i - 3, coarse[i.index()])
-
-    loop(0, 8, copy_residual)
-    loop(0, 10, copy_coarse)
-
-    coarse_weights = Weights(coarse_weights_ref, 2, -6)
-    coarse_weights.fill(-6, 10, coarse_w, at(residual_w, -6), inside_of(4 * chip, 4 * n_chips))
-    coarse_sweeps(coarse_weights, one, two, -6, 10)
+        coarse_w.put(i - 4, coarse[i.index()])
+
+    loop(0, 10, copy_residual)
+    loop(0, 12, copy_coarse)
+
+    coarse_weights = Weights(coarse_weights_ref, 2, -7)
+    coarse_weights.fill(-7, 11, coarse_w, at(residual_w, -7), inside_of(4 * chip, 4 * n_chips))
+    coarse_sweeps(coarse_weights, one, two, -7, 11)
 
     def prolong(i):
         correction = two(i)
@@ -434,52 +428,51 @@
             k = 2 * i + half
             field.put(k, pressure(k) + correction)
 
-    loop(-3, 7, prolong)
-
-    weights = Weights(weights_ref, 1, -6)
+    loop(-4, 8, prolong)
+
+    weights = Weights(weights_ref, 1, -8)
+    sweep(weights, field, other, -6, 14)
+    sweep(weights, other, field, -5, 13)
     sweep(weights, field, other, -4, 12)
-    sweep(weights, other, field, -3, 11)
-    sweep(weights, field, other, -2, 10)
-    sweep(weights, other, pressure_new, -1, 9)
-    residual_planes(weights, pressure_new, residual_new, 0, 0, 4)
-    first = jnp.where(north, 2, 5)
-    for i in range(3):
-        sent[i] = pressure_new_ref[first + i, PAD : PAD + ROWS]
-    sent[3] = packed(residual_new[0], residual_new[1], residual_new[2], residual_new[3])
-    sent_far[...] = residual_new[jnp.where(north, 0, 3)]
+    sweep(weights, other, pressure_new, -3, 11)
+    residual_planes(weights, pressure_new, residual_new, -1, -1, 5)
+    sent[0] = pressure_new_ref[jnp.where(north, 6, 7), PAD : PAD + ROWS]
+    r = jnp.where(north, 2, 0)
+    sent[1] = packed(
+        residual_new[r], residual_new[r + 1], residual_new[r + 2], residual_new[r + 3]
+    )
 
 
 def finish(
-    n_chips, mobile_ref, weights_ref, pressure, residual, coarse_weights_ref, got, far, swapped,
-    velocity, species, u_rims, v_rims, x_rims, y_low, y_high,
+    n_chips, mobile_ref, weights_ref, pressure, residual, coarse_weights_ref, got, swapped,
+    velocity, species, outer, u_beside, v_rims, sides, y_low, y_high,
     velocity_out, pressure_out, species_out,
     residual_w, pressure_w, one_ref, two_ref, field_ref, other_ref, final_pad,
 ):
-    north, cross, _ = whereabouts(n_chips)
+    north, cross, chip = whereabouts(n_chips)
+    before, after = inner(n_chips, chip)
     for ref in (one_ref, two_ref, field_ref, other_ref, final_pad):
         clear_pads(ref)
     one, two = Field(one_ref, -5), Field(two_ref, -5)
     field, other, final = Field(field_ref, -4), Field(other_ref, -4), Field(final_pad, -2)
-    a, b = got[3], swapped[3]
-    left, right = unpacked(jnp.where(north, a, b)), unpacked(jnp.where(north, b, a))
+    left = unpacked(jnp.where(before, swapped[0, 0], 0.0))
+    right = unpacked(jnp.where(after, swapped[1, 1], 0.0))
     for i in range(4):
-        residual_w[1 + i] = left[i]
-        residual_w[5 + i] = residual[i]
-        residual_w[9 + i] = right[i]
-    residual_w[0] = far[...]
-    residual_w[13] = far[...]
-    for i in range(3):
-        pressure_w[i] = got[i]
-        pressure_w[13 + i] = got[i]
-    known = Field(pressure, -1)
+        residual_w[i] = left[i]
+        residual_w[10 + i] = right[i]
+    for i in range(6):
+        residual_w[4 + i] = residual[i]
+    pressure_w[0] = jnp.where(before, got[0, 0], 0.0)
+    pressure_w[15] = jnp.where(after, got[1, 0], 0.0)
+    known = Field(pressure, -3)
 
     def copy_pressure(i):
         pressure_w[(i + 4).index()] = known(i)
 
-    loop(-1, 9, copy_pressure)
+    loop(-3, 11, copy_pressure)
 
     shift, coarse_shift = jnp.where(north, 0, 4), jnp.where(north, 0, 2)
-    coarse_weights = Weights(coarse_weights_ref, 2, -6, coarse_shift, at(residual_w, -5))
+    coarse_weights = Weights(coarse_weights_ref, 2, -7, coarse_shift, at(residual_w, -5))
 
     def right_side(i):
         k = (i + 5).index()
@@ -498,7 +491,7 @@
 
     loop(-2, 4, prolong)
 
-    weights = Weights(weights_ref, 1, -6, shift)
+    weights = Weights(weights_ref, 1, -8, shift)
     sweep(weights, field, other, -3, 7)
     sweep(weights, other, final, -2, 6)
 
@@ -506,21 +499,33 @@
     own = pl.ds(start + 8, BLOCK)
     row, lane = rows_of((BLOCK, LANES)), lanes_of((BLOCK, LANES))
 
+    beyond = outer[pl.ds(start, BLOCK)]
+    u_low = jnp.where(north, beyond, u_beside[...])
+    u_high = jnp.where(north, u_beside[...], beyond)
+
     def u_out(x):
         if x < 0:
-            u = u_rims[0]
+            u = u_low
         elif x > 3:
-            u = u_rims[1]
+            u = u_high
         else:
             u = velocity[0, x]
         slope = 0.5 * (final_pad[x + 3, own] - final_pad[x + 1, own])
-        return u - mobile_ref[shift + (x + 7), own] * slope
+        return u - mobile_ref[shift + (x + 9), own] * slope
 
     u = [u_out(x) for x in range(-1, 5)]
+
+    def species_beside(s, side):
+        at_rim = BLOCK * s + (128 if side == 0 else 400)
+        outside = sides[side, at_rim : at_rim + BLOCK]
+        outside = jnp.where(before if side == 0 else after, outside, 0.0)
+        inside = sides[side, 544 + BLOCK * s : 560 + BLOCK * s]
+        return jnp.where(north, outside, inside) if side == 0 else jnp.where(north, inside, outside)
+
     wide = pl.ds(start, 32)
     for x in range(4):
         p = final_pad[x + 2, wide]
-        m = mobile_ref[shift + (x + 7), wide]
+        m = mobile_ref[shift + (x + 9), wide]
         p_own = p[8:24]
         v = velocity[1, x] - m[8:24] * (0.5 * (p[9:25] - p[7:23]))
         v_low = v_rims[x : x + 1] - m[7:8] * (0.5 * (p[8:9] - p[6:7]))
@@ -559,15 +564,14 @@
         from_zp = jnp.where(lane < LANES - 1, -time_step * jnp.minimum(flow_zp, 0.0), 0.0)
         for s in range(SPECIES):
             c = species[s, x]
-            rim = slice(BLOCK * s, BLOCK * (s + 1))
             if x > 0:
                 c_xm = species[s, x - 1]
             else:
-                c_xm = x_rims[0, rim]
+                c_xm = species_beside(s, 0)
             if x < 3:
                 c_xp = species[s, x + 1]
             else:
-                c_xp = x_rims[1, rim]
+                c_xp = species_beside(s, 1)
             r = 4 * s + x
             c_ym = jnp.where(row == 0, y_low[r : r + 1], roll_rows(c, 1))
             c_yp = jnp.where(row == BLOCK - 1, y_high[r : r + 1], roll_rows(c, -1))
@@ -595,8 +599,23 @@
     )(*operands)
 
 
+def gathered_over(array, groups):
+    return lax.all_gather(array, ("slab", "cross"), axis_index_groups=groups)
+
+
 def local(n_chips, velocity, density, source, species):
-    groups = [[(2 * j + k) * 4 + c for c in range(4) for k in range(2)] for j in range(n_chips)]
+    def device(slab, cross):
+        return 4 * slab + cross
+
+    chips = [[device(2 * j + k, c) for c in range(4) for k in range(2)] for j in range(n_chips)]
+    cores = [
+        [device(2 * j, c), device(2 * j + 1, c)] for j in range(n_chips) for c in range(4)
+    ]
+    facing = [
+        [device(2 * j + 1, c), device(2 * j + 2, c)] for j in range(n_chips - 1) for c in range(4)
+    ]
+    for slab in (0, 2 * n_chips - 1):
+        facing += [[device(slab, 0), device(slab, 1)], [device(slab, 2), device(slab, 3)]]
 
     def beside(distance):
         pairs = []
@@ -623,42 +642,42 @@
         velocity, density, source,
         where=HBM, semaphores=3, grant=63,
     )
-    gathered = lax.all_gather(own, ("slab", "cross"), axis_index_groups=groups)
-    mobile, target, edge, sent = call(
-        bind(assemble), [plane(8), plane(8), plane(2), plane(14)], [], gathered
+    gathered = gathered_over(own, chips)
+    sent, sent_far, edge = call(bind(assemble), [plane(17), plane(2), plane(2)], [], gathered)
+    near = lax.ppermute(sent, "slab", beside(1))
+    far = lax.ppermute(sent_far, "slab", beside(2))
+    species_near, species_beside, edge_low, edge_high = call(
+        bind(species_edges), [(144, LANES), (144, LANES), (40, LANES), (40, LANES)], [], species
     )
-    got = lax.ppermute(sent, "slab", beside(1))
-    swapped = lax.ppermute(got, "slab", within)
-    mobile_w, weights, pressure, residual, coarse, outer, sent, rim, edge_low, edge_high = call(
+    y_low = lax.ppermute(edge_high, "cross", upward)
+    y_high = lax.ppermute(edge_low, "cross", downward)
+    u_beside, v_rims = call(bind(flow_rims), [(BLOCK, LANES), (8, LANES)], [], gathered)
+    mine = jnp.concatenate([near, far], 0)
+    swapped = lax.ppermute(mine, "slab", within)
+    mobile_w, weights, pressure, residual, coarse, outer, sent_two = call(
         bind(first_cycle),
         [
-            padded(22), (8, *plane(20)), padded(20), plane(8), plane(10), PLANE, (272, LANES),
-            (144, LANES), (40, LANES), (40, LANES),
+            padded(26), (8, *plane(24)), padded(24), plane(10), plane(12), PLANE, (272, LANES),
         ],
-        [plane(20), padded(20)],
-        mobile, target, edge, got, swapped, species,
+        [plane(24), padded(24)],
+        sent, edge, mine, swapped, species_near,
     )
-    near = lax.ppermute(sent, "slab", beside(1))
-    y_low = lax.ppermute(edge_high, "cross", upward)
-    y_high = lax.ppermute(edge_low, "cross", downward)
-    u_rims, v_rims = call(bind(flow_rims), [(2, BLOCK, LANES), (8, LANES)], [], gathered, outer)
-    opposite = lax.ppermute(jnp.concatenate([near[:128], rim], 0), "slab", within)
-    pressure, residual, coarse_weights, sent, sent_far = call(
+    near = gathered_over(sent_two, facing).reshape(544, LANES)
+    sides = gathered_over(jnp.concatenate([near, species_beside], 0), cores)
+    pressure, residual, coarse_weights, sent = call(
         bind(second_cycle),
-        [padded(10), plane(4), (8, *plane(16)), plane(4), PLANE],
-        [padded(18), plane(16), padded(16), padded(16), padded(20), padded(20)],
-        weights, pressure, residual, coarse, near, opposite,
+        [padded(14), plane(6), (8, *plane(18)), plane(2)],
+        [padded(20), plane(18), padded(18), padded(18), padded(24), padded(24)],
+        weights, pressure, residual, coarse, sides,
     )
-    got = lax.ppermute(sent, "slab", beside(1))
-    far = lax.ppermute(sent_far, "slab", beside(2))
-    (x_rims,) = call(bind(species_rims), [(2, 144, LANES)], [], near, opposite)
-    swapped = lax.ppermute(got, "slab", within)
+    near = gathered_over(sent, facing)
+    swapped = gathered_over(near[:, 1], cores)
     return call(
         bind(finish),
         [velocity.shape, density.shape, species.shape],
         [plane(14), plane(16), padded(12), padded(12), padded(12), padded(12), padded(8)],
-        mobile_w, weights, pressure, residual, coarse_weights, got, far, swapped,
-        velocity, species, u_rims, v_rims, x_rims, y_low, y_high,
+        mobile_w, weights, pressure, residual, coarse_weights, near, swapped,
+        velocity, species, outer, u_beside, v_rims, sides, y_low, y_high,
     )
 
 

time: 112 us -> 97.7 us (0.87)
  the two profiles are of different devices: /device:TPU:72 before, /device:TPU:257 now
where the time goes in v4:
time: 97.7 us; the launch traced here: 97.4 us
  blocking collectives  49.4 us (51%)
  starting transfers between devices  23.9 us (24%)
  Pallas kernels  16 us (16%)
  waiting for transfers between devices  6.24 us (6%)
  local copies, waits for them, and re-layouts  1.01 us (1%)
    all_gather x5, blocking collectives, gathered_over(): return lax.all_gather(array, ('slab', 'cross'), axis_index_groups=groups)  49.4 us
    pallas_call x7, Pallas kernels, call(): pl.pallas_call(kernel, out_shape=shapes, in_specs=[pl.BlockSpec(memory_sp...  16 us
    ppermute x1, starting transfers between devices, local(): swapped = lax.ppermute(mine, 'slab', within)  9.01 us
    ppermute x1, starting transfers between devices, local(): y_high = lax.ppermute(edge_low, 'cross', downward)  6.37 us
    ppermute x1, waiting for transfers between devices, local(): near = lax.ppermute(sent, 'slab', beside(1))  4.51 us
    ppermute x1, starting transfers between devices, local(): far = lax.ppermute(sent_far, 'slab', beside(2))  3.32 us
    ppermute x1, starting transfers between devices, local(): near = lax.ppermute(sent, 'slab', beside(1))  3.3 us
  transfers between devices with their start and end apart: 5, of which 2 were waited for; matrix products, arithmetic and copies ran while one was open for 0% of the time, Pallas kernels for 11%

profile of v4, /device:TPU:257, one launch (start us, length us, event | category | flops | bytes accessed | tf_op | source)
XLA Modules:
  0.0 97.4 jit_solution(1032883110887135479)
XLA Ops:
  0.6 1.7 %shard_map.67 = f32[168,128]{1,0:T(8,128)} custom-call(f32[3,4,16,128]{3,2,1,0:T(8,128)} %velocity.1, f32[4,16,128]{2,1,0:T(8,128)} %density_in.1, f32[4,16,128]{2,1,0:T(8,128)} %source_in.1), custom_call_target="tpu_custom_call" | custom-call | flops 1000000 | bytes 1000000 | tf_op jit(solution)/shard_map/pallas_call | solution.py:590
  2.3 24.6 %all-gather = f32[1344,128]{1,0:T(8,128)S(1)} all-gather(f32[168,128]{1,0:T(8,128)} %shard_map.67), channel_id=2, replica_groups={{0,4,1,5,2,6,3,7},{8,12,9,13,10,14,11,15},{16,20,17,21,18,22,19,23},{24..., dimensions={0}, use_global_device_ids=true | all-gather | bytes 774144 | tf_op jit(solution)/shard_map/all_gather | solution.py:603
  26.9 0.1 shard_map.68
  27.0 3.3 %collective-permute-start = (f32[17,64,128]{2,1,0:T(8,128)S(1)}, f32[17,64,128]{2,1,0:T(8,128)S(1)}, u32[]{:S(2)}, u32[]{:S(2)}) collective-permute-start(f32[17,64,128]{2,1,0:T(8,128)S(1)} %get-tuple-element.23.own), channel_id=1, source_target_pairs={{4,8},{8,4},{12,16},{16,12},{20,24},{24,20},{28,32},{32,28},{36,40... | collective-permute-start | bytes 1671176 | tf_op jit(solution)/shard_map/ppermute | solution.py:647
  30.3 3.3 %collective-permute-start.1 = (f32[2,64,128]{2,1,0:T(8,128)S(1)}, f32[2,64,128]{2,1,0:T(8,128)S(1)}, u32[]{:S(2)}, u32[]{:S(2)}) collective-permute-start(f32[2,64,128]{2,1,0:T(8,128)S(1)} %get-tuple-element.25), channel_id=1, source_target_pairs={{4,16},{16,4},{12,24},{24,12},{20,32},{32,20},{28,40},{40,28},{36,... | collective-permute-start | bytes 196616 | tf_op jit(solution)/shard_map/ppermute | solution.py:648
  33.6 4.5 %collective-permute-done = f32[17,64,128]{2,1,0:T(8,128)S(1)} collective-permute-done((f32[17,64,128]{2,1,0:T(8,128)S(1)}, f32[17,64,128]{2,1,0:T(8,128)S(1)}, u32[]{:S(2)}, u32[]{:S(2)}) %collective-permute-start) | collective-permute-done | bytes 557088 | tf_op jit(solution)/shard_map/ppermute | solution.py:647
  38.2 1.7 %collective-permute-done.1 = f32[2,64,128]{2,1,0:T(8,128)S(1)} collective-permute-done((f32[2,64,128]{2,1,0:T(8,128)S(1)}, f32[2,64,128]{2,1,0:T(8,128)S(1)}, u32[]{:S(2)}, u32[]{:S(2)}) %collective-permute-start.1) | collective-permute-done | bytes 65568 | tf_op jit(solution)/shard_map/ppermute | solution.py:648
  39.9 9.0 %collective-permute-start.2 = (f32[19,64,128]{2,1,0:T(8,128)S(1)}, f32[19,64,128]{2,1,0:T(8,128)S(1)}, u32[]{:S(2)}, u32[]{:S(2)}) collective-permute-start(f32[19,64,128]{2,1,0:T(8,128)S(1)} %constant_dynamic-update-slice_fusion.mine), channel_id=1, source_target_pairs={{0,4},{4,0},{8,12},{12,8},{16,20},{20,16},{24,28},{28,24},{32,36},... | collective-permute-start | bytes 1867784 | tf_op jit(solution)/shard_map/ppermute | solution.py:656
  48.9 0.0 copy-start
  48.9 1.0 copy-done
  49.9 1.9 %collective-permute-start.3 = (f32[40,128]{1,0:T(8,128)S(1)}, f32[40,128]{1,0:T(8,128)S(1)}, u32[]{:S(2)}, u32[]{:S(2)}) collective-permute-start(f32[40,128]{1,0:T(8,128)S(1)} %get-tuple-element.41), channel_id=1, source_target_pairs={{0,1},{1,2},{2,3},{4,5},{5,6},{6,7},{8,9},{9,10},{10,11},{12,13},{... | collective-permute-start | bytes 61448 | tf_op jit(solution)/shard_map/ppermute | solution.py:652
  51.9 6.4 %collective-permute-start.4 = (f32[40,128]{1,0:T(8,128)S(1)}, f32[40,128]{1,0:T(8,128)S(1)}, u32[]{:S(2)}, u32[]{:S(2)}) collective-permute-start(f32[40,128]{1,0:T(8,128)S(1)} %get-tuple-element.42), channel_id=1, source_target_pairs={{1,0},{2,1},{3,2},{5,4},{6,5},{7,6},{9,8},{10,9},{11,10},{13,12},{... | collective-permute-start | bytes 61448 | tf_op jit(solution)/shard_map/ppermute | solution.py:653
  58.3 0.0 collective-permute-done.2.swapped
  58.3 4.5 %shard_map.70 = (f32[26,80,128]{2,1,0:T(8,128)S(1)}, f32[8,24,64,128]{3,2,1,0:T(8,128)S(1)}, f32[24,80,128]{2,1,0:T(8,128)S(1)}, f32[10,64,128]{2,1,0:T(8,128)S(...) custom-call(f32[17,64,128]{2,1,0:T(8,128)S(1)} %get-tuple-element.23.own, ...), custom_call_target="tpu_custom_call" | custom-call | flops 1000000 | bytes 1000000 | tf_op jit(solution)/shard_map/pallas_call | solution.py:590
  62.8 5.2 %all-gather.1 = f32[544,128]{1,0:T(8,128)S(1)} all-gather(f32[272,128]{1,0:T(8,128)S(1)} %get-tuple-element.32), channel_id=3, replica_groups={{4,8},{5,9},{6,10},{7,11},{12,16},{13,17},{14,18},{15,19},{20,24},{21,2..., dimensions={0}, use_global_device_ids=true | all-gather | bytes 417792 | tf_op jit(solution)/shard_map/all_gather | solution.py:603
  68.0 7.9 %all-gather.2 = f32[1376,128]{1,0:T(8,128)S(1)} all-gather(f32[688,128]{1,0:T(8,128)S(1)} %pad_maximum_fusion), channel_id=4, replica_groups={{0,4},{1,5},{2,6},{3,7},{8,12},{9,13},{10,14},{11,15},{16,20},{17,21},{..., dimensions={0}, use_global_device_ids=true | all-gather | bytes 1056768 | tf_op jit(solution)/shard_map/all_gather | solution.py:603
  75.9 0.0 copy-start.1
  75.9 0.0 copy-start.2
  75.9 6.5 %shard_map.71 = (f32[14,80,128]{2,1,0:T(8,128)S(1)}, f32[6,64,128]{2,1,0:T(8,128)S(1)}, f32[8,18,64,128]{3,2,1,0:T(8,128)S(1)}, f32[2,64,128]{2,1,0:T(8,128)S(1)}) custom-call(f32[8,24,64,128]{3,2,1,0:T(8,128)S(1)} %get-tuple-element.28.weights_ref, f32[24,80,128]{2,1,0:T(8,128)S(1)} %get-tuple-element.29.pressure_ref, ...), custom_call_target="tpu_custom_call" | custom-call | flops 1000000 | bytes 1000000 | tf_op jit(solution)/shard_map/pallas_call | solution.py:590
  82.5 4.4 %all-gather.3 = f32[4,64,128]{2,1,0:T(8,128)S(1)} all-gather(f32[2,64,128]{2,1,0:T(8,128)S(1)} %get-tuple-element.37), channel_id=5, replica_groups={{4,8},{5,9},{6,10},{7,11},{12,16},{13,17},{14,18},{15,19},{20,24},{21,2..., dimensions={0}, use_global_device_ids=true | all-gather | bytes 196608 | tf_op jit(solution)/shard_map/all_gather | solution.py:603
  86.8 7.3 %all-gather.4 = f32[4,1,64,128]{3,2,1,0:T(8,128)S(1)} all-gather(f32[2,1,64,128]{3,2,1,0:T(8,128)S(1)} %slice.4), channel_id=6, replica_groups={{0,4},{1,5},{2,6},{3,7},{8,12},{9,13},{10,14},{11,15},{16,20},{17,21},{..., dimensions={0}, use_global_device_ids=true | all-gather | bytes 196608 | tf_op jit(solution)/shard_map/all_gather | solution.py:603
  94.2 0.0 collective-permute-done.3.y_low
  94.2 0.0 collective-permute-done.4.y_high
  94.2 0.0 copy-done.1
  94.2 0.0 copy-done.2
  94.2 3.2 %shard_map.73 = (f32[3,4,16,128]{3,2,1,0:T(8,128)}, f32[4,16,128]{2,1,0:T(8,128)}, f32[9,4,16,128]{3,2,1,0:T(8,128)}) custom-call(f32[26,80,128]{2,1,0:T(8,128)S(1)} %get-tuple-element.27.mobile_ref, f32[8,24,64,128]{3,2,1,0:T(8,128)S(1)} %get-tuple-element.28.weights_ref, f32[14,80,128]{2,1,0:T(8,128)S(1)} %get-tuple-element.34.pressure, ...), custom_call_target="tpu_custom_call" | custom-call | flops 1000000 | bytes 1000000 | tf_op jit(solution)/shard_map/pallas_call | solution.py:590
  (6 shorter events, 0.1 us)
Async XLA Ops:
  27.0 11.1 %collective-permute-start = (f32[17,64,128]{2,1,0:T(8,128)S(1)}, f32[17,64,128]{2,1,0:T(8,128)S(1)}, u32[]{:S(2)}, u32[]{:S(2)}) collective-permute-start(f32[17,64,128]{2,1,0:T(8,128)S(1)} %get-tuple-element.23.own), channel_id=1, source_target_pairs={{4,8},{8,4},{12,16},{16,12},{20,24},{24,20},{28,32},{32,28},{36,40... | collective-permute-start | bytes 1671176 | tf_op jit(solution)/shard_map/ppermute | solution.py:647
  30.3 9.6 %collective-permute-start.1 = (f32[2,64,128]{2,1,0:T(8,128)S(1)}, f32[2,64,128]{2,1,0:T(8,128)S(1)}, u32[]{:S(2)}, u32[]{:S(2)}) collective-permute-start(f32[2,64,128]{2,1,0:T(8,128)S(1)} %get-tuple-element.25), channel_id=1, source_target_pairs={{4,16},{16,4},{12,24},{24,12},{20,32},{32,20},{28,40},{40,28},{36,... | collective-permute-start | bytes 196616 | tf_op jit(solution)/shard_map/ppermute | solution.py:648
  39.9 18.4 %collective-permute-start.2 = (f32[19,64,128]{2,1,0:T(8,128)S(1)}, f32[19,64,128]{2,1,0:T(8,128)S(1)}, u32[]{:S(2)}, u32[]{:S(2)}) collective-permute-start(f32[19,64,128]{2,1,0:T(8,128)S(1)} %constant_dynamic-update-slice_fusion.mine), channel_id=1, source_target_pairs={{0,4},{4,0},{8,12},{12,8},{16,20},{20,16},{24,28},{28,24},{32,36},... | collective-permute-start | bytes 1867784 | tf_op jit(solution)/shard_map/ppermute | solution.py:656
  48.9 1.0 copy-start
  49.9 44.2 %collective-permute-start.3 = (f32[40,128]{1,0:T(8,128)S(1)}, f32[40,128]{1,0:T(8,128)S(1)}, u32[]{:S(2)}, u32[]{:S(2)}) collective-permute-start(f32[40,128]{1,0:T(8,128)S(1)} %get-tuple-element.41), channel_id=1, source_target_pairs={{0,1},{1,2},{2,3},{4,5},{5,6},{6,7},{8,9},{9,10},{10,11},{12,13},{... | collective-permute-start | bytes 61448 | tf_op jit(solution)/shard_map/ppermute | solution.py:652
  51.9 42.3 %collective-permute-start.4 = (f32[40,128]{1,0:T(8,128)S(1)}, f32[40,128]{1,0:T(8,128)S(1)}, u32[]{:S(2)}, u32[]{:S(2)}) collective-permute-start(f32[40,128]{1,0:T(8,128)S(1)} %get-tuple-element.42), channel_id=1, source_target_pairs={{1,0},{2,1},{3,2},{5,4},{6,5},{7,6},{9,8},{10,9},{11,10},{13,12},{... | collective-permute-start | bytes 61448 | tf_op jit(solution)/shard_map/ppermute | solution.py:653
  75.9 18.2 %copy-start.1 = (f32[9,4,16,128]{3,2,1,0:T(8,128)S(1)}, f32[9,4,16,128]{3,2,1,0:T(8,128)}, u32[]{:S(2)}) copy-start(f32[9,4,16,128]{3,2,1,0:T(8,128)} %species.3) | copy-start | bytes 884740
  75.9 18.2 %copy-start.2 = (f32[3,4,16,128]{3,2,1,0:T(8,128)S(1)}, f32[3,4,16,128]{3,2,1,0:T(8,128)}, u32[]{:S(2)}) copy-start(f32[3,4,16,128]{3,2,1,0:T(8,128)} %velocity.1) | copy-start | bytes 294916

commit v5 on v4

--- a/solution.py
+++ b/solution.py
@@ -128,33 +128,33 @@
             scaled = (damping * valid) / (diagonal + (1.0 - valid))
             half = 0.5 * scaled
             k = self.place(i)
-            self.ref[0, k] = (m + x_m) * half
-            self.ref[1, k] = (m + x_p) * half
-            self.ref[2, k] = (m + y_m) * half
-            self.ref[3, k] = (m + y_p) * half
-            self.ref[4, k] = jnp.where(z_low, (m + z_m) * half, 0.0)
-            self.ref[5, k] = jnp.where(z_high, (m + z_p) * half, 0.0)
+            self.ref[0, k, 0:ROWS] = (m + x_m) * half
+            self.ref[1, k, 0:ROWS] = (m + x_p) * half
+            self.ref[2, k, 0:ROWS] = (m + y_m) * half
+            self.ref[3, k, 0:ROWS] = (m + y_p) * half
+            self.ref[4, k, 0:ROWS] = jnp.where(z_low, (m + z_m) * half, 0.0)
+            self.ref[5, k, 0:ROWS] = jnp.where(z_high, (m + z_p) * half, 0.0)
             if s == 1:
-                self.ref[6, k] = target(i) * scaled
-                self.ref[7, k] = diagonal * (1.0 / damping)
+                self.ref[6, k, 0:ROWS] = target(i) * scaled
+                self.ref[7, k, 0:ROWS] = diagonal * (1.0 / damping)
             else:
-                self.ref[6, k] = target(i) * (4.0 * scaled)
-                self.ref[7, k] = 4.0 * scaled
+                self.ref[6, k, 0:ROWS] = target(i) * (4.0 * scaled)
+                self.ref[7, k, 0:ROWS] = 4.0 * scaled
 
         loop(low, high, body)
 
     def side(self, i):
         if self.constant is not None:
             return self.constant(i)
-        return self.ref[6, self.place(i)]
+        return self.ref[6, self.place(i), 0:ROWS]
 
     def change(self, field, i):
         s = self.step
         k = self.place(i)
         p = field(i)
-        total = self.ref[0, k] * field(i - 1) + self.ref[1, k] * field(i + 1)
-        total = total + (self.ref[2, k] * field(i, -s) + self.ref[3, k] * field(i, s))
-        total = total + (self.ref[4, k] * roll_lanes(p, s) + self.ref[5, k] * roll_lanes(p, -s))
+        total = self.ref[0, k, 0:ROWS] * field(i - 1) + self.ref[1, k, 0:ROWS] * field(i + 1)
+        total = total + (self.ref[2, k, 0:ROWS] * field(i, -s) + self.ref[3, k, 0:ROWS] * field(i, s))
+        total = total + (self.ref[4, k, 0:ROWS] * roll_lanes(p, s) + self.ref[5, k, 0:ROWS] * roll_lanes(p, -s))
         return p, (total - self.side(i)) - damping * p
 
 
@@ -209,7 +209,7 @@
         total = 0.0
         for half in range(2):
             _, change = weights.change(field, 2 * i + half)
-            total = total - change * weights.ref[7, weights.place(2 * i + half)]
+            total = total - change * weights.ref[7, weights.place(2 * i + half), 0:ROWS]
         result[(i - result_low).index()] = 0.125 * pair_sum(total)
 
     loop(low, high, body)
@@ -391,20 +391,17 @@
     coarse_ref, residual_w, one_ref, two_ref, field_ref, other_ref,
 ):
     north, _, chip = whereabouts(n_chips)
-    before, after = inner(n_chips, chip)
     for ref in (pressure_new_ref, coarse_ref, one_ref, two_ref, field_ref, other_ref):
         clear_pads(ref)
     coarse_w, one, two = Field(coarse_ref, -8), Field(one_ref, -7), Field(two_ref, -7)
     field, other = Field(field_ref, -8), Field(other_ref, -8)
     pressure, pressure_new = Field(pressure_ref, -8), Field(pressure_new_ref, -3)
 
-    left = unpacked(jnp.where(before, got[0, 0:64], 0.0))
-    right = unpacked(jnp.where(after, got[1, 272:336], 0.0))
+    left, right = unpacked(got[0, 0:64]), unpacked(got[1, 0:64])
     for i in range(4):
         residual_w[i] = left[i]
         residual_w[14 + i] = right[i]
-    left = unpacked(jnp.where(before, got[0, 64:128], 0.0))
-    right = unpacked(jnp.where(after, got[1, 336:400], 0.0))
+    left, right = unpacked(got[0, 64:128]), unpacked(got[1, 64:128])
     for i in range(4):
         coarse_w.put(Place(0, i - 8), left[i])
         coarse_w.put(Place(0, i + 8), right[i])
@@ -476,7 +473,7 @@
 
     def right_side(i):
         k = (i + 5).index()
-        factor = coarse_weights_ref[7, coarse_weights.place(i)]
+        factor = coarse_weights_ref[7, coarse_weights.place(i), 0:ROWS]
         residual_w[k] = residual_w[(i + 5).index(coarse_shift)] * factor
 
     for k in range(12):
@@ -516,10 +513,8 @@
     u = [u_out(x) for x in range(-1, 5)]
 
     def species_beside(s, side):
-        at_rim = BLOCK * s + (128 if side == 0 else 400)
-        outside = sides[side, at_rim : at_rim + BLOCK]
-        outside = jnp.where(before if side == 0 else after, outside, 0.0)
-        inside = sides[side, 544 + BLOCK * s : 560 + BLOCK * s]
+        outside = sides[side, 128 + BLOCK * s : 144 + BLOCK * s]
+        inside = sides[side, 272 + BLOCK * s : 288 + BLOCK * s]
         return jnp.where(north, outside, inside) if side == 0 else jnp.where(north, inside, outside)
 
     wide = pl.ds(start, 32)
@@ -634,6 +629,9 @@
     def padded(n):
         return (n, *PADDED)
 
+    def skewed(n):
+        return (8, n + (1 - n) % 4, ROWS + 8, LANES)
+
     def bind(kernel):
         return functools.partial(kernel, n_chips)
 
@@ -649,24 +647,24 @@
     species_near, species_beside, edge_low, edge_high = call(
         bind(species_edges), [(144, LANES), (144, LANES), (40, LANES), (40, LANES)], [], species
     )
-    y_low = lax.ppermute(edge_high, "cross", upward)
-    y_high = lax.ppermute(edge_low, "cross", downward)
-    u_beside, v_rims = call(bind(flow_rims), [(BLOCK, LANES), (8, LANES)], [], gathered)
     mine = jnp.concatenate([near, far], 0)
     swapped = lax.ppermute(mine, "slab", within)
     mobile_w, weights, pressure, residual, coarse, outer, sent_two = call(
         bind(first_cycle),
         [
-            padded(26), (8, *plane(24)), padded(24), plane(10), plane(12), PLANE, (272, LANES),
+            padded(26), skewed(24), padded(24), plane(10), plane(12), PLANE, (272, LANES),
         ],
         [plane(24), padded(24)],
         sent, edge, mine, swapped, species_near,
     )
-    near = gathered_over(sent_two, facing).reshape(544, LANES)
+    near = lax.ppermute(sent_two, "slab", beside(1))
+    y_low = lax.ppermute(edge_high, "cross", upward)
+    y_high = lax.ppermute(edge_low, "cross", downward)
+    u_beside, v_rims = call(bind(flow_rims), [(BLOCK, LANES), (8, LANES)], [], gathered)
     sides = gathered_over(jnp.concatenate([near, species_beside], 0), cores)
     pressure, residual, coarse_weights, sent = call(
         bind(second_cycle),
-        [padded(14), plane(6), (8, *plane(18)), plane(2)],
+        [padded(14), plane(6), skewed(18), plane(2)],
         [padded(20), plane(18), padded(18), padded(18), padded(24), padded(24)],
         weights, pressure, residual, coarse, sides,
     )

time: 97.7 us -> 93.5 us (0.957)
  the two profiles are of different devices: /device:TPU:257 before, /device:TPU:65 now
where the time goes in v5:
time: 93.5 us; the launch traced here: 93.1 us
  blocking collectives  42.9 us (46%)
  starting transfers between devices  25.6 us (27%)
  Pallas kernels  15.9 us (17%)
  waiting for transfers between devices  6.87 us (7%)
  local copies, waits for them, and re-layouts  1.02 us (1%)
    all_gather x4, blocking collectives, gathered_over(): return lax.all_gather(array, ('slab', 'cross'), axis_index_groups=groups)  42.9 us
    pallas_call x7, Pallas kernels, call(): pl.pallas_call(kernel, out_shape=shapes, in_specs=[pl.BlockSpec(memory_sp...  15.9 us
    ppermute x1, starting transfers between devices, local(): y_low = lax.ppermute(edge_high, 'cross', upward)  8.38 us
    ppermute x1, starting transfers between devices, local(): swapped = lax.ppermute(mine, 'slab', within)  7.34 us
    ppermute x1, waiting for transfers between devices, local(): near = lax.ppermute(sent, 'slab', beside(1))  4.58 us
    ppermute x1, starting transfers between devices, local(): far = lax.ppermute(sent_far, 'slab', beside(2))  3.32 us
    ppermute x1, starting transfers between devices, local(): near = lax.ppermute(sent, 'slab', beside(1))  3.23 us
    ppermute x1, starting transfers between devices, local(): near = lax.ppermute(sent_two, 'slab', beside(1))  2.05 us
  transfers between devices with their start and end apart: 6, of which 3 were waited for; matrix products, arithmetic and copies ran while one was open for 0% of the time, Pallas kernels for 7%

profile of v5, /device:TPU:65, one launch (start us, length us, event | category | flops | bytes accessed | tf_op | source)
XLA Modules:
  0.0 93.1 jit_solution(1951406787280293578)
XLA Ops:
  0.6 1.7 %shard_map.67 = f32[168,128]{1,0:T(8,128)} custom-call(f32[3,4,16,128]{3,2,1,0:T(8,128)} %velocity.1, f32[4,16,128]{2,1,0:T(8,128)} %density_in.1, f32[4,16,128]{2,1,0:T(8,128)} %source_in.1), custom_call_target="tpu_custom_call" | custom-call | flops 1000000 | bytes 1000000 | tf_op jit(solution)/shard_map/pallas_call | solution.py:585
  2.3 26.8 %all-gather = f32[1344,128]{1,0:T(8,128)S(1)} all-gather(f32[168,128]{1,0:T(8,128)} %shard_map.67), channel_id=2, replica_groups={{0,4,1,5,2,6,3,7},{8,12,9,13,10,14,11,15},{16,20,17,21,18,22,19,23},{24..., dimensions={0}, use_global_device_ids=true | all-gather | bytes 774144 | tf_op jit(solution)/shard_map/all_gather | solution.py:598
  29.1 0.1 shard_map.68
  29.2 3.2 %collective-permute-start = (f32[17,64,128]{2,1,0:T(8,128)S(1)}, f32[17,64,128]{2,1,0:T(8,128)S(1)}, u32[]{:S(2)}, u32[]{:S(2)}) collective-permute-start(f32[17,64,128]{2,1,0:T(8,128)S(1)} %get-tuple-element.23.own), channel_id=1, source_target_pairs={{4,8},{8,4},{12,16},{16,12},{20,24},{24,20},{28,32},{32,28},{36,40... | collective-permute-start | bytes 1671176 | tf_op jit(solution)/shard_map/ppermute | solution.py:645
  32.4 3.3 %collective-permute-start.1 = (f32[2,64,128]{2,1,0:T(8,128)S(1)}, f32[2,64,128]{2,1,0:T(8,128)S(1)}, u32[]{:S(2)}, u32[]{:S(2)}) collective-permute-start(f32[2,64,128]{2,1,0:T(8,128)S(1)} %get-tuple-element.25), channel_id=1, source_target_pairs={{4,16},{16,4},{12,24},{24,12},{20,32},{32,20},{28,40},{40,28},{36,... | collective-permute-start | bytes 196616 | tf_op jit(solution)/shard_map/ppermute | solution.py:646
  35.7 4.6 %collective-permute-done = f32[17,64,128]{2,1,0:T(8,128)S(1)} collective-permute-done((f32[17,64,128]{2,1,0:T(8,128)S(1)}, f32[17,64,128]{2,1,0:T(8,128)S(1)}, u32[]{:S(2)}, u32[]{:S(2)}) %collective-permute-start) | collective-permute-done | bytes 557088 | tf_op jit(solution)/shard_map/ppermute | solution.py:645
  40.4 1.6 %collective-permute-done.1 = f32[2,64,128]{2,1,0:T(8,128)S(1)} collective-permute-done((f32[2,64,128]{2,1,0:T(8,128)S(1)}, f32[2,64,128]{2,1,0:T(8,128)S(1)}, u32[]{:S(2)}, u32[]{:S(2)}) %collective-permute-start.1) | collective-permute-done | bytes 65568 | tf_op jit(solution)/shard_map/ppermute | solution.py:646
  42.0 7.3 %collective-permute-start.2 = (f32[19,64,128]{2,1,0:T(8,128)S(1)}, f32[19,64,128]{2,1,0:T(8,128)S(1)}, u32[]{:S(2)}, u32[]{:S(2)}) collective-permute-start(f32[19,64,128]{2,1,0:T(8,128)S(1)} %constant_dynamic-update-slice_fusion.mine), channel_id=1, source_target_pairs={{0,4},{4,0},{8,12},{12,8},{16,20},{20,16},{24,28},{28,24},{32,36},... | collective-permute-start | bytes 1867784 | tf_op jit(solution)/shard_map/ppermute | solution.py:651
  49.4 0.0 copy-start
  49.4 1.0 %copy-done = f32[9,4,16,128]{3,2,1,0:T(8,128)S(1)} copy-done((f32[9,4,16,128]{3,2,1,0:T(8,128)S(1)}, f32[9,4,16,128]{3,2,1,0:T(8,128)}, u32[]{:S(2)}) %copy-start) | copy-done | bytes 294936
  50.4 0.6 collective-permute-done.2.swapped
  51.0 4.5 %shard_map.70 = (f32[26,80,128]{2,1,0:T(8,128)S(1)}, f32[8,25,72,128]{3,2,1,0:T(8,128)S(1)}, f32[24,80,128]{2,1,0:T(8,128)S(1)}, f32[10,64,128]{2,1,0:T(8,128)S(...) custom-call(f32[17,64,128]{2,1,0:T(8,128)S(1)} %get-tuple-element.23.own, ...), custom_call_target="tpu_custom_call" | custom-call | flops 1000000 | bytes 1000000 | tf_op jit(solution)/shard_map/pallas_call | solution.py:585
  55.5 0.0 copy-start.1
  55.5 0.0 copy-start.2
  55.5 2.1 %collective-permute-start.3 = (f32[272,128]{1,0:T(8,128)S(1)}, f32[272,128]{1,0:T(8,128)S(1)}, u32[]{:S(2)}, u32[]{:S(2)}) collective-permute-start(f32[272,128]{1,0:T(8,128)S(1)} %get-tuple-element.32), channel_id=1, source_target_pairs={{4,8},{8,4},{12,16},{16,12},{20,24},{24,20},{28,32},{32,28},{36,40... | collective-permute-start | bytes 417800 | tf_op jit(solution)/shard_map/ppermute | solution.py:660
  57.6 8.4 %collective-permute-start.4 = (f32[40,128]{1,0:T(8,128)S(1)}, f32[40,128]{1,0:T(8,128)S(1)}, u32[]{:S(2)}, u32[]{:S(2)}) collective-permute-start(f32[40,128]{1,0:T(8,128)S(1)} %get-tuple-element.41), channel_id=1, source_target_pairs={{0,1},{1,2},{2,3},{4,5},{5,6},{6,7},{8,9},{9,10},{10,11},{12,13},{... | collective-permute-start | bytes 61448 | tf_op jit(solution)/shard_map/ppermute | solution.py:661
  66.0 1.3 %collective-permute-start.5 = (f32[40,128]{1,0:T(8,128)S(1)}, f32[40,128]{1,0:T(8,128)S(1)}, u32[]{:S(2)}, u32[]{:S(2)}) collective-permute-start(f32[40,128]{1,0:T(8,128)S(1)} %get-tuple-element.42), channel_id=1, source_target_pairs={{1,0},{2,1},{3,2},{5,4},{6,5},{7,6},{9,8},{10,9},{11,10},{13,12},{... | collective-permute-start | bytes 61448 | tf_op jit(solution)/shard_map/ppermute | solution.py:662
  67.3 0.0 collective-permute-done.3
  67.4 5.6 %all-gather.1 = f32[832,128]{1,0:T(8,128)S(1)} all-gather(f32[416,128]{1,0:T(8,128)S(1)} %pad_maximum_fusion), channel_id=3, replica_groups={{0,4},{1,5},{2,6},{3,7},{8,12},{9,13},{10,14},{11,15},{16,20},{17,21},{..., dimensions={0}, use_global_device_ids=true | all-gather | bytes 638976 | tf_op jit(solution)/shard_map/all_gather | solution.py:598
  73.0 6.5 %shard_map.71 = (f32[14,80,128]{2,1,0:T(8,128)S(1)}, f32[6,64,128]{2,1,0:T(8,128)S(1)}, f32[8,21,72,128]{3,2,1,0:T(8,128)S(1)}, f32[2,64,128]{2,1,0:T(8,128)S(1)}) custom-call(f32[8,25,72,128]{3,2,1,0:T(8,128)S(1)} %get-tuple-element.28.weights_ref, f32[24,80,128]{2,1,0:T(8,128)S(1)} %get-tuple-element.29.pressure_ref, ...), custom_call_target="tpu_custom_call" | custom-call | flops 1000000 | bytes 1000000 | tf_op jit(solution)/shard_map/pallas_call | solution.py:585
  79.5 4.4 %all-gather.2 = f32[4,64,128]{2,1,0:T(8,128)S(1)} all-gather(f32[2,64,128]{2,1,0:T(8,128)S(1)} %get-tuple-element.37), channel_id=4, replica_groups={{4,8},{5,9},{6,10},{7,11},{12,16},{13,17},{14,18},{15,19},{20,24},{21,2..., dimensions={0}, use_global_device_ids=true | all-gather | bytes 196608 | tf_op jit(solution)/shard_map/all_gather | solution.py:598
  83.8 6.1 %all-gather.3 = f32[4,1,64,128]{3,2,1,0:T(8,128)S(1)} all-gather(f32[2,1,64,128]{3,2,1,0:T(8,128)S(1)} %slice.4), channel_id=5, replica_groups={{0,4},{1,5},{2,6},{3,7},{8,12},{9,13},{10,14},{11,15},{16,20},{17,21},{..., dimensions={0}, use_global_device_ids=true | all-gather | bytes 196608 | tf_op jit(solution)/shard_map/all_gather | solution.py:598
  90.0 0.0 collective-permute-done.4.y_low
  90.0 0.0 collective-permute-done.5.y_high
  90.0 0.0 copy-done.1
  90.0 0.0 copy-done.2
  90.0 3.2 %shard_map.73 = (f32[3,4,16,128]{3,2,1,0:T(8,128)}, f32[4,16,128]{2,1,0:T(8,128)}, f32[9,4,16,128]{3,2,1,0:T(8,128)}) custom-call(f32[26,80,128]{2,1,0:T(8,128)S(1)} %get-tuple-element.27.mobile_ref, f32[8,25,72,128]{3,2,1,0:T(8,128)S(1)} %get-tuple-element.28.weights_ref, f32[14,80,128]{2,1,0:T(8,128)S(1)} %get-tuple-element.34.pressure, ...), custom_call_target="tpu_custom_call" | custom-call | flops 1000000 | bytes 1000000 | tf_op jit(solution)/shard_map/pallas_call | solution.py:585
  (6 shorter events, 0.1 us)
Async XLA Ops:
  29.2 11.1 %collective-permute-start = (f32[17,64,128]{2,1,0:T(8,128)S(1)}, f32[17,64,128]{2,1,0:T(8,128)S(1)}, u32[]{:S(2)}, u32[]{:S(2)}) collective-permute-start(f32[17,64,128]{2,1,0:T(8,128)S(1)} %get-tuple-element.23.own), channel_id=1, source_target_pairs={{4,8},{8,4},{12,16},{16,12},{20,24},{24,20},{28,32},{32,28},{36,40... | collective-permute-start | bytes 1671176 | tf_op jit(solution)/shard_map/ppermute | solution.py:645
  32.4 9.6 %collective-permute-start.1 = (f32[2,64,128]{2,1,0:T(8,128)S(1)}, f32[2,64,128]{2,1,0:T(8,128)S(1)}, u32[]{:S(2)}, u32[]{:S(2)}) collective-permute-start(f32[2,64,128]{2,1,0:T(8,128)S(1)} %get-tuple-element.25), channel_id=1, source_target_pairs={{4,16},{16,4},{12,24},{24,12},{20,32},{32,20},{28,40},{40,28},{36,... | collective-permute-start | bytes 196616 | tf_op jit(solution)/shard_map/ppermute | solution.py:646
  42.0 9.0 %collective-permute-start.2 = (f32[19,64,128]{2,1,0:T(8,128)S(1)}, f32[19,64,128]{2,1,0:T(8,128)S(1)}, u32[]{:S(2)}, u32[]{:S(2)}) collective-permute-start(f32[19,64,128]{2,1,0:T(8,128)S(1)} %constant_dynamic-update-slice_fusion.mine), channel_id=1, source_target_pairs={{0,4},{4,0},{8,12},{12,8},{16,20},{20,16},{24,28},{28,24},{32,36},... | collective-permute-start | bytes 1867784 | tf_op jit(solution)/shard_map/ppermute | solution.py:651
  49.4 1.0 %copy-start = (f32[9,4,16,128]{3,2,1,0:T(8,128)S(1)}, f32[9,4,16,128]{3,2,1,0:T(8,128)}, u32[]{:S(2)}) copy-start(f32[9,4,16,128]{3,2,1,0:T(8,128)} %species.3) | copy-start | bytes 884740
  55.5 34.4 %copy-start.1 = (f32[9,4,16,128]{3,2,1,0:T(8,128)S(1)}, f32[9,4,16,128]{3,2,1,0:T(8,128)}, u32[]{:S(2)}) copy-start(f32[9,4,16,128]{3,2,1,0:T(8,128)} %species.3) | copy-start | bytes 884740
  55.5 34.4 %copy-start.2 = (f32[3,4,16,128]{3,2,1,0:T(8,128)S(1)}, f32[3,4,16,128]{3,2,1,0:T(8,128)}, u32[]{:S(2)}) copy-start(f32[3,4,16,128]{3,2,1,0:T(8,128)} %velocity.1) | copy-start | bytes 294916
  55.5 11.8 %collective-permute-start.3 = (f32[272,128]{1,0:T(8,128)S(1)}, f32[272,128]{1,0:T(8,128)S(1)}, u32[]{:S(2)}, u32[]{:S(2)}) collective-permute-start(f32[272,128]{1,0:T(8,128)S(1)} %get-tuple-element.32), channel_id=1, source_target_pairs={{4,8},{8,4},{12,16},{16,12},{20,24},{24,20},{28,32},{32,28},{36,40... | collective-permute-start | bytes 417800 | tf_op jit(solution)/shard_map/ppermute | solution.py:660
  57.6 32.3 %collective-permute-start.4 = (f32[40,128]{1,0:T(8,128)S(1)}, f32[40,128]{1,0:T(8,128)S(1)}, u32[]{:S(2)}, u32[]{:S(2)}) collective-permute-start(f32[40,128]{1,0:T(8,128)S(1)} %get-tuple-element.41), channel_id=1, source_target_pairs={{0,1},{1,2},{2,3},{4,5},{5,6},{6,7},{8,9},{9,10},{10,11},{12,13},{... | collective-permute-start | bytes 61448 | tf_op jit(solution)/shard_map/ppermute | solution.py:661
  66.0 24.0 %collective-permute-start.5 = (f32[40,128]{1,0:T(8,128)S(1)}, f32[40,128]{1,0:T(8,128)S(1)}, u32[]{:S(2)}, u32[]{:S(2)}) collective-permute-start(f32[40,128]{1,0:T(8,128)S(1)} %get-tuple-element.42), channel_id=1, source_target_pairs={{1,0},{2,1},{3,2},{5,4},{6,5},{7,6},{9,8},{10,9},{11,10},{13,12},{... | collective-permute-start | bytes 61448 | tf_op jit(solution)/shard_map/ppermute | solution.py:662

commit v6 on v4

--- a/solution.py
+++ b/solution.py
@@ -40,21 +40,8 @@
 
 
 def loop(low, high, body):
-    count = high - low
-    some = next(u for u in (4, 5, 6, 3, 7, 2, 1) if count % u == 0)
-
-    def several(start):
-        for u in range(some):
-            body(Place(start, low + u))
-
-    def step(i, carry):
-        several(i * some)
-        return carry
-
-    if count == some:
-        several(0)
-    else:
-        lax.fori_loop(0, count // some, step, 0)
+    for u in range(high - low):
+        body(Place(0, low + u))
 
 
 def rows_of(shape):

time: 97.7 us -> 94.8 us (0.970)
  Pallas kernels: 16 us -> 13.2 us
    pallas_call x7, Pallas kernels: 16 us -> 13.2 us  [call(): pl.pallas_call(kernel, out_shape=shapes, in_specs=[pl.BlockSpec(memory_sp...]
  transfers between devices with their start and end apart: 5 -> 5, of which waited for: 2 -> 2; matrix products, arithmetic and copies ran while one was open for 0% -> 0% of each run, Pallas kernels for 11% -> 9%
where the time goes in v6:
time: 94.8 us; the launch traced here: 94.5 us
  blocking collectives  49.4 us (52%)
  starting transfers between devices  23.9 us (25%)
  Pallas kernels  13.2 us (14%)
  waiting for transfers between devices  6.24 us (7%)
  local copies, waits for them, and re-layouts  1.01 us (1%)
    all_gather x5, blocking collectives, gathered_over(): return lax.all_gather(array, ('slab', 'cross'), axis_index_groups=groups)  49.4 us
    pallas_call x7, Pallas kernels, call(): pl.pallas_call(kernel, out_shape=shapes, in_specs=[pl.BlockSpec(memory_sp...  13.2 us
    ppermute x1, starting transfers between devices, local(): swapped = lax.ppermute(mine, 'slab', within)  9.01 us
    ppermute x1, starting transfers between devices, local(): y_high = lax.ppermute(edge_low, 'cross', downward)  6.37 us
    ppermute x1, waiting for transfers between devices, local(): near = lax.ppermute(sent, 'slab', beside(1))  4.51 us
    ppermute x1, starting transfers between devices, local(): far = lax.ppermute(sent_far, 'slab', beside(2))  3.32 us
    ppermute x1, starting transfers between devices, local(): near = lax.ppermute(sent, 'slab', beside(1))  3.3 us
    ppermute x1, starting transfers between devices, local(): y_low = lax.ppermute(edge_high, 'cross', upward)  1.92 us
  transfers between devices with their start and end apart: 5, of which 2 were waited for; matrix products, arithmetic and copies ran while one was open for 0% of the time, Pallas kernels for 9%

profile of v6, /device:TPU:257, one launch (start us, length us, event | category | flops | bytes accessed | tf_op | source)
XLA Modules:
  0.0 94.5 jit_solution(1513685102071694981)
XLA Ops:
  0.6 1.7 %shard_map.67 = f32[168,128]{1,0:T(8,128)} custom-call(f32[3,4,16,128]{3,2,1,0:T(8,128)} %velocity.1, f32[4,16,128]{2,1,0:T(8,128)} %density_in.1, f32[4,16,128]{2,1,0:T(8,128)} %source_in.1), custom_call_target="tpu_custom_call" | custom-call | flops 1000000 | bytes 1000000 | tf_op jit(solution)/shard_map/pallas_call | solution.py:577
  2.3 24.6 %all-gather = f32[1344,128]{1,0:T(8,128)S(1)} all-gather(f32[168,128]{1,0:T(8,128)} %shard_map.67), channel_id=2, replica_groups={{0,4,1,5,2,6,3,7},{8,12,9,13,10,14,11,15},{16,20,17,21,18,22,19,23},{24..., dimensions={0}, use_global_device_ids=true | all-gather | bytes 774144 | tf_op jit(solution)/shard_map/all_gather | solution.py:590
  26.9 0.1 shard_map.68
  27.0 3.3 %collective-permute-start = (f32[17,64,128]{2,1,0:T(8,128)S(1)}, f32[17,64,128]{2,1,0:T(8,128)S(1)}, u32[]{:S(2)}, u32[]{:S(2)}) collective-permute-start(f32[17,64,128]{2,1,0:T(8,128)S(1)} %get-tuple-element.23.own), channel_id=1, source_target_pairs={{4,8},{8,4},{12,16},{16,12},{20,24},{24,20},{28,32},{32,28},{36,40... | collective-permute-start | bytes 1671176 | tf_op jit(solution)/shard_map/ppermute | solution.py:634
  30.3 3.3 %collective-permute-start.1 = (f32[2,64,128]{2,1,0:T(8,128)S(1)}, f32[2,64,128]{2,1,0:T(8,128)S(1)}, u32[]{:S(2)}, u32[]{:S(2)}) collective-permute-start(f32[2,64,128]{2,1,0:T(8,128)S(1)} %get-tuple-element.25), channel_id=1, source_target_pairs={{4,16},{16,4},{12,24},{24,12},{20,32},{32,20},{28,40},{40,28},{36,... | collective-permute-start | bytes 196616 | tf_op jit(solution)/shard_map/ppermute | solution.py:635
  33.6 4.5 %collective-permute-done = f32[17,64,128]{2,1,0:T(8,128)S(1)} collective-permute-done((f32[17,64,128]{2,1,0:T(8,128)S(1)}, f32[17,64,128]{2,1,0:T(8,128)S(1)}, u32[]{:S(2)}, u32[]{:S(2)}) %collective-permute-start) | collective-permute-done | bytes 557088 | tf_op jit(solution)/shard_map/ppermute | solution.py:634
  38.2 1.7 %collective-permute-done.1 = f32[2,64,128]{2,1,0:T(8,128)S(1)} collective-permute-done((f32[2,64,128]{2,1,0:T(8,128)S(1)}, f32[2,64,128]{2,1,0:T(8,128)S(1)}, u32[]{:S(2)}, u32[]{:S(2)}) %collective-permute-start.1) | collective-permute-done | bytes 65568 | tf_op jit(solution)/shard_map/ppermute | solution.py:635
  39.9 9.0 %collective-permute-start.2 = (f32[19,64,128]{2,1,0:T(8,128)S(1)}, f32[19,64,128]{2,1,0:T(8,128)S(1)}, u32[]{:S(2)}, u32[]{:S(2)}) collective-permute-start(f32[19,64,128]{2,1,0:T(8,128)S(1)} %constant_dynamic-update-slice_fusion.mine), channel_id=1, source_target_pairs={{0,4},{4,0},{8,12},{12,8},{16,20},{20,16},{24,28},{28,24},{32,36},... | collective-permute-start | bytes 1867784 | tf_op jit(solution)/shard_map/ppermute | solution.py:643
  48.9 0.0 copy-start
  48.9 1.0 %copy-done = f32[9,4,16,128]{3,2,1,0:T(8,128)S(1)} copy-done((f32[9,4,16,128]{3,2,1,0:T(8,128)S(1)}, f32[9,4,16,128]{3,2,1,0:T(8,128)}, u32[]{:S(2)}) %copy-start) | copy-done | bytes 294936
  49.9 1.9 %collective-permute-start.3 = (f32[40,128]{1,0:T(8,128)S(1)}, f32[40,128]{1,0:T(8,128)S(1)}, u32[]{:S(2)}, u32[]{:S(2)}) collective-permute-start(f32[40,128]{1,0:T(8,128)S(1)} %get-tuple-element.41), channel_id=1, source_target_pairs={{0,1},{1,2},{2,3},{4,5},{5,6},{6,7},{8,9},{9,10},{10,11},{12,13},{... | collective-permute-start | bytes 61448 | tf_op jit(solution)/shard_map/ppermute | solution.py:639
  51.9 6.4 %collective-permute-start.4 = (f32[40,128]{1,0:T(8,128)S(1)}, f32[40,128]{1,0:T(8,128)S(1)}, u32[]{:S(2)}, u32[]{:S(2)}) collective-permute-start(f32[40,128]{1,0:T(8,128)S(1)} %get-tuple-element.42), channel_id=1, source_target_pairs={{1,0},{2,1},{3,2},{5,4},{6,5},{7,6},{9,8},{10,9},{11,10},{13,12},{... | collective-permute-start | bytes 61448 | tf_op jit(solution)/shard_map/ppermute | solution.py:640
  58.3 0.0 collective-permute-done.2.swapped
  58.3 3.4 %shard_map.70 = (f32[26,80,128]{2,1,0:T(8,128)S(1)}, f32[8,24,64,128]{3,2,1,0:T(8,128)S(1)}, f32[24,80,128]{2,1,0:T(8,128)S(1)}, f32[10,64,128]{2,1,0:T(8,128)S(...) custom-call(f32[17,64,128]{2,1,0:T(8,128)S(1)} %get-tuple-element.23.own, ...), custom_call_target="tpu_custom_call" | custom-call | flops 1000000 | bytes 1000000 | tf_op jit(solution)/shard_map/pallas_call | solution.py:577
  61.7 5.2 %all-gather.1 = f32[544,128]{1,0:T(8,128)S(1)} all-gather(f32[272,128]{1,0:T(8,128)S(1)} %get-tuple-element.32), channel_id=3, replica_groups={{4,8},{5,9},{6,10},{7,11},{12,16},{13,17},{14,18},{15,19},{20,24},{21,2..., dimensions={0}, use_global_device_ids=true | all-gather | bytes 417792 | tf_op jit(solution)/shard_map/all_gather | solution.py:590
  66.9 7.9 %all-gather.2 = f32[1376,128]{1,0:T(8,128)S(1)} all-gather(f32[688,128]{1,0:T(8,128)S(1)} %pad_maximum_fusion), channel_id=4, replica_groups={{0,4},{1,5},{2,6},{3,7},{8,12},{9,13},{10,14},{11,15},{16,20},{17,21},{..., dimensions={0}, use_global_device_ids=true | all-gather | bytes 1056768 | tf_op jit(solution)/shard_map/all_gather | solution.py:590
  74.8 0.0 copy-start.1
  74.8 0.0 copy-start.2
  74.8 5.2 %shard_map.71 = (f32[14,80,128]{2,1,0:T(8,128)S(1)}, f32[6,64,128]{2,1,0:T(8,128)S(1)}, f32[8,18,64,128]{3,2,1,0:T(8,128)S(1)}, f32[2,64,128]{2,1,0:T(8,128)S(1)}) custom-call(f32[8,24,64,128]{3,2,1,0:T(8,128)S(1)} %get-tuple-element.28.weights_ref, f32[24,80,128]{2,1,0:T(8,128)S(1)} %get-tuple-element.29.pressure_ref, ...), custom_call_target="tpu_custom_call" | custom-call | flops 1000000 | bytes 1000000 | tf_op jit(solution)/shard_map/pallas_call | solution.py:577
  80.0 4.4 %all-gather.3 = f32[4,64,128]{2,1,0:T(8,128)S(1)} all-gather(f32[2,64,128]{2,1,0:T(8,128)S(1)} %get-tuple-element.37), channel_id=5, replica_groups={{4,8},{5,9},{6,10},{7,11},{12,16},{13,17},{14,18},{15,19},{20,24},{21,2..., dimensions={0}, use_global_device_ids=true | all-gather | bytes 196608 | tf_op jit(solution)/shard_map/all_gather | solution.py:590
  84.4 7.3 %all-gather.4 = f32[4,1,64,128]{3,2,1,0:T(8,128)S(1)} all-gather(f32[2,1,64,128]{3,2,1,0:T(8,128)S(1)} %slice.4), channel_id=6, replica_groups={{0,4},{1,5},{2,6},{3,7},{8,12},{9,13},{10,14},{11,15},{16,20},{17,21},{..., dimensions={0}, use_global_device_ids=true | all-gather | bytes 196608 | tf_op jit(solution)/shard_map/all_gather | solution.py:590
  91.7 0.0 collective-permute-done.3.y_low
  91.7 0.0 collective-permute-done.4.y_high
  91.7 0.0 copy-done.1
  91.7 0.0 copy-done.2
  91.7 2.8 %shard_map.73 = (f32[3,4,16,128]{3,2,1,0:T(8,128)}, f32[4,16,128]{2,1,0:T(8,128)}, f32[9,4,16,128]{3,2,1,0:T(8,128)}) custom-call(f32[26,80,128]{2,1,0:T(8,128)S(1)} %get-tuple-element.27.mobile_ref, f32[8,24,64,128]{3,2,1,0:T(8,128)S(1)} %get-tuple-element.28.weights_ref, f32[14,80,128]{2,1,0:T(8,128)S(1)} %get-tuple-element.34.pressure, ...), custom_call_target="tpu_custom_call" | custom-call | flops 1000000 | bytes 1000000 | tf_op jit(solution)/shard_map/pallas_call | solution.py:577
  (6 shorter events, 0.1 us)
Async XLA Ops:
  27.0 11.1 %collective-permute-start = (f32[17,64,128]{2,1,0:T(8,128)S(1)}, f32[17,64,128]{2,1,0:T(8,128)S(1)}, u32[]{:S(2)}, u32[]{:S(2)}) collective-permute-start(f32[17,64,128]{2,1,0:T(8,128)S(1)} %get-tuple-element.23.own), channel_id=1, source_target_pairs={{4,8},{8,4},{12,16},{16,12},{20,24},{24,20},{28,32},{32,28},{36,40... | collective-permute-start | bytes 1671176 | tf_op jit(solution)/shard_map/ppermute | solution.py:634
  30.3 9.6 %collective-permute-start.1 = (f32[2,64,128]{2,1,0:T(8,128)S(1)}, f32[2,64,128]{2,1,0:T(8,128)S(1)}, u32[]{:S(2)}, u32[]{:S(2)}) collective-permute-start(f32[2,64,128]{2,1,0:T(8,128)S(1)} %get-tuple-element.25), channel_id=1, source_target_pairs={{4,16},{16,4},{12,24},{24,12},{20,32},{32,20},{28,40},{40,28},{36,... | collective-permute-start | bytes 196616 | tf_op jit(solution)/shard_map/ppermute | solution.py:635
  39.9 18.4 %collective-permute-start.2 = (f32[19,64,128]{2,1,0:T(8,128)S(1)}, f32[19,64,128]{2,1,0:T(8,128)S(1)}, u32[]{:S(2)}, u32[]{:S(2)}) collective-permute-start(f32[19,64,128]{2,1,0:T(8,128)S(1)} %constant_dynamic-update-slice_fusion.mine), channel_id=1, source_target_pairs={{0,4},{4,0},{8,12},{12,8},{16,20},{20,16},{24,28},{28,24},{32,36},... | collective-permute-start | bytes 1867784 | tf_op jit(solution)/shard_map/ppermute | solution.py:643
  48.9 1.0 %copy-start = (f32[9,4,16,128]{3,2,1,0:T(8,128)S(1)}, f32[9,4,16,128]{3,2,1,0:T(8,128)}, u32[]{:S(2)}) copy-start(f32[9,4,16,128]{3,2,1,0:T(8,128)} %species.3) | copy-start | bytes 884740
  49.9 41.8 %collective-permute-start.3 = (f32[40,128]{1,0:T(8,128)S(1)}, f32[40,128]{1,0:T(8,128)S(1)}, u32[]{:S(2)}, u32[]{:S(2)}) collective-permute-start(f32[40,128]{1,0:T(8,128)S(1)} %get-tuple-element.41), channel_id=1, source_target_pairs={{0,1},{1,2},{2,3},{4,5},{5,6},{6,7},{8,9},{9,10},{10,11},{12,13},{... | collective-permute-start | bytes 61448 | tf_op jit(solution)/shard_map/ppermute | solution.py:639
  51.9 39.8 %collective-permute-start.4 = (f32[40,128]{1,0:T(8,128)S(1)}, f32[40,128]{1,0:T(8,128)S(1)}, u32[]{:S(2)}, u32[]{:S(2)}) collective-permute-start(f32[40,128]{1,0:T(8,128)S(1)} %get-tuple-element.42), channel_id=1, source_target_pairs={{1,0},{2,1},{3,2},{5,4},{6,5},{7,6},{9,8},{10,9},{11,10},{13,12},{... | collective-permute-start | bytes 61448 | tf_op jit(solution)/shard_map/ppermute | solution.py:640
  74.8 16.9 %copy-start.1 = (f32[9,4,16,128]{3,2,1,0:T(8,128)S(1)}, f32[9,4,16,128]{3,2,1,0:T(8,128)}, u32[]{:S(2)}) copy-start(f32[9,4,16,128]{3,2,1,0:T(8,128)} %species.3) | copy-start | bytes 884740
  74.8 16.9 %copy-start.2 = (f32[3,4,16,128]{3,2,1,0:T(8,128)S(1)}, f32[3,4,16,128]{3,2,1,0:T(8,128)}, u32[]{:S(2)}) copy-start(f32[3,4,16,128]{3,2,1,0:T(8,128)} %velocity.1) | copy-start | bytes 294916

commit v7 on v6

--- a/solution.py
+++ b/solution.py
@@ -64,7 +64,7 @@
 
 
 PAD = 8
-PADDED = (ROWS + 2 * PAD, LANES)
+HALF = ROWS // 2
 
 
 class Field:
@@ -72,20 +72,27 @@
         self.ref = ref
         self.low = low
         self.shift = shift
+        self.rows = ref.shape[1] - 2 * PAD
 
     def __call__(self, i, rows=0):
         k = (i - self.low).index(self.shift)
-        return self.ref[k, PAD + rows : PAD + rows + ROWS]
+        return self.ref[k, PAD + rows : PAD + rows + self.rows]
 
     def put(self, i, value):
-        self.ref[(i - self.low).index(), PAD : PAD + ROWS] = value
+        self.ref[(i - self.low).index(), PAD : PAD + self.rows] = value
+
+    def every_other(self, i, first):
+        return self.ref[(i - self.low).index(), pl.ds(PAD + first, HALF, stride=2)]
+
+    def put_every_other(self, i, first, value):
+        self.ref[(i - self.low).index(), pl.ds(PAD + first, HALF, stride=2)] = value
 
 
 def clear_pads(ref):
     nothing = jnp.zeros((PAD, LANES), jnp.float32)
     for k in range(ref.shape[0]):
         ref[k, 0:PAD] = nothing
-        ref[k, PAD + ROWS :] = nothing
+        ref[k, ref.shape[1] - PAD :] = nothing
 
 
 class Weights:
@@ -101,13 +108,13 @@
 
     def fill(self, low, high, mobile, target, inside):
         s = self.step
-        lane = lanes_of(PLANE)
+        lane = lanes_of((mobile.rows, LANES))
         z_low, z_high = lane >= s, lane < LANES - s
 
         def body(i):
             m = mobile(i)
             x_m, x_p = mobile(i - 1), mobile(i + 1)
-            y_m, y_p = mobile(i, -s), mobile(i, s)
+            y_m, y_p = mobile(i, -1), mobile(i, 1)
             z_m = jnp.where(z_low, roll_lanes(m, s), 0.0)
             z_p = jnp.where(z_high, roll_lanes(m, -s), 0.0)
             diagonal = 3.0 * m + 0.5 * ((x_m + x_p) + (y_m + y_p) + (z_m + z_p))
@@ -140,7 +147,7 @@
         k = self.place(i)
         p = field(i)
         total = self.ref[0, k] * field(i - 1) + self.ref[1, k] * field(i + 1)
-        total = total + (self.ref[2, k] * field(i, -s) + self.ref[3, k] * field(i, s))
+        total = total + (self.ref[2, k] * field(i, -1) + self.ref[3, k] * field(i, 1))
         total = total + (self.ref[4, k] * roll_lanes(p, s) + self.ref[5, k] * roll_lanes(p, -s))
         return p, (total - self.side(i)) - damping * p
 
@@ -164,40 +171,48 @@
     loop(low, high, body)
 
 
-def pair_sum(q):
-    row, lane = rows_of(PLANE), lanes_of(PLANE)
-    q = q + jnp.where(lane % 2 == 0, roll_lanes(q, -1), roll_lanes(q, 1))
-    return q + jnp.where(row % 2 == 0, roll_rows(q, -1), roll_rows(q, 1))
-
-
-def packed(a, b, c, d):
-    row, lane = rows_of(PLANE), lanes_of(PLANE)
-    even = lane % 2 == 0
-    return jnp.where(row % 2 == 0, jnp.where(even, a, b), jnp.where(even, c, d))
+def restricted(first, second):
+    q = first + second
+    even = lanes_of(q.shape) % 2 == 0
+    return 0.125 * (q + jnp.where(even, roll_lanes(q, -1), roll_lanes(q, 1)))
+
+
+def packed(planes):
+    even = lanes_of((HALF, LANES)) % 2 == 0
+    a, b, c, d = planes
+    return jnp.where(even, a, b), jnp.where(even, c, d)
 
 
 def unpacked(v):
-    row, lane = rows_of(PLANE), lanes_of(PLANE)
-    even, upper = lane % 2 == 0, row % 2 == 0
-    first = jnp.where(even, v, roll_lanes(v, 1))
-    second = jnp.where(even, roll_lanes(v, -1), v)
-
-    def low_row(x):
-        return jnp.where(upper, x, roll_rows(x, 1))
-
-    def high_row(x):
-        return jnp.where(upper, roll_rows(x, -1), x)
-
-    return low_row(first), low_row(second), high_row(first), high_row(second)
-
-
-def residual_planes(weights, field, result, result_low, low, high):
+    even = lanes_of((HALF, LANES)) % 2 == 0
+    planes = []
+    for half in (v[:HALF], v[HALF:]):
+        planes.append(jnp.where(even, half, roll_lanes(half, 1)))
+        planes.append(jnp.where(even, roll_lanes(half, -1), half))
+    return planes
+
+
+def residual_planes(weights, field, result, result_low, low, high, scratch):
     def body(i):
         total = 0.0
         for half in range(2):
             _, change = weights.change(field, 2 * i + half)
             total = total - change * weights.ref[7, weights.place(2 * i + half)]
-        result[(i - result_low).index()] = 0.125 * pair_sum(total)
+        k = (i - low).index()
+        scratch[k] = total
+        odd = scratch[k, pl.ds(1, HALF, stride=2)]
+        result[(i - result_low).index()] = restricted(scratch[k, pl.ds(0, HALF, stride=2)], odd)
+
+    loop(low, high, body)
+
+
+def prolong(correction, known, result, low, high):
+    def body(i):
+        added = correction(i)
+        for half in range(2):
+            for first in range(2):
+                k = 2 * i + half
+                result.put_every_other(k, first, known(k, first) + added)
 
     loop(low, high, body)
 
@@ -305,7 +320,7 @@
 def first_cycle(
     n_chips, own, edge, mine, swapped, species_near,
     mobile_ref, weights_ref, pressure_ref, residual, coarse, outer, sent,
-    target_w, field_ref,
+    target_w, field_ref, rows_ref,
 ):
     north, _, chip = whereabouts(n_chips)
     clear_pads(mobile_ref)
@@ -347,17 +362,20 @@
     weights.fill(-8, 16, mobile_w, at(target_w, -8), inside_of(8 * chip, 8 * n_chips))
     first_sweep(weights, field, -8, 16)
     sweep(weights, field, pressure, -7, 15)
-    residual_planes(weights, pressure, residual, -3, -3, 7)
+    residual_planes(weights, pressure, residual, -3, -3, 7, rows_ref)
 
     def restrict(i):
-        pair = mobile_w(2 * i) + mobile_w(2 * i + 1)
-        coarse[(i + 4).index()] = 0.125 * pair_sum(pair)
+        rows = [
+            mobile_w.every_other(2 * i, first) + mobile_w.every_other(2 * i + 1, first)
+            for first in range(2)
+        ]
+        coarse[(i + 4).index()] = restricted(*rows)
 
     loop(-4, 8, restrict)
     r = jnp.where(north, 6, 0)
-    sent[0:64] = packed(residual[r], residual[r + 1], residual[r + 2], residual[r + 3])
+    sent[0:32], sent[32:64] = packed([residual[r + k] for k in range(4)])
     m = jnp.where(north, 8, 0)
-    sent[64:128] = packed(coarse[m], coarse[m + 1], coarse[m + 2], coarse[m + 3])
+    sent[64:96], sent[96:128] = packed([coarse[m + k] for k in range(4)])
     sent[128:272] = species_near[...]
 
 
@@ -375,7 +393,7 @@
 def second_cycle(
     n_chips, weights_ref, pressure_ref, residual, coarse, got,
     pressure_new_ref, residual_new, coarse_weights_ref, sent,
-    coarse_ref, residual_w, one_ref, two_ref, field_ref, other_ref,
+    coarse_ref, residual_w, one_ref, two_ref, field_ref, other_ref, rows_ref,
 ):
     north, _, chip = whereabouts(n_chips)
     before, after = inner(n_chips, chip)
@@ -409,25 +427,17 @@
     coarse_weights.fill(-7, 11, coarse_w, at(residual_w, -7), inside_of(4 * chip, 4 * n_chips))
     coarse_sweeps(coarse_weights, one, two, -7, 11)
 
-    def prolong(i):
-        correction = two(i)
-        for half in range(2):
-            k = 2 * i + half
-            field.put(k, pressure(k) + correction)
-
-    loop(-4, 8, prolong)
+    prolong(two, pressure.every_other, field, -4, 8)
 
     weights = Weights(weights_ref, 1, -8)
     sweep(weights, field, other, -6, 14)
     sweep(weights, other, field, -5, 13)
     sweep(weights, field, other, -4, 12)
     sweep(weights, other, pressure_new, -3, 11)
-    residual_planes(weights, pressure_new, residual_new, -1, -1, 5)
+    residual_planes(weights, pressure_new, residual_new, -1, -1, 5, rows_ref)
     sent[0] = pressure_new_ref[jnp.where(north, 6, 7), PAD : PAD + ROWS]
     r = jnp.where(north, 2, 0)
-    sent[1] = packed(
-        residual_new[r], residual_new[r + 1], residual_new[r + 2], residual_new[r + 3]
-    )
+    sent[1, 0:32], sent[1, 32:64] = packed([residual_new[r + k] for k in range(4)])
 
 
 def finish(
@@ -470,13 +480,10 @@
         right_side(Place(0, k - 5))
     coarse_sweeps(coarse_weights, one, two, -5, 7)
 
-    def prolong(i):
-        correction = two(i)
-        for half in range(2):
-            k = 2 * i + half
-            field.put(k, pressure_w[(k + 4).index(shift)] + correction)
-
-    loop(-2, 4, prolong)
+    def known_rows(i, first):
+        return pressure_w[(i + 4).index(shift), pl.ds(first, HALF, stride=2)]
+
+    prolong(two, known_rows, field, -2, 4)
 
     weights = Weights(weights_ref, 1, -8, shift)
     sweep(weights, field, other, -3, 7)
@@ -618,8 +625,11 @@
     def plane(n):
         return (n, ROWS, LANES)
 
-    def padded(n):
-        return (n, *PADDED)
+    def padded(n, rows=ROWS):
+        return (n, rows + 2 * PAD, LANES)
+
+    def halved(n):
+        return (n, HALF, LANES)
 
     def bind(kernel):
         return functools.partial(kernel, n_chips)
@@ -644,17 +654,20 @@
     mobile_w, weights, pressure, residual, coarse, outer, sent_two = call(
         bind(first_cycle),
         [
-            padded(26), (8, *plane(24)), padded(24), plane(10), plane(12), PLANE, (272, LANES),
+            padded(26), (8, *plane(24)), padded(24), halved(10), halved(12), PLANE, (272, LANES),
         ],
-        [plane(24), padded(24)],
+        [plane(24), padded(24), plane(10)],
         sent, edge, mine, swapped, species_near,
     )
     near = gathered_over(sent_two, facing).reshape(544, LANES)
     sides = gathered_over(jnp.concatenate([near, species_beside], 0), cores)
     pressure, residual, coarse_weights, sent = call(
         bind(second_cycle),
-        [padded(14), plane(6), (8, *plane(18)), plane(2)],
-        [padded(20), plane(18), padded(18), padded(18), padded(24), padded(24)],
+        [padded(14), halved(6), (8, *halved(18)), plane(2)],
+        [
+            padded(20, HALF), halved(18), padded(18, HALF), padded(18, HALF), padded(24), padded(24),
+            plane(6),
+        ],
         weights, pressure, residual, coarse, sides,
     )
     near = gathered_over(sent, facing)
@@ -662,7 +675,10 @@
     return call(
         bind(finish),
         [velocity.shape, density.shape, species.shape],
-        [plane(14), plane(16), padded(12), padded(12), padded(12), padded(12), padded(8)],
+        [
+            halved(14), plane(16), padded(12, HALF), padded(12, HALF), padded(12), padded(12),
+            padded(8),
+        ],
         mobile_w, weights, pressure, residual, coarse_weights, near, swapped,
         velocity, species, outer, u_beside, v_rims, sides, y_low, y_high,
     )

time: 94.8 us -> 92.1 us (0.972)
  Pallas kernels: 13.2 us -> 11.4 us
  local copies, waits for them, and re-layouts: 1.01 us -> 0.06 us
    pallas_call x7, Pallas kernels: 13.2 us -> 11.4 us  [call(): pl.pallas_call(kernel, out_shape=shapes, in_specs=[pl.BlockSpec(memory_sp...]
    unnamed x7 -> x5, local copies, waits for them, and re-layouts: 1 us -> 0.04 us
  transfers between devices with their start and end apart: 5 -> 5, of which waited for: 2 -> 2; matrix products, arithmetic and copies ran while one was open for 0% -> 0% of each run, Pallas kernels for 9% -> 8%
where the time goes in v7:
time: 92.1 us; the launch traced here: 91.8 us
  blocking collectives  49.4 us (54%)
  starting transfers between devices  23.9 us (26%)
  Pallas kernels  11.4 us (12%)
  waiting for transfers between devices  6.24 us (7%)
    all_gather x5, blocking collectives, gathered_over(): return lax.all_gather(array, ('slab', 'cross'), axis_index_groups=groups)  49.4 us
    pallas_call x7, Pallas kernels, call(): pl.pallas_call(kernel, out_shape=shapes, in_specs=[pl.BlockSpec(memory_sp...  11.4 us
    ppermute x1, starting transfers between devices, local(): swapped = lax.ppermute(mine, 'slab', within)  9.01 us
    ppermute x1, starting transfers between devices, local(): y_high = lax.ppermute(edge_low, 'cross', downward)  6.37 us
    ppermute x1, waiting for transfers between devices, local(): near = lax.ppermute(sent, 'slab', beside(1))  4.51 us
    ppermute x1, starting transfers between devices, local(): far = lax.ppermute(sent_far, 'slab', beside(2))  3.32 us
    ppermute x1, starting transfers between devices, local(): near = lax.ppermute(sent, 'slab', beside(1))  3.3 us
    ppermute x1, starting transfers between devices, local(): y_low = lax.ppermute(edge_high, 'cross', upward)  1.92 us
  transfers between devices with their start and end apart: 5, of which 2 were waited for; matrix products, arithmetic and copies ran while one was open for 0% of the time, Pallas kernels for 8%

profile of v7, /device:TPU:257, one launch (start us, length us, event | category | flops | bytes accessed | tf_op | source)
XLA Modules:
  0.0 91.8 jit_solution(2356930731327017463)
XLA Ops:
  0.6 0.0 copy-start
  0.6 1.7 %shard_map.67 = f32[168,128]{1,0:T(8,128)} custom-call(f32[3,4,16,128]{3,2,1,0:T(8,128)} %velocity.1, f32[4,16,128]{2,1,0:T(8,128)} %density_in.1, f32[4,16,128]{2,1,0:T(8,128)} %source_in.1), custom_call_target="tpu_custom_call" | custom-call | flops 1000000 | bytes 1000000 | tf_op jit(solution)/shard_map/pallas_call | solution.py:584
  2.4 24.6 %all-gather = f32[1344,128]{1,0:T(8,128)S(1)} all-gather(f32[168,128]{1,0:T(8,128)} %shard_map.67), channel_id=2, replica_groups={{0,4,1,5,2,6,3,7},{8,12,9,13,10,14,11,15},{16,20,17,21,18,22,19,23},{24..., dimensions={0}, use_global_device_ids=true | all-gather | bytes 774144 | tf_op jit(solution)/shard_map/all_gather | solution.py:597
  27.0 0.1 shard_map.68
  27.0 3.3 %collective-permute-start = (f32[17,64,128]{2,1,0:T(8,128)S(1)}, f32[17,64,128]{2,1,0:T(8,128)S(1)}, u32[]{:S(2)}, u32[]{:S(2)}) collective-permute-start(f32[17,64,128]{2,1,0:T(8,128)S(1)} %get-tuple-element.23.own), channel_id=1, source_target_pairs={{4,8},{8,4},{12,16},{16,12},{20,24},{24,20},{28,32},{32,28},{36,40... | collective-permute-start | bytes 1671176 | tf_op jit(solution)/shard_map/ppermute | solution.py:644
  30.4 3.3 %collective-permute-start.1 = (f32[2,64,128]{2,1,0:T(8,128)S(1)}, f32[2,64,128]{2,1,0:T(8,128)S(1)}, u32[]{:S(2)}, u32[]{:S(2)}) collective-permute-start(f32[2,64,128]{2,1,0:T(8,128)S(1)} %get-tuple-element.25), channel_id=1, source_target_pairs={{4,16},{16,4},{12,24},{24,12},{20,32},{32,20},{28,40},{40,28},{36,... | collective-permute-start | bytes 196616 | tf_op jit(solution)/shard_map/ppermute | solution.py:645
  33.7 4.5 %collective-permute-done = f32[17,64,128]{2,1,0:T(8,128)S(1)} collective-permute-done((f32[17,64,128]{2,1,0:T(8,128)S(1)}, f32[17,64,128]{2,1,0:T(8,128)S(1)}, u32[]{:S(2)}, u32[]{:S(2)}) %collective-permute-start) | collective-permute-done | bytes 557088 | tf_op jit(solution)/shard_map/ppermute | solution.py:644
  38.2 1.7 %collective-permute-done.1 = f32[2,64,128]{2,1,0:T(8,128)S(1)} collective-permute-done((f32[2,64,128]{2,1,0:T(8,128)S(1)}, f32[2,64,128]{2,1,0:T(8,128)S(1)}, u32[]{:S(2)}, u32[]{:S(2)}) %collective-permute-start.1) | collective-permute-done | bytes 65568 | tf_op jit(solution)/shard_map/ppermute | solution.py:645
  40.0 9.0 %collective-permute-start.2 = (f32[19,64,128]{2,1,0:T(8,128)S(1)}, f32[19,64,128]{2,1,0:T(8,128)S(1)}, u32[]{:S(2)}, u32[]{:S(2)}) collective-permute-start(f32[19,64,128]{2,1,0:T(8,128)S(1)} %constant_dynamic-update-slice_fusion.mine), channel_id=1, source_target_pairs={{0,4},{4,0},{8,12},{12,8},{16,20},{20,16},{24,28},{28,24},{32,36},... | collective-permute-start | bytes 1867784 | tf_op jit(solution)/shard_map/ppermute | solution.py:653
  49.0 0.0 copy-done
  49.0 1.9 %collective-permute-start.3 = (f32[40,128]{1,0:T(8,128)S(1)}, f32[40,128]{1,0:T(8,128)S(1)}, u32[]{:S(2)}, u32[]{:S(2)}) collective-permute-start(f32[40,128]{1,0:T(8,128)S(1)} %get-tuple-element.41), channel_id=1, source_target_pairs={{0,1},{1,2},{2,3},{4,5},{5,6},{6,7},{8,9},{9,10},{10,11},{12,13},{... | collective-permute-start | bytes 61448 | tf_op jit(solution)/shard_map/ppermute | solution.py:649
  51.0 6.4 %collective-permute-start.4 = (f32[40,128]{1,0:T(8,128)S(1)}, f32[40,128]{1,0:T(8,128)S(1)}, u32[]{:S(2)}, u32[]{:S(2)}) collective-permute-start(f32[40,128]{1,0:T(8,128)S(1)} %get-tuple-element.42), channel_id=1, source_target_pairs={{1,0},{2,1},{3,2},{5,4},{6,5},{7,6},{9,8},{10,9},{11,10},{13,12},{... | collective-permute-start | bytes 61448 | tf_op jit(solution)/shard_map/ppermute | solution.py:650
  57.4 0.0 collective-permute-done.2.swapped
  57.4 3.3 %shard_map.70 = (f32[26,80,128]{2,1,0:T(8,128)S(1)}, f32[8,24,64,128]{3,2,1,0:T(8,128)S(1)}, f32[24,80,128]{2,1,0:T(8,128)S(1)}, f32[10,32,128]{2,1,0:T(8,128)S(...) custom-call(f32[17,64,128]{2,1,0:T(8,128)S(1)} %get-tuple-element.23.own, ...), custom_call_target="tpu_custom_call" | custom-call | flops 1000000 | bytes 1000000 | tf_op jit(solution)/shard_map/pallas_call | solution.py:584
  60.7 5.2 %all-gather.1 = f32[544,128]{1,0:T(8,128)S(1)} all-gather(f32[272,128]{1,0:T(8,128)S(1)} %get-tuple-element.32), channel_id=3, replica_groups={{4,8},{5,9},{6,10},{7,11},{12,16},{13,17},{14,18},{15,19},{20,24},{21,2..., dimensions={0}, use_global_device_ids=true | all-gather | bytes 417792 | tf_op jit(solution)/shard_map/all_gather | solution.py:597
  65.9 7.9 %all-gather.2 = f32[1376,128]{1,0:T(8,128)S(1)} all-gather(f32[688,128]{1,0:T(8,128)S(1)} %pad_maximum_fusion), channel_id=4, replica_groups={{0,4},{1,5},{2,6},{3,7},{8,12},{9,13},{10,14},{11,15},{16,20},{17,21},{..., dimensions={0}, use_global_device_ids=true | all-gather | bytes 1056768 | tf_op jit(solution)/shard_map/all_gather | solution.py:597
  73.8 0.0 copy-start.1
  73.8 3.9 %shard_map.71 = (f32[14,80,128]{2,1,0:T(8,128)S(1)}, f32[6,32,128]{2,1,0:T(8,128)S(1)}, f32[8,18,32,128]{3,2,1,0:T(8,128)S(1)}, f32[2,64,128]{2,1,0:T(8,128)S(1)}) custom-call(f32[8,24,64,128]{3,2,1,0:T(8,128)S(1)} %get-tuple-element.28.weights_ref, f32[24,80,128]{2,1,0:T(8,128)S(1)} %get-tuple-element.29.pressure_ref, ...), custom_call_target="tpu_custom_call" | custom-call | flops 1000000 | bytes 1000000 | tf_op jit(solution)/shard_map/pallas_call | solution.py:584
  77.7 4.4 %all-gather.3 = f32[4,64,128]{2,1,0:T(8,128)S(1)} all-gather(f32[2,64,128]{2,1,0:T(8,128)S(1)} %get-tuple-element.37), channel_id=5, replica_groups={{4,8},{5,9},{6,10},{7,11},{12,16},{13,17},{14,18},{15,19},{20,24},{21,2..., dimensions={0}, use_global_device_ids=true | all-gather | bytes 196608 | tf_op jit(solution)/shard_map/all_gather | solution.py:597
  82.1 7.3 %all-gather.4 = f32[4,1,64,128]{3,2,1,0:T(8,128)S(1)} all-gather(f32[2,1,64,128]{3,2,1,0:T(8,128)S(1)} %slice.4), channel_id=6, replica_groups={{0,4},{1,5},{2,6},{3,7},{8,12},{9,13},{10,14},{11,15},{16,20},{17,21},{..., dimensions={0}, use_global_device_ids=true | all-gather | bytes 196608 | tf_op jit(solution)/shard_map/all_gather | solution.py:597
  89.4 0.0 collective-permute-done.3.y_low
  89.4 0.0 collective-permute-done.4.y_high
  89.4 0.0 copy-done.1
  89.4 2.3 %shard_map.73 = (f32[3,4,16,128]{3,2,1,0:T(8,128)}, f32[4,16,128]{2,1,0:T(8,128)}, f32[9,4,16,128]{3,2,1,0:T(8,128)}) custom-call(f32[26,80,128]{2,1,0:T(8,128)S(1)} %get-tuple-element.27.mobile_ref, f32[8,24,64,128]{3,2,1,0:T(8,128)S(1)} %get-tuple-element.28.weights_ref, f32[14,80,128]{2,1,0:T(8,128)S(1)} %get-tuple-element.34.pressure, ...), custom_call_target="tpu_custom_call" | custom-call | flops 1000000 | bytes 1000000 | tf_op jit(solution)/shard_map/pallas_call | solution.py:584
  (6 shorter events, 0.1 us)
Async XLA Ops:
  0.6 48.4 %copy-start = (f32[9,4,16,128]{3,2,1,0:T(8,128)S(1)}, f32[9,4,16,128]{3,2,1,0:T(8,128)}, u32[]{:S(2)}) copy-start(f32[9,4,16,128]{3,2,1,0:T(8,128)} %species.3) | copy-start | bytes 884740
  27.0 11.1 %collective-permute-start = (f32[17,64,128]{2,1,0:T(8,128)S(1)}, f32[17,64,128]{2,1,0:T(8,128)S(1)}, u32[]{:S(2)}, u32[]{:S(2)}) collective-permute-start(f32[17,64,128]{2,1,0:T(8,128)S(1)} %get-tuple-element.23.own), channel_id=1, source_target_pairs={{4,8},{8,4},{12,16},{16,12},{20,24},{24,20},{28,32},{32,28},{36,40... | collective-permute-start | bytes 1671176 | tf_op jit(solution)/shard_map/ppermute | solution.py:644
  30.4 9.6 %collective-permute-start.1 = (f32[2,64,128]{2,1,0:T(8,128)S(1)}, f32[2,64,128]{2,1,0:T(8,128)S(1)}, u32[]{:S(2)}, u32[]{:S(2)}) collective-permute-start(f32[2,64,128]{2,1,0:T(8,128)S(1)} %get-tuple-element.25), channel_id=1, source_target_pairs={{4,16},{16,4},{12,24},{24,12},{20,32},{32,20},{28,40},{40,28},{36,... | collective-permute-start | bytes 196616 | tf_op jit(solution)/shard_map/ppermute | solution.py:645
  40.0 17.4 %collective-permute-start.2 = (f32[19,64,128]{2,1,0:T(8,128)S(1)}, f32[19,64,128]{2,1,0:T(8,128)S(1)}, u32[]{:S(2)}, u32[]{:S(2)}) collective-permute-start(f32[19,64,128]{2,1,0:T(8,128)S(1)} %constant_dynamic-update-slice_fusion.mine), channel_id=1, source_target_pairs={{0,4},{4,0},{8,12},{12,8},{16,20},{20,16},{24,28},{28,24},{32,36},... | collective-permute-start | bytes 1867784 | tf_op jit(solution)/shard_map/ppermute | solution.py:653
  49.0 40.4 %collective-permute-start.3 = (f32[40,128]{1,0:T(8,128)S(1)}, f32[40,128]{1,0:T(8,128)S(1)}, u32[]{:S(2)}, u32[]{:S(2)}) collective-permute-start(f32[40,128]{1,0:T(8,128)S(1)} %get-tuple-element.41), channel_id=1, source_target_pairs={{0,1},{1,2},{2,3},{4,5},{5,6},{6,7},{8,9},{9,10},{10,11},{12,13},{... | collective-permute-start | bytes 61448 | tf_op jit(solution)/shard_map/ppermute | solution.py:649
  51.0 38.5 %collective-permute-start.4 = (f32[40,128]{1,0:T(8,128)S(1)}, f32[40,128]{1,0:T(8,128)S(1)}, u32[]{:S(2)}, u32[]{:S(2)}) collective-permute-start(f32[40,128]{1,0:T(8,128)S(1)} %get-tuple-element.42), channel_id=1, source_target_pairs={{1,0},{2,1},{3,2},{5,4},{6,5},{7,6},{9,8},{10,9},{11,10},{13,12},{... | collective-permute-start | bytes 61448 | tf_op jit(solution)/shard_map/ppermute | solution.py:650
  73.8 15.7 %copy-start.1 = (f32[3,4,16,128]{3,2,1,0:T(8,128)S(1)}, f32[3,4,16,128]{3,2,1,0:T(8,128)}, u32[]{:S(2)}) copy-start(f32[3,4,16,128]{3,2,1,0:T(8,128)} %velocity.1) | copy-start | bytes 294916

commit v8 on v7

--- a/solution.py
+++ b/solution.py
@@ -15,7 +15,7 @@
 BLOCK = 16
 SPECIES = 9
 EDGE = 160
-OWN = EDGE + 8
+OWN = EDGE + 80
 damping = 0.8
 time_step = 0.25
 
@@ -231,11 +231,17 @@
     return slab % 2 == 0, jnp.minimum(jnp.maximum(cross, 0), 3), chip
 
 
-def prepare(velocity_in, density_in, source_in, out, velocity, density, source, semaphore):
+def prepare(
+    velocity_in, density_in, source_in, species_in, out,
+    velocity, density, source, species, semaphore,
+):
     copies = [
         pltpu.make_async_copy(there, here, semaphore.at[k])
         for k, (there, here) in enumerate(
-            [(density_in, density), (velocity_in, velocity), (source_in, source)]
+            [
+                (density_in, density), (velocity_in, velocity), (source_in, source),
+                (species_in, species),
+            ]
         )
     ]
     for copy in copies:
@@ -262,6 +268,12 @@
         out[r + 4 : r + 5] = velocity[1, x, BLOCK - 1 : BLOCK]
     out[128:144] = velocity[0, 0]
     out[144:160] = velocity[0, 3]
+    copies[3].wait()
+    for s in range(SPECIES):
+        for x in range(4):
+            r = EDGE + 8 + 4 * s + x
+            out[r : r + 1] = species[s, x, 0:1]
+            out[r + 36 : r + 37] = species[s, x, BLOCK - 1 : BLOCK]
 
 
 def assemble(n_chips, gathered, sent, sent_far, edge):
@@ -292,21 +304,15 @@
     sent_far[1] = u
 
 
-def species_edges(n_chips, species, near, beside, edge_low, edge_high):
+def species_edges(n_chips, species, near, beside):
     north, _, _ = whereabouts(n_chips)
     outward, inward = jnp.where(north, 0, 3), jnp.where(north, 3, 0)
     for s in range(SPECIES):
         near[BLOCK * s : BLOCK * (s + 1)] = species[s, outward]
         beside[BLOCK * s : BLOCK * (s + 1)] = species[s, inward]
-        for x in range(4):
-            r = 4 * s + x
-            edge_low[r : r + 1] = species[s, x, 0:1]
-            edge_high[r : r + 1] = species[s, x, BLOCK - 1 : BLOCK]
-    edge_low[36:40] = jnp.zeros((4, LANES), jnp.float32)
-    edge_high[36:40] = jnp.zeros((4, LANES), jnp.float32)
-
-
-def flow_rims(n_chips, gathered, u_beside, v_rims):
+
+
+def flow_rims(n_chips, gathered, u_beside, v_rims, y_low, y_high):
     north, cross, _ = whereabouts(n_chips)
     core = jnp.where(north, 0, 1)
     partner = 2 * cross + jnp.where(north, 1, 0)
@@ -315,10 +321,12 @@
     above = gathered[2 * jnp.minimum(cross + 1, 3) + core, EDGE:OWN]
     v_rims[0:4] = jnp.where(cross > 0, below[4:8], 0.0)
     v_rims[4:8] = jnp.where(cross < 3, above[0:4], 0.0)
+    y_low[...] = jnp.where(cross > 0, below[44:80], 0.0)
+    y_high[...] = jnp.where(cross < 3, above[8:44], 0.0)
 
 
 def first_cycle(
-    n_chips, own, edge, mine, swapped, species_near,
+    n_chips, own, edge, mine, swapped,
     mobile_ref, weights_ref, pressure_ref, residual, coarse, outer, sent,
     target_w, field_ref, rows_ref,
 ):
@@ -376,7 +384,6 @@
     sent[0:32], sent[32:64] = packed([residual[r + k] for k in range(4)])
     m = jnp.where(north, 8, 0)
     sent[64:96], sent[96:128] = packed([coarse[m + k] for k in range(4)])
-    sent[128:272] = species_near[...]
 
 
 def coarse_sweeps(weights, one, two, low, high):
@@ -404,12 +411,12 @@
     pressure, pressure_new = Field(pressure_ref, -8), Field(pressure_new_ref, -3)
 
     left = unpacked(jnp.where(before, got[0, 0:64], 0.0))
-    right = unpacked(jnp.where(after, got[1, 272:336], 0.0))
+    right = unpacked(jnp.where(after, got[1, 128:192], 0.0))
     for i in range(4):
         residual_w[i] = left[i]
         residual_w[14 + i] = right[i]
     left = unpacked(jnp.where(before, got[0, 64:128], 0.0))
-    right = unpacked(jnp.where(after, got[1, 336:400], 0.0))
+    right = unpacked(jnp.where(after, got[1, 192:256], 0.0))
     for i in range(4):
         coarse_w.put(Place(0, i - 8), left[i])
         coarse_w.put(Place(0, i + 8), right[i])
@@ -442,7 +449,7 @@
 
 def finish(
     n_chips, mobile_ref, weights_ref, pressure, residual, coarse_weights_ref, got, swapped,
-    velocity, species, outer, u_beside, v_rims, sides, y_low, y_high,
+    velocity, species, outer, u_beside, v_rims, outer_rim, sides, y_low, y_high,
     velocity_out, pressure_out, species_out,
     residual_w, pressure_w, one_ref, two_ref, field_ref, other_ref, final_pad,
 ):
@@ -510,10 +517,8 @@
     u = [u_out(x) for x in range(-1, 5)]
 
     def species_beside(s, side):
-        at_rim = BLOCK * s + (128 if side == 0 else 400)
-        outside = sides[side, at_rim : at_rim + BLOCK]
-        outside = jnp.where(before if side == 0 else after, outside, 0.0)
-        inside = sides[side, 544 + BLOCK * s : 560 + BLOCK * s]
+        outside = outer_rim[BLOCK * s : BLOCK * (s + 1)]
+        inside = sides[side, 256 + BLOCK * s : 272 + BLOCK * s]
         return jnp.where(north, outside, inside) if side == 0 else jnp.where(north, inside, outside)
 
     wide = pl.ds(start, 32)
@@ -619,8 +624,6 @@
         return pairs
 
     within = [pair for j in range(n_chips) for pair in ((2 * j, 2 * j + 1), (2 * j + 1, 2 * j))]
-    upward = [(c, c + 1) for c in range(3)]
-    downward = [(c + 1, c) for c in range(3)]
 
     def plane(n):
         return (n, ROWS, LANES)
@@ -635,31 +638,32 @@
         return functools.partial(kernel, n_chips)
 
     (own,) = call(
-        prepare, [(OWN, LANES)], [velocity.shape, density.shape, source.shape],
-        velocity, density, source,
-        where=HBM, semaphores=3, grant=63,
+        prepare, [(OWN, LANES)], [velocity.shape, density.shape, source.shape, species.shape],
+        velocity, density, source, species,
+        where=HBM, semaphores=4, grant=63,
     )
     gathered = gathered_over(own, chips)
     sent, sent_far, edge = call(bind(assemble), [plane(17), plane(2), plane(2)], [], gathered)
     near = lax.ppermute(sent, "slab", beside(1))
     far = lax.ppermute(sent_far, "slab", beside(2))
-    species_near, species_beside, edge_low, edge_high = call(
-        bind(species_edges), [(144, LANES), (144, LANES), (40, LANES), (40, LANES)], [], species
+    species_near, species_beside = call(
+        bind(species_edges), [(144, LANES), (144, LANES)], [], species
     )
-    y_low = lax.ppermute(edge_high, "cross", upward)
-    y_high = lax.ppermute(edge_low, "cross", downward)
-    u_beside, v_rims = call(bind(flow_rims), [(BLOCK, LANES), (8, LANES)], [], gathered)
+    outer_rim = lax.ppermute(species_near, "slab", beside(1))
+    u_beside, v_rims, y_low, y_high = call(
+        bind(flow_rims), [(BLOCK, LANES), (8, LANES), (36, LANES), (36, LANES)], [], gathered
+    )
     mine = jnp.concatenate([near, far], 0)
     swapped = lax.ppermute(mine, "slab", within)
     mobile_w, weights, pressure, residual, coarse, outer, sent_two = call(
         bind(first_cycle),
         [
-            padded(26), (8, *plane(24)), padded(24), halved(10), halved(12), PLANE, (272, LANES),
+            padded(26), (8, *plane(24)), padded(24), halved(10), halved(12), PLANE, (128, LANES),
         ],
         [plane(24), padded(24), plane(10)],
-        sent, edge, mine, swapped, species_near,
+        sent, edge, mine, swapped,
     )
-    near = gathered_over(sent_two, facing).reshape(544, LANES)
+    near = gathered_over(sent_two, facing).reshape(256, LANES)
     sides = gathered_over(jnp.concatenate([near, species_beside], 0), cores)
     pressure, residual, coarse_weights, sent = call(
         bind(second_cycle),
@@ -680,7 +684,7 @@
             padded(8),
         ],
         mobile_w, weights, pressure, residual, coarse_weights, near, swapped,
-        velocity, species, outer, u_beside, v_rims, sides, y_low, y_high,
+        velocity, species, outer, u_beside, v_rims, outer_rim, sides, y_low, y_high,
     )
 
 

time: 92.1 us -> 90.5 us (0.983)
  starting transfers between devices: 23.9 us -> 18.8 us
  blocking collectives: 49.4 us -> 53 us
    ppermute x2 -> x1, starting transfers between devices: 8.29 us -> 1.92 us  [local(): outer_rim = lax.ppermute(species_near, 'slab', beside(1))]
    all_gather x5, blocking collectives: 49.4 us -> 53 us  [gathered_over(): return lax.all_gather(array, ('slab', 'cross'), axis_index_groups=groups)]
    ppermute x1, starting transfers between devices: 3.3 us -> 4.41 us  [local(): near = lax.ppermute(sent, 'slab', beside(1))]
  transfers between devices with their start and end apart: 5 -> 4, of which waited for: 2 -> 2; matrix products, arithmetic and copies ran while one was open for 0% -> 0% of each run, Pallas kernels for 8% -> 8%
where the time goes in v8:
time: 90.5 us; the launch traced here: 90.2 us
  blocking collectives  53 us (59%)
  starting transfers between devices  18.8 us (21%)
  Pallas kernels  11.4 us (13%)
  waiting for transfers between devices  6.23 us (7%)
    all_gather x5, blocking collectives, gathered_over(): return lax.all_gather(array, ('slab', 'cross'), axis_index_groups=groups)  53 us
    pallas_call x7, Pallas kernels, call(): pl.pallas_call(kernel, out_shape=shapes, in_specs=[pl.BlockSpec(memory_sp...  11.4 us
    ppermute x1, starting transfers between devices, local(): swapped = lax.ppermute(mine, 'slab', within)  9.11 us
    ppermute x1, starting transfers between devices, local(): near = lax.ppermute(sent, 'slab', beside(1))  4.41 us
    ppermute x1, waiting for transfers between devices, local(): near = lax.ppermute(sent, 'slab', beside(1))  4.17 us
    ppermute x1, starting transfers between devices, local(): far = lax.ppermute(sent_far, 'slab', beside(2))  3.32 us
    ppermute x1, waiting for transfers between devices, local(): far = lax.ppermute(sent_far, 'slab', beside(2))  2.06 us
    ppermute x1, starting transfers between devices, local(): outer_rim = lax.ppermute(species_near, 'slab', beside(1))  1.92 us
  transfers between devices with their start and end apart: 4, of which 2 were waited for; matrix products, arithmetic and copies ran while one was open for 0% of the time, Pallas kernels for 8%

profile of v8, /device:TPU:257, one launch (start us, length us, event | category | flops | bytes accessed | tf_op | source)
XLA Modules:
  0.0 90.2 jit_solution(16160651389912638455)
XLA Ops:
  0.6 0.0 copy-start
  0.6 1.8 %shard_map.67 = f32[240,128]{1,0:T(8,128)} custom-call(f32[3,4,16,128]{3,2,1,0:T(8,128)} %velocity.1, f32[4,16,128]{2,1,0:T(8,128)} %density_in.1, f32[4,16,128]{2,1,0:T(8,128)} %source_in.1, f32[9,4,16,128]{3,2,1,0:T(8,128)} %species.3), custom_call_target="tpu_custom_call" | custom-call | flops 1000000 | bytes 1000000 | tf_op jit(solution)/shard_map/pallas_call | solution.py:589
  2.4 26.6 %all-gather = f32[1920,128]{1,0:T(8,128)S(1)} all-gather(f32[240,128]{1,0:T(8,128)} %shard_map.67), channel_id=2, replica_groups={{0,4,1,5,2,6,3,7},{8,12,9,13,10,14,11,15},{16,20,17,21,18,22,19,23},{24..., dimensions={0}, use_global_device_ids=true | all-gather | bytes 1105920 | tf_op jit(solution)/shard_map/all_gather | solution.py:602
  29.0 0.1 shard_map.68
  29.1 4.4 %collective-permute-start = (f32[17,64,128]{2,1,0:T(8,128)S(1)}, f32[17,64,128]{2,1,0:T(8,128)S(1)}, u32[]{:S(2)}, u32[]{:S(2)}) collective-permute-start(f32[17,64,128]{2,1,0:T(8,128)S(1)} %get-tuple-element.23.own), channel_id=1, source_target_pairs={{4,8},{8,4},{12,16},{16,12},{20,24},{24,20},{28,32},{32,28},{36,40... | collective-permute-start | bytes 1671176 | tf_op jit(solution)/shard_map/ppermute | solution.py:647
  33.5 3.3 %collective-permute-start.1 = (f32[2,64,128]{2,1,0:T(8,128)S(1)}, f32[2,64,128]{2,1,0:T(8,128)S(1)}, u32[]{:S(2)}, u32[]{:S(2)}) collective-permute-start(f32[2,64,128]{2,1,0:T(8,128)S(1)} %get-tuple-element.25), channel_id=1, source_target_pairs={{4,16},{16,4},{12,24},{24,12},{20,32},{32,20},{28,40},{40,28},{36,... | collective-permute-start | bytes 196616 | tf_op jit(solution)/shard_map/ppermute | solution.py:648
  36.8 4.2 %collective-permute-done = f32[17,64,128]{2,1,0:T(8,128)S(1)} collective-permute-done((f32[17,64,128]{2,1,0:T(8,128)S(1)}, f32[17,64,128]{2,1,0:T(8,128)S(1)}, u32[]{:S(2)}, u32[]{:S(2)}) %collective-permute-start) | collective-permute-done | bytes 557088 | tf_op jit(solution)/shard_map/ppermute | solution.py:647
  41.0 2.1 %collective-permute-done.1 = f32[2,64,128]{2,1,0:T(8,128)S(1)} collective-permute-done((f32[2,64,128]{2,1,0:T(8,128)S(1)}, f32[2,64,128]{2,1,0:T(8,128)S(1)}, u32[]{:S(2)}, u32[]{:S(2)}) %collective-permute-start.1) | collective-permute-done | bytes 65568 | tf_op jit(solution)/shard_map/ppermute | solution.py:648
  43.1 9.1 %collective-permute-start.2 = (f32[19,64,128]{2,1,0:T(8,128)S(1)}, f32[19,64,128]{2,1,0:T(8,128)S(1)}, u32[]{:S(2)}, u32[]{:S(2)}) collective-permute-start(f32[19,64,128]{2,1,0:T(8,128)S(1)} %constant_dynamic-update-slice_fusion.mine), channel_id=1, source_target_pairs={{0,4},{4,0},{8,12},{12,8},{16,20},{20,16},{24,28},{28,24},{32,36},... | collective-permute-start | bytes 1867784 | tf_op jit(solution)/shard_map/ppermute | solution.py:657
  52.2 0.0 copy-done
  52.3 1.9 %collective-permute-start.3 = (f32[144,128]{1,0:T(8,128)S(1)}, f32[144,128]{1,0:T(8,128)S(1)}, u32[]{:S(2)}, u32[]{:S(2)}) collective-permute-start(f32[144,128]{1,0:T(8,128)S(1)} %get-tuple-element.40), channel_id=1, source_target_pairs={{4,8},{8,4},{12,16},{16,12},{20,24},{24,20},{28,32},{32,28},{36,40... | collective-permute-start | bytes 221192 | tf_op jit(solution)/shard_map/ppermute | solution.py:652
  54.2 0.0 collective-permute-done.2.swapped
  54.3 3.3 %shard_map.69 = (f32[26,80,128]{2,1,0:T(8,128)S(1)}, f32[8,24,64,128]{3,2,1,0:T(8,128)S(1)}, f32[24,80,128]{2,1,0:T(8,128)S(1)}, f32[10,32,128]{2,1,0:T(8,128)S(...) custom-call(f32[17,64,128]{2,1,0:T(8,128)S(1)} %get-tuple-element.23.own, ...), custom_call_target="tpu_custom_call" | custom-call | flops 1000000 | bytes 1000000 | tf_op jit(solution)/shard_map/pallas_call | solution.py:589
  57.5 4.7 %all-gather.1 = f32[256,128]{1,0:T(8,128)S(1)} all-gather(f32[128,128]{1,0:T(8,128)S(1)} %get-tuple-element.31), channel_id=3, replica_groups={{4,8},{5,9},{6,10},{7,11},{12,16},{13,17},{14,18},{15,19},{20,24},{21,2..., dimensions={0}, use_global_device_ids=true | all-gather | bytes 196608 | tf_op jit(solution)/shard_map/all_gather | solution.py:602
  62.2 10.1 %all-gather.2 = f32[800,128]{1,0:T(8,128)S(1)} all-gather(f32[400,128]{1,0:T(8,128)S(1)} %pad_maximum_fusion), channel_id=4, replica_groups={{0,4},{1,5},{2,6},{3,7},{8,12},{9,13},{10,14},{11,15},{16,20},{17,21},{..., dimensions={0}, use_global_device_ids=true | all-gather | bytes 614400 | tf_op jit(solution)/shard_map/all_gather | solution.py:602
  72.3 0.0 copy-start.1
  72.3 3.9 %shard_map.71 = (f32[14,80,128]{2,1,0:T(8,128)S(1)}, f32[6,32,128]{2,1,0:T(8,128)S(1)}, f32[8,18,32,128]{3,2,1,0:T(8,128)S(1)}, f32[2,64,128]{2,1,0:T(8,128)S(1)}) custom-call(f32[8,24,64,128]{3,2,1,0:T(8,128)S(1)} %get-tuple-element.27.weights_ref, f32[24,80,128]{2,1,0:T(8,128)S(1)} %get-tuple-element.28.pressure_ref, ...), custom_call_target="tpu_custom_call" | custom-call | flops 1000000 | bytes 1000000 | tf_op jit(solution)/shard_map/pallas_call | solution.py:589
  76.2 4.4 %all-gather.3 = f32[4,64,128]{2,1,0:T(8,128)S(1)} all-gather(f32[2,64,128]{2,1,0:T(8,128)S(1)} %get-tuple-element.36), channel_id=5, replica_groups={{4,8},{5,9},{6,10},{7,11},{12,16},{13,17},{14,18},{15,19},{20,24},{21,2..., dimensions={0}, use_global_device_ids=true | all-gather | bytes 196608 | tf_op jit(solution)/shard_map/all_gather | solution.py:602
  80.6 7.3 %all-gather.4 = f32[4,1,64,128]{3,2,1,0:T(8,128)S(1)} all-gather(f32[2,1,64,128]{3,2,1,0:T(8,128)S(1)} %slice.4), channel_id=6, replica_groups={{0,4},{1,5},{2,6},{3,7},{8,12},{9,13},{10,14},{11,15},{16,20},{17,21},{..., dimensions={0}, use_global_device_ids=true | all-gather | bytes 196608 | tf_op jit(solution)/shard_map/all_gather | solution.py:602
  87.9 0.0 collective-permute-done.3.outer_rim
  87.9 0.0 copy-done.1
  87.9 2.3 %shard_map.73 = (f32[3,4,16,128]{3,2,1,0:T(8,128)}, f32[4,16,128]{2,1,0:T(8,128)}, f32[9,4,16,128]{3,2,1,0:T(8,128)}) custom-call(f32[26,80,128]{2,1,0:T(8,128)S(1)} %get-tuple-element.26.mobile_ref, f32[8,24,64,128]{3,2,1,0:T(8,128)S(1)} %get-tuple-element.27.weights_ref, f32[14,80,128]{2,1,0:T(8,128)S(1)} %get-tuple-element.33.pressure, ...), custom_call_target="tpu_custom_call" | custom-call | flops 1000000 | bytes 1000000 | tf_op jit(solution)/shard_map/pallas_call | solution.py:589
  (6 shorter events, 0.1 us)
Async XLA Ops:
  0.6 51.6 %copy-start = (f32[9,4,16,128]{3,2,1,0:T(8,128)S(1)}, f32[9,4,16,128]{3,2,1,0:T(8,128)}, u32[]{:S(2)}) copy-start(f32[9,4,16,128]{3,2,1,0:T(8,128)} %species.3) | copy-start | bytes 884740
  29.1 11.9 %collective-permute-start = (f32[17,64,128]{2,1,0:T(8,128)S(1)}, f32[17,64,128]{2,1,0:T(8,128)S(1)}, u32[]{:S(2)}, u32[]{:S(2)}) collective-permute-start(f32[17,64,128]{2,1,0:T(8,128)S(1)} %get-tuple-element.23.own), channel_id=1, source_target_pairs={{4,8},{8,4},{12,16},{16,12},{20,24},{24,20},{28,32},{32,28},{36,40... | collective-permute-start | bytes 1671176 | tf_op jit(solution)/shard_map/ppermute | solution.py:647
  33.5 9.6 %collective-permute-start.1 = (f32[2,64,128]{2,1,0:T(8,128)S(1)}, f32[2,64,128]{2,1,0:T(8,128)S(1)}, u32[]{:S(2)}, u32[]{:S(2)}) collective-permute-start(f32[2,64,128]{2,1,0:T(8,128)S(1)} %get-tuple-element.25), channel_id=1, source_target_pairs={{4,16},{16,4},{12,24},{24,12},{20,32},{32,20},{28,40},{40,28},{36,... | collective-permute-start | bytes 196616 | tf_op jit(solution)/shard_map/ppermute | solution.py:648
  43.1 11.1 %collective-permute-start.2 = (f32[19,64,128]{2,1,0:T(8,128)S(1)}, f32[19,64,128]{2,1,0:T(8,128)S(1)}, u32[]{:S(2)}, u32[]{:S(2)}) collective-permute-start(f32[19,64,128]{2,1,0:T(8,128)S(1)} %constant_dynamic-update-slice_fusion.mine), channel_id=1, source_target_pairs={{0,4},{4,0},{8,12},{12,8},{16,20},{20,16},{24,28},{28,24},{32,36},... | collective-permute-start | bytes 1867784 | tf_op jit(solution)/shard_map/ppermute | solution.py:657
  52.3 35.6 %collective-permute-start.3 = (f32[144,128]{1,0:T(8,128)S(1)}, f32[144,128]{1,0:T(8,128)S(1)}, u32[]{:S(2)}, u32[]{:S(2)}) collective-permute-start(f32[144,128]{1,0:T(8,128)S(1)} %get-tuple-element.40), channel_id=1, source_target_pairs={{4,8},{8,4},{12,16},{16,12},{20,24},{24,20},{28,32},{32,28},{36,40... | collective-permute-start | bytes 221192 | tf_op jit(solution)/shard_map/ppermute | solution.py:652
  72.3 15.6 %copy-start.1 = (f32[3,4,16,128]{3,2,1,0:T(8,128)S(1)}, f32[3,4,16,128]{3,2,1,0:T(8,128)}, u32[]{:S(2)}) copy-start(f32[3,4,16,128]{3,2,1,0:T(8,128)} %velocity.1) | copy-start | bytes 294916

commit v9 on v8

--- a/solution.py
+++ b/solution.py
@@ -298,10 +298,9 @@
                 sent[8 + 4 * k + x, rows] = t
         edge[0, rows] = gathered[2 * c, 128:144]
         edge[1, rows] = gathered[2 * c + 1, 144:160]
-    u = edge[jnp.where(north, 0, 1)]
-    sent[16] = u
-    sent_far[0] = sent[jnp.where(north, 0, 7)]
-    sent_far[1] = u
+    sent[16] = edge[jnp.where(north, 0, 1)]
+    sent_far[0] = sent[jnp.where(north, 7, 0)]
+    sent_far[1] = edge[jnp.where(north, 1, 0)]
 
 
 def species_edges(n_chips, species, near, beside):
@@ -353,10 +352,10 @@
         target_w[(i + 16).index()] = right
 
     loop(0, 8, copy)
-    left, right = sides(17)
+    right, left = sides(17)
     mobile_w.put(Place(0, -9), left)
     mobile_w.put(Place(0, 16), right)
-    left, right = sides(18)
+    right, left = sides(18)
     target_w[0] = target_w[0] - 0.5 * left
     target_w[23] = target_w[23] + 0.5 * right
     left, right = sides(16)
@@ -616,12 +615,11 @@
     for slab in (0, 2 * n_chips - 1):
         facing += [[device(slab, 0), device(slab, 1)], [device(slab, 2), device(slab, 3)]]
 
-    def beside(distance):
-        pairs = []
-        for j in range(n_chips - distance):
-            left, right = 2 * j + 1, 2 * (j + distance)
-            pairs += [(left, right), (right, left)]
-        return pairs
+    def both_ways(pairs):
+        return [pair for left, right in pairs for pair in ((left, right), (right, left))]
+
+    beside = both_ways([(2 * j + 1, 2 * j + 2) for j in range(n_chips - 1)])
+    two_away = both_ways([(2 * j, 2 * j + 5) for j in range(n_chips - 2)])
 
     within = [pair for j in range(n_chips) for pair in ((2 * j, 2 * j + 1), (2 * j + 1, 2 * j))]
 
@@ -644,12 +642,12 @@
     )
     gathered = gathered_over(own, chips)
     sent, sent_far, edge = call(bind(assemble), [plane(17), plane(2), plane(2)], [], gathered)
-    near = lax.ppermute(sent, "slab", beside(1))
-    far = lax.ppermute(sent_far, "slab", beside(2))
+    near = lax.ppermute(sent, "slab", beside)
+    far = lax.ppermute(sent_far, "slab", two_away)
     species_near, species_beside = call(
         bind(species_edges), [(144, LANES), (144, LANES)], [], species
     )
-    outer_rim = lax.ppermute(species_near, "slab", beside(1))
+    outer_rim = lax.ppermute(species_near, "slab", beside)
     u_beside, v_rims, y_low, y_high = call(
         bind(flow_rims), [(BLOCK, LANES), (8, LANES), (36, LANES), (36, LANES)], [], gathered
     )

time: 90.5 us -> 91.2 us (level)
  blocking collectives: 53 us -> 56.1 us
  waiting for transfers between devices: 6.23 us -> 4.06 us
    ppermute x1, starting transfers between devices: 9.11 us -> 2.58 us  [local(): swapped = lax.ppermute(mine, 'slab', within)]
    ppermute x3, starting transfers between devices: 9.65 us -> 15.9 us  [the longest x1 8.55 us: local(): far = lax.ppermute(sent_far, 'slab', two_away)]
    all_gather x5, blocking collectives: 53 us -> 56.1 us  [gathered_over(): return lax.all_gather(array, ('slab', 'cross'), axis_index_groups=groups)]
    ppermute x3, waiting for transfers between devices: 6.23 us -> 4.06 us  [the longest x1 4.05 us: local(): far = lax.ppermute(sent_far, 'slab', two_away)]
  transfers between devices with their start and end apart: 4 -> 4, of which waited for: 2 -> 1; matrix products, arithmetic and copies ran while one was open for 0% -> 0% of each run, Pallas kernels for 8% -> 8%
where the time goes in v9:
time: 91.2 us; the launch traced here: 90.9 us
  blocking collectives  56.1 us (62%)
  starting transfers between devices  18.5 us (20%)
  Pallas kernels  11.4 us (12%)
  waiting for transfers between devices  4.06 us (4%)
    all_gather x5, blocking collectives, gathered_over(): return lax.all_gather(array, ('slab', 'cross'), axis_index_groups=groups)  56.1 us
    pallas_call x7, Pallas kernels, call(): pl.pallas_call(kernel, out_shape=shapes, in_specs=[pl.BlockSpec(memory_sp...  11.4 us
    ppermute x1, starting transfers between devices, local(): far = lax.ppermute(sent_far, 'slab', two_away)  8.55 us
    ppermute x1, starting transfers between devices, local(): near = lax.ppermute(sent, 'slab', beside)  4.41 us
    ppermute x1, waiting for transfers between devices, local(): far = lax.ppermute(sent_far, 'slab', two_away)  4.05 us
    ppermute x1, starting transfers between devices, local(): outer_rim = lax.ppermute(species_near, 'slab', beside)  2.95 us
    ppermute x1, starting transfers between devices, local(): swapped = lax.ppermute(mine, 'slab', within)  2.58 us
  transfers between devices with their start and end apart: 4, of which 1 were waited for; matrix products, arithmetic and copies ran while one was open for 0% of the time, Pallas kernels for 8%

profile of v9, /device:TPU:257, one launch (start us, length us, event | category | flops | bytes accessed | tf_op | source)
XLA Modules:
  0.0 90.9 jit_solution(13045273328375758891)
XLA Ops:
  0.6 0.0 copy-start
  0.6 1.8 %shard_map.67 = f32[240,128]{1,0:T(8,128)} custom-call(f32[3,4,16,128]{3,2,1,0:T(8,128)} %velocity.1, f32[4,16,128]{2,1,0:T(8,128)} %density_in.1, f32[4,16,128]{2,1,0:T(8,128)} %source_in.1, f32[9,4,16,128]{3,2,1,0:T(8,128)} %species.3), custom_call_target="tpu_custom_call" | custom-call | flops 1000000 | bytes 1000000 | tf_op jit(solution)/shard_map/pallas_call | solution.py:588
  2.4 26.6 %all-gather = f32[1920,128]{1,0:T(8,128)S(1)} all-gather(f32[240,128]{1,0:T(8,128)} %shard_map.67), channel_id=2, replica_groups={{0,4,1,5,2,6,3,7},{8,12,9,13,10,14,11,15},{16,20,17,21,18,22,19,23},{24..., dimensions={0}, use_global_device_ids=true | all-gather | bytes 1105920 | tf_op jit(solution)/shard_map/all_gather | solution.py:601
  29.0 0.1 shard_map.68
  29.1 4.4 %collective-permute-start = (f32[17,64,128]{2,1,0:T(8,128)S(1)}, f32[17,64,128]{2,1,0:T(8,128)S(1)}, u32[]{:S(2)}, u32[]{:S(2)}) collective-permute-start(f32[17,64,128]{2,1,0:T(8,128)S(1)} %get-tuple-element.23.own), channel_id=1, source_target_pairs={{4,8},{8,4},{12,16},{16,12},{20,24},{24,20},{28,32},{32,28},{36,40... | collective-permute-start | bytes 1671176 | tf_op jit(solution)/shard_map/ppermute | solution.py:645
  33.5 8.5 %collective-permute-start.1 = (f32[2,64,128]{2,1,0:T(8,128)S(1)}, f32[2,64,128]{2,1,0:T(8,128)S(1)}, u32[]{:S(2)}, u32[]{:S(2)}) collective-permute-start(f32[2,64,128]{2,1,0:T(8,128)S(1)} %get-tuple-element.25), channel_id=1, source_target_pairs={{0,20},{20,0},{8,28},{28,8},{16,36},{36,16},{24,44},{44,24},{32,52... | collective-permute-start | bytes 196616 | tf_op jit(solution)/shard_map/ppermute | solution.py:646
  42.1 0.0 collective-permute-done
  42.1 4.1 %collective-permute-done.1 = f32[2,64,128]{2,1,0:T(8,128)S(1)} collective-permute-done((f32[2,64,128]{2,1,0:T(8,128)S(1)}, f32[2,64,128]{2,1,0:T(8,128)S(1)}, u32[]{:S(2)}, u32[]{:S(2)}) %collective-permute-start.1) | collective-permute-done | bytes 65568 | tf_op jit(solution)/shard_map/ppermute | solution.py:646
  46.2 2.6 %collective-permute-start.2 = (f32[19,64,128]{2,1,0:T(8,128)S(1)}, f32[19,64,128]{2,1,0:T(8,128)S(1)}, u32[]{:S(2)}, u32[]{:S(2)}) collective-permute-start(f32[19,64,128]{2,1,0:T(8,128)S(1)} %constant_dynamic-update-slice_fusion.mine), channel_id=1, source_target_pairs={{0,4},{4,0},{8,12},{12,8},{16,20},{20,16},{24,28},{28,24},{32,36},... | collective-permute-start | bytes 1867784 | tf_op jit(solution)/shard_map/ppermute | solution.py:655
  48.8 0.0 copy-done
  48.8 3.0 %collective-permute-start.3 = (f32[144,128]{1,0:T(8,128)S(1)}, f32[144,128]{1,0:T(8,128)S(1)}, u32[]{:S(2)}, u32[]{:S(2)}) collective-permute-start(f32[144,128]{1,0:T(8,128)S(1)} %get-tuple-element.40), channel_id=1, source_target_pairs={{4,8},{8,4},{12,16},{16,12},{20,24},{24,20},{28,32},{32,28},{36,40... | collective-permute-start | bytes 221192 | tf_op jit(solution)/shard_map/ppermute | solution.py:650
  51.8 0.0 collective-permute-done.2.swapped
  51.8 3.3 %shard_map.69 = (f32[26,80,128]{2,1,0:T(8,128)S(1)}, f32[8,24,64,128]{3,2,1,0:T(8,128)S(1)}, f32[24,80,128]{2,1,0:T(8,128)S(1)}, f32[10,32,128]{2,1,0:T(8,128)S(...) custom-call(f32[17,64,128]{2,1,0:T(8,128)S(1)} %get-tuple-element.23.own, ...), custom_call_target="tpu_custom_call" | custom-call | flops 1000000 | bytes 1000000 | tf_op jit(solution)/shard_map/pallas_call | solution.py:588
  55.1 4.7 %all-gather.1 = f32[256,128]{1,0:T(8,128)S(1)} all-gather(f32[128,128]{1,0:T(8,128)S(1)} %get-tuple-element.31), channel_id=3, replica_groups={{4,8},{5,9},{6,10},{7,11},{12,16},{13,17},{14,18},{15,19},{20,24},{21,2..., dimensions={0}, use_global_device_ids=true | all-gather | bytes 196608 | tf_op jit(solution)/shard_map/all_gather | solution.py:601
  59.8 13.2 %all-gather.2 = f32[800,128]{1,0:T(8,128)S(1)} all-gather(f32[400,128]{1,0:T(8,128)S(1)} %pad_maximum_fusion), channel_id=4, replica_groups={{0,4},{1,5},{2,6},{3,7},{8,12},{9,13},{10,14},{11,15},{16,20},{17,21},{..., dimensions={0}, use_global_device_ids=true | all-gather | bytes 614400 | tf_op jit(solution)/shard_map/all_gather | solution.py:601
  73.0 0.0 copy-start.1
  73.0 3.9 %shard_map.71 = (f32[14,80,128]{2,1,0:T(8,128)S(1)}, f32[6,32,128]{2,1,0:T(8,128)S(1)}, f32[8,18,32,128]{3,2,1,0:T(8,128)S(1)}, f32[2,64,128]{2,1,0:T(8,128)S(1)}) custom-call(f32[8,24,64,128]{3,2,1,0:T(8,128)S(1)} %get-tuple-element.27.weights_ref, f32[24,80,128]{2,1,0:T(8,128)S(1)} %get-tuple-element.28.pressure_ref, ...), custom_call_target="tpu_custom_call" | custom-call | flops 1000000 | bytes 1000000 | tf_op jit(solution)/shard_map/pallas_call | solution.py:588
  76.9 4.4 %all-gather.3 = f32[4,64,128]{2,1,0:T(8,128)S(1)} all-gather(f32[2,64,128]{2,1,0:T(8,128)S(1)} %get-tuple-element.36), channel_id=5, replica_groups={{4,8},{5,9},{6,10},{7,11},{12,16},{13,17},{14,18},{15,19},{20,24},{21,2..., dimensions={0}, use_global_device_ids=true | all-gather | bytes 196608 | tf_op jit(solution)/shard_map/all_gather | solution.py:601
  81.3 7.3 %all-gather.4 = f32[4,1,64,128]{3,2,1,0:T(8,128)S(1)} all-gather(f32[2,1,64,128]{3,2,1,0:T(8,128)S(1)} %slice.4), channel_id=6, replica_groups={{0,4},{1,5},{2,6},{3,7},{8,12},{9,13},{10,14},{11,15},{16,20},{17,21},{..., dimensions={0}, use_global_device_ids=true | all-gather | bytes 196608 | tf_op jit(solution)/shard_map/all_gather | solution.py:601
  88.6 0.0 collective-permute-done.3.outer_rim
  88.6 0.0 copy-done.1
  88.6 2.3 %shard_map.73 = (f32[3,4,16,128]{3,2,1,0:T(8,128)}, f32[4,16,128]{2,1,0:T(8,128)}, f32[9,4,16,128]{3,2,1,0:T(8,128)}) custom-call(f32[26,80,128]{2,1,0:T(8,128)S(1)} %get-tuple-element.26.mobile_ref, f32[8,24,64,128]{3,2,1,0:T(8,128)S(1)} %get-tuple-element.27.weights_ref, f32[14,80,128]{2,1,0:T(8,128)S(1)} %get-tuple-element.33.pressure, ...), custom_call_target="tpu_custom_call" | custom-call | flops 1000000 | bytes 1000000 | tf_op jit(solution)/shard_map/pallas_call | solution.py:588
  (6 shorter events, 0.1 us)
Async XLA Ops:
  0.6 48.1 %copy-start = (f32[9,4,16,128]{3,2,1,0:T(8,128)S(1)}, f32[9,4,16,128]{3,2,1,0:T(8,128)}, u32[]{:S(2)}) copy-start(f32[9,4,16,128]{3,2,1,0:T(8,128)} %species.3) | copy-start | bytes 884740
  29.1 13.0 %collective-permute-start = (f32[17,64,128]{2,1,0:T(8,128)S(1)}, f32[17,64,128]{2,1,0:T(8,128)S(1)}, u32[]{:S(2)}, u32[]{:S(2)}) collective-permute-start(f32[17,64,128]{2,1,0:T(8,128)S(1)} %get-tuple-element.23.own), channel_id=1, source_target_pairs={{4,8},{8,4},{12,16},{16,12},{20,24},{24,20},{28,32},{32,28},{36,40... | collective-permute-start | bytes 1671176 | tf_op jit(solution)/shard_map/ppermute | solution.py:645
  33.5 12.7 %collective-permute-start.1 = (f32[2,64,128]{2,1,0:T(8,128)S(1)}, f32[2,64,128]{2,1,0:T(8,128)S(1)}, u32[]{:S(2)}, u32[]{:S(2)}) collective-permute-start(f32[2,64,128]{2,1,0:T(8,128)S(1)} %get-tuple-element.25), channel_id=1, source_target_pairs={{0,20},{20,0},{8,28},{28,8},{16,36},{36,16},{24,44},{44,24},{32,52... | collective-permute-start | bytes 196616 | tf_op jit(solution)/shard_map/ppermute | solution.py:646
  46.2 5.6 %collective-permute-start.2 = (f32[19,64,128]{2,1,0:T(8,128)S(1)}, f32[19,64,128]{2,1,0:T(8,128)S(1)}, u32[]{:S(2)}, u32[]{:S(2)}) collective-permute-start(f32[19,64,128]{2,1,0:T(8,128)S(1)} %constant_dynamic-update-slice_fusion.mine), channel_id=1, source_target_pairs={{0,4},{4,0},{8,12},{12,8},{16,20},{20,16},{24,28},{28,24},{32,36},... | collective-permute-start | bytes 1867784 | tf_op jit(solution)/shard_map/ppermute | solution.py:655
  48.8 39.8 %collective-permute-start.3 = (f32[144,128]{1,0:T(8,128)S(1)}, f32[144,128]{1,0:T(8,128)S(1)}, u32[]{:S(2)}, u32[]{:S(2)}) collective-permute-start(f32[144,128]{1,0:T(8,128)S(1)} %get-tuple-element.40), channel_id=1, source_target_pairs={{4,8},{8,4},{12,16},{16,12},{20,24},{24,20},{28,32},{32,28},{36,40... | collective-permute-start | bytes 221192 | tf_op jit(solution)/shard_map/ppermute | solution.py:650
  73.0 15.6 %copy-start.1 = (f32[3,4,16,128]{3,2,1,0:T(8,128)S(1)}, f32[3,4,16,128]{3,2,1,0:T(8,128)}, u32[]{:S(2)}) copy-start(f32[3,4,16,128]{3,2,1,0:T(8,128)} %velocity.1) | copy-start | bytes 294916

commit v10 on v9

--- a/solution.py
+++ b/solution.py
@@ -15,7 +15,7 @@
 BLOCK = 16
 SPECIES = 9
 EDGE = 160
-OWN = EDGE + 80
+OWN = EDGE + 8
 damping = 0.8
 time_step = 0.25
 
@@ -232,15 +232,13 @@
 
 
 def prepare(
-    velocity_in, density_in, source_in, species_in, out,
-    velocity, density, source, species, semaphore,
+    velocity_in, density_in, source_in, out, velocity, density, source, semaphore
 ):
     copies = [
         pltpu.make_async_copy(there, here, semaphore.at[k])
         for k, (there, here) in enumerate(
             [
                 (density_in, density), (velocity_in, velocity), (source_in, source),
-                (species_in, species),
             ]
         )
     ]
@@ -268,12 +266,6 @@
         out[r + 4 : r + 5] = velocity[1, x, BLOCK - 1 : BLOCK]
     out[128:144] = velocity[0, 0]
     out[144:160] = velocity[0, 3]
-    copies[3].wait()
-    for s in range(SPECIES):
-        for x in range(4):
-            r = EDGE + 8 + 4 * s + x
-            out[r : r + 1] = species[s, x, 0:1]
-            out[r + 36 : r + 37] = species[s, x, BLOCK - 1 : BLOCK]
 
 
 def assemble(n_chips, gathered, sent, sent_far, edge):
@@ -303,15 +295,19 @@
     sent_far[1] = edge[jnp.where(north, 1, 0)]
 
 
-def species_edges(n_chips, species, near, beside):
+def species_edges(n_chips, species, near, beside, edge_low, edge_high):
     north, _, _ = whereabouts(n_chips)
     outward, inward = jnp.where(north, 0, 3), jnp.where(north, 3, 0)
     for s in range(SPECIES):
         near[BLOCK * s : BLOCK * (s + 1)] = species[s, outward]
         beside[BLOCK * s : BLOCK * (s + 1)] = species[s, inward]
-
-
-def flow_rims(n_chips, gathered, u_beside, v_rims, y_low, y_high):
+        for x in range(4):
+            r = 4 * s + x
+            edge_low[r : r + 1] = species[s, x, 0:1]
+            edge_high[r : r + 1] = species[s, x, BLOCK - 1 : BLOCK]
+
+
+def flow_rims(n_chips, gathered, u_beside, v_rims):
     north, cross, _ = whereabouts(n_chips)
     core = jnp.where(north, 0, 1)
     partner = 2 * cross + jnp.where(north, 1, 0)
@@ -320,8 +316,6 @@
     above = gathered[2 * jnp.minimum(cross + 1, 3) + core, EDGE:OWN]
     v_rims[0:4] = jnp.where(cross > 0, below[4:8], 0.0)
     v_rims[4:8] = jnp.where(cross < 3, above[0:4], 0.0)
-    y_low[...] = jnp.where(cross > 0, below[44:80], 0.0)
-    y_high[...] = jnp.where(cross < 3, above[8:44], 0.0)
 
 
 def first_cycle(
@@ -636,21 +630,21 @@
         return functools.partial(kernel, n_chips)
 
     (own,) = call(
-        prepare, [(OWN, LANES)], [velocity.shape, density.shape, source.shape, species.shape],
-        velocity, density, source, species,
-        where=HBM, semaphores=4, grant=63,
+        prepare, [(OWN, LANES)], [velocity.shape, density.shape, source.shape],
+        velocity, density, source,
+        where=HBM, semaphores=3, grant=63,
     )
     gathered = gathered_over(own, chips)
     sent, sent_far, edge = call(bind(assemble), [plane(17), plane(2), plane(2)], [], gathered)
     near = lax.ppermute(sent, "slab", beside)
     far = lax.ppermute(sent_far, "slab", two_away)
-    species_near, species_beside = call(
-        bind(species_edges), [(144, LANES), (144, LANES)], [], species
+    species_near, species_beside, edge_low, edge_high = call(
+        bind(species_edges), [(144, LANES), (144, LANES), (36, LANES), (36, LANES)], [], species
     )
+    y_low = lax.ppermute(edge_high, "cross", [(c, c + 1) for c in range(3)])
+    y_high = lax.ppermute(edge_low, "cross", [(c + 1, c) for c in range(3)])
     outer_rim = lax.ppermute(species_near, "slab", beside)
-    u_beside, v_rims, y_low, y_high = call(
-        bind(flow_rims), [(BLOCK, LANES), (8, LANES), (36, LANES), (36, LANES)], [], gathered
-    )
+    u_beside, v_rims = call(bind(flow_rims), [(BLOCK, LANES), (8, LANES)], [], gathered)
     mine = jnp.concatenate([near, far], 0)
     swapped = lax.ppermute(mine, "slab", within)
     mobile_w, weights, pressure, residual, coarse, outer, sent_two = call(

time: 91.2 us -> 95.2 us (1.044)
  starting transfers between devices: 18.5 us -> 26.7 us
  blocking collectives: 56.1 us -> 51.7 us
    ppermute x0 -> x2, starting transfers between devices: none -> 8.29 us  [the longest x1 6.37 us: local(): y_high = lax.ppermute(edge_low, 'cross', [(c + 1, c) for c in range(3)])]
    all_gather x5, blocking collectives: 56.1 us -> 51.7 us  [gathered_over(): return lax.all_gather(array, ('slab', 'cross'), axis_index_groups=groups)]
    ppermute x1, starting transfers between devices: 2.58 us -> 3.76 us  [local(): swapped = lax.ppermute(mine, 'slab', within)]
    ppermute x1, starting transfers between devices: 4.41 us -> 3.3 us  [local(): near = lax.ppermute(sent, 'slab', beside)]
  transfers between devices with their start and end apart: 4 -> 6, of which waited for: 1 -> 1; matrix products, arithmetic and copies ran while one was open for 0% -> 0% of each run, Pallas kernels for 8% -> 8%
where the time goes in v10:
time: 95.2 us; the launch traced here: 94.9 us
  blocking collectives  51.7 us (54%)
  starting transfers between devices  26.7 us (28%)
  Pallas kernels  11.4 us (12%)
  waiting for transfers between devices  4.26 us (4%)
    all_gather x5, blocking collectives, gathered_over(): return lax.all_gather(array, ('slab', 'cross'), axis_index_groups=groups)  51.7 us
    pallas_call x7, Pallas kernels, call(): pl.pallas_call(kernel, out_shape=shapes, in_specs=[pl.BlockSpec(memory_sp...  11.4 us
    ppermute x1, starting transfers between devices, local(): far = lax.ppermute(sent_far, 'slab', two_away)  8.45 us
    ppermute x1, starting transfers between devices, local(): y_high = lax.ppermute(edge_low, 'cross', [(c + 1, c) for c in range(3)])  6.37 us
    ppermute x1, waiting for transfers between devices, local(): far = lax.ppermute(sent_far, 'slab', two_away)  4.24 us
    ppermute x1, starting transfers between devices, local(): swapped = lax.ppermute(mine, 'slab', within)  3.76 us
    ppermute x1, starting transfers between devices, local(): near = lax.ppermute(sent, 'slab', beside)  3.3 us
    ppermute x1, starting transfers between devices, local(): outer_rim = lax.ppermute(species_near, 'slab', beside)  2.86 us
  transfers between devices with their start and end apart: 6, of which 1 were waited for; matrix products, arithmetic and copies ran while one was open for 0% of the time, Pallas kernels for 8%

profile of v10, /device:TPU:257, one launch (start us, length us, event | category | flops | bytes accessed | tf_op | source)
XLA Modules:
  0.0 94.9 jit_solution(1671401650371184200)
XLA Ops:
  0.6 0.0 copy-start
  0.6 1.7 %shard_map.67 = f32[168,128]{1,0:T(8,128)} custom-call(f32[3,4,16,128]{3,2,1,0:T(8,128)} %velocity.1, f32[4,16,128]{2,1,0:T(8,128)} %density_in.1, f32[4,16,128]{2,1,0:T(8,128)} %source_in.1), custom_call_target="tpu_custom_call" | custom-call | flops 1000000 | bytes 1000000 | tf_op jit(solution)/shard_map/pallas_call | solution.py:582
  2.4 24.6 %all-gather = f32[1344,128]{1,0:T(8,128)S(1)} all-gather(f32[168,128]{1,0:T(8,128)} %shard_map.67), channel_id=2, replica_groups={{0,4,1,5,2,6,3,7},{8,12,9,13,10,14,11,15},{16,20,17,21,18,22,19,23},{24..., dimensions={0}, use_global_device_ids=true | all-gather | bytes 774144 | tf_op jit(solution)/shard_map/all_gather | solution.py:595
  27.0 0.1 shard_map.68
  27.0 3.3 %collective-permute-start = (f32[17,64,128]{2,1,0:T(8,128)S(1)}, f32[17,64,128]{2,1,0:T(8,128)S(1)}, u32[]{:S(2)}, u32[]{:S(2)}) collective-permute-start(f32[17,64,128]{2,1,0:T(8,128)S(1)} %get-tuple-element.23.own), channel_id=1, source_target_pairs={{4,8},{8,4},{12,16},{16,12},{20,24},{24,20},{28,32},{32,28},{36,40... | collective-permute-start | bytes 1671176 | tf_op jit(solution)/shard_map/ppermute | solution.py:639
  30.4 8.4 %collective-permute-start.1 = (f32[2,64,128]{2,1,0:T(8,128)S(1)}, f32[2,64,128]{2,1,0:T(8,128)S(1)}, u32[]{:S(2)}, u32[]{:S(2)}) collective-permute-start(f32[2,64,128]{2,1,0:T(8,128)S(1)} %get-tuple-element.25), channel_id=1, source_target_pairs={{0,20},{20,0},{8,28},{28,8},{16,36},{36,16},{24,44},{44,24},{32,52... | collective-permute-start | bytes 196616 | tf_op jit(solution)/shard_map/ppermute | solution.py:640
  38.8 0.0 collective-permute-done
  38.9 4.2 %collective-permute-done.1 = f32[2,64,128]{2,1,0:T(8,128)S(1)} collective-permute-done((f32[2,64,128]{2,1,0:T(8,128)S(1)}, f32[2,64,128]{2,1,0:T(8,128)S(1)}, u32[]{:S(2)}, u32[]{:S(2)}) %collective-permute-start.1) | collective-permute-done | bytes 65568 | tf_op jit(solution)/shard_map/ppermute | solution.py:640
  43.1 3.8 %collective-permute-start.2 = (f32[19,64,128]{2,1,0:T(8,128)S(1)}, f32[19,64,128]{2,1,0:T(8,128)S(1)}, u32[]{:S(2)}, u32[]{:S(2)}) collective-permute-start(f32[19,64,128]{2,1,0:T(8,128)S(1)} %constant_dynamic-update-slice_fusion.mine), channel_id=1, source_target_pairs={{0,4},{4,0},{8,12},{12,8},{16,20},{20,16},{24,28},{28,24},{32,36},... | collective-permute-start | bytes 1867784 | tf_op jit(solution)/shard_map/ppermute | solution.py:649
  46.9 0.0 copy-done
  46.9 1.9 %collective-permute-start.4 = (f32[36,128]{1,0:T(8,128)S(1)}, f32[36,128]{1,0:T(8,128)S(1)}, u32[]{:S(2)}, u32[]{:S(2)}) collective-permute-start(f32[36,128]{1,0:T(8,128)S(1)} %get-tuple-element.41), channel_id=1, source_target_pairs={{0,1},{1,2},{2,3},{4,5},{5,6},{6,7},{8,9},{9,10},{10,11},{12,13},{... | collective-permute-start | bytes 55304 | tf_op jit(solution)/shard_map/ppermute | solution.py:644
  48.9 6.4 %collective-permute-start.5 = (f32[36,128]{1,0:T(8,128)S(1)}, f32[36,128]{1,0:T(8,128)S(1)}, u32[]{:S(2)}, u32[]{:S(2)}) collective-permute-start(f32[36,128]{1,0:T(8,128)S(1)} %get-tuple-element.42), channel_id=1, source_target_pairs={{1,0},{2,1},{3,2},{5,4},{6,5},{7,6},{9,8},{10,9},{11,10},{13,12},{... | collective-permute-start | bytes 55304 | tf_op jit(solution)/shard_map/ppermute | solution.py:645
  55.3 2.9 %collective-permute-start.3 = (f32[144,128]{1,0:T(8,128)S(1)}, f32[144,128]{1,0:T(8,128)S(1)}, u32[]{:S(2)}, u32[]{:S(2)}) collective-permute-start(f32[144,128]{1,0:T(8,128)S(1)} %get-tuple-element.40), channel_id=1, source_target_pairs={{4,8},{8,4},{12,16},{16,12},{20,24},{24,20},{28,32},{32,28},{36,40... | collective-permute-start | bytes 221192 | tf_op jit(solution)/shard_map/ppermute | solution.py:646
  58.2 0.0 collective-permute-done.2.swapped
  58.2 3.3 %shard_map.69 = (f32[26,80,128]{2,1,0:T(8,128)S(1)}, f32[8,24,64,128]{3,2,1,0:T(8,128)S(1)}, f32[24,80,128]{2,1,0:T(8,128)S(1)}, f32[10,32,128]{2,1,0:T(8,128)S(...) custom-call(f32[17,64,128]{2,1,0:T(8,128)S(1)} %get-tuple-element.23.own, ...), custom_call_target="tpu_custom_call" | custom-call | flops 1000000 | bytes 1000000 | tf_op jit(solution)/shard_map/pallas_call | solution.py:582
  61.4 4.7 %all-gather.1 = f32[256,128]{1,0:T(8,128)S(1)} all-gather(f32[128,128]{1,0:T(8,128)S(1)} %get-tuple-element.31), channel_id=3, replica_groups={{4,8},{5,9},{6,10},{7,11},{12,16},{13,17},{14,18},{15,19},{20,24},{21,2..., dimensions={0}, use_global_device_ids=true | all-gather | bytes 196608 | tf_op jit(solution)/shard_map/all_gather | solution.py:595
  66.1 10.7 %all-gather.2 = f32[800,128]{1,0:T(8,128)S(1)} all-gather(f32[400,128]{1,0:T(8,128)S(1)} %pad_maximum_fusion), channel_id=4, replica_groups={{0,4},{1,5},{2,6},{3,7},{8,12},{9,13},{10,14},{11,15},{16,20},{17,21},{..., dimensions={0}, use_global_device_ids=true | all-gather | bytes 614400 | tf_op jit(solution)/shard_map/all_gather | solution.py:595
  76.8 0.0 copy-start.1
  76.9 3.9 %shard_map.71 = (f32[14,80,128]{2,1,0:T(8,128)S(1)}, f32[6,32,128]{2,1,0:T(8,128)S(1)}, f32[8,18,32,128]{3,2,1,0:T(8,128)S(1)}, f32[2,64,128]{2,1,0:T(8,128)S(1)}) custom-call(f32[8,24,64,128]{3,2,1,0:T(8,128)S(1)} %get-tuple-element.27.weights_ref, f32[24,80,128]{2,1,0:T(8,128)S(1)} %get-tuple-element.28.pressure_ref, ...), custom_call_target="tpu_custom_call" | custom-call | flops 1000000 | bytes 1000000 | tf_op jit(solution)/shard_map/pallas_call | solution.py:582
  80.8 4.4 %all-gather.3 = f32[4,64,128]{2,1,0:T(8,128)S(1)} all-gather(f32[2,64,128]{2,1,0:T(8,128)S(1)} %get-tuple-element.36), channel_id=5, replica_groups={{4,8},{5,9},{6,10},{7,11},{12,16},{13,17},{14,18},{15,19},{20,24},{21,2..., dimensions={0}, use_global_device_ids=true | all-gather | bytes 196608 | tf_op jit(solution)/shard_map/all_gather | solution.py:595
  85.2 7.3 %all-gather.4 = f32[4,1,64,128]{3,2,1,0:T(8,128)S(1)} all-gather(f32[2,1,64,128]{3,2,1,0:T(8,128)S(1)} %slice.4), channel_id=6, replica_groups={{0,4},{1,5},{2,6},{3,7},{8,12},{9,13},{10,14},{11,15},{16,20},{17,21},{..., dimensions={0}, use_global_device_ids=true | all-gather | bytes 196608 | tf_op jit(solution)/shard_map/all_gather | solution.py:595
  92.5 0.0 collective-permute-done.4.y_low
  92.5 0.0 collective-permute-done.5.y_high
  92.5 0.0 collective-permute-done.3.outer_rim
  92.5 0.0 copy-done.1
  92.5 2.3 %shard_map.73 = (f32[3,4,16,128]{3,2,1,0:T(8,128)}, f32[4,16,128]{2,1,0:T(8,128)}, f32[9,4,16,128]{3,2,1,0:T(8,128)}) custom-call(f32[26,80,128]{2,1,0:T(8,128)S(1)} %get-tuple-element.26.mobile_ref, f32[8,24,64,128]{3,2,1,0:T(8,128)S(1)} %get-tuple-element.27.weights_ref, f32[14,80,128]{2,1,0:T(8,128)S(1)} %get-tuple-element.33.pressure, ...), custom_call_target="tpu_custom_call" | custom-call | flops 1000000 | bytes 1000000 | tf_op jit(solution)/shard_map/pallas_call | solution.py:582
  (6 shorter events, 0.1 us)
Async XLA Ops:
  0.6 46.3 %copy-start = (f32[9,4,16,128]{3,2,1,0:T(8,128)S(1)}, f32[9,4,16,128]{3,2,1,0:T(8,128)}, u32[]{:S(2)}) copy-start(f32[9,4,16,128]{3,2,1,0:T(8,128)} %species.3) | copy-start | bytes 884740
  27.0 11.8 %collective-permute-start = (f32[17,64,128]{2,1,0:T(8,128)S(1)}, f32[17,64,128]{2,1,0:T(8,128)S(1)}, u32[]{:S(2)}, u32[]{:S(2)}) collective-permute-start(f32[17,64,128]{2,1,0:T(8,128)S(1)} %get-tuple-element.23.own), channel_id=1, source_target_pairs={{4,8},{8,4},{12,16},{16,12},{20,24},{24,20},{28,32},{32,28},{36,40... | collective-permute-start | bytes 1671176 | tf_op jit(solution)/shard_map/ppermute | solution.py:639
  30.4 12.8 %collective-permute-start.1 = (f32[2,64,128]{2,1,0:T(8,128)S(1)}, f32[2,64,128]{2,1,0:T(8,128)S(1)}, u32[]{:S(2)}, u32[]{:S(2)}) collective-permute-start(f32[2,64,128]{2,1,0:T(8,128)S(1)} %get-tuple-element.25), channel_id=1, source_target_pairs={{0,20},{20,0},{8,28},{28,8},{16,36},{36,16},{24,44},{44,24},{32,52... | collective-permute-start | bytes 196616 | tf_op jit(solution)/shard_map/ppermute | solution.py:640
  43.1 15.0 %collective-permute-start.2 = (f32[19,64,128]{2,1,0:T(8,128)S(1)}, f32[19,64,128]{2,1,0:T(8,128)S(1)}, u32[]{:S(2)}, u32[]{:S(2)}) collective-permute-start(f32[19,64,128]{2,1,0:T(8,128)S(1)} %constant_dynamic-update-slice_fusion.mine), channel_id=1, source_target_pairs={{0,4},{4,0},{8,12},{12,8},{16,20},{20,16},{24,28},{28,24},{32,36},... | collective-permute-start | bytes 1867784 | tf_op jit(solution)/shard_map/ppermute | solution.py:649
  46.9 45.6 %collective-permute-start.4 = (f32[36,128]{1,0:T(8,128)S(1)}, f32[36,128]{1,0:T(8,128)S(1)}, u32[]{:S(2)}, u32[]{:S(2)}) collective-permute-start(f32[36,128]{1,0:T(8,128)S(1)} %get-tuple-element.41), channel_id=1, source_target_pairs={{0,1},{1,2},{2,3},{4,5},{5,6},{6,7},{8,9},{9,10},{10,11},{12,13},{... | collective-permute-start | bytes 55304 | tf_op jit(solution)/shard_map/ppermute | solution.py:644
  48.9 43.6 %collective-permute-start.5 = (f32[36,128]{1,0:T(8,128)S(1)}, f32[36,128]{1,0:T(8,128)S(1)}, u32[]{:S(2)}, u32[]{:S(2)}) collective-permute-start(f32[36,128]{1,0:T(8,128)S(1)} %get-tuple-element.42), channel_id=1, source_target_pairs={{1,0},{2,1},{3,2},{5,4},{6,5},{7,6},{9,8},{10,9},{11,10},{13,12},{... | collective-permute-start | bytes 55304 | tf_op jit(solution)/shard_map/ppermute | solution.py:645
  55.3 37.3 %collective-permute-start.3 = (f32[144,128]{1,0:T(8,128)S(1)}, f32[144,128]{1,0:T(8,128)S(1)}, u32[]{:S(2)}, u32[]{:S(2)}) collective-permute-start(f32[144,128]{1,0:T(8,128)S(1)} %get-tuple-element.40), channel_id=1, source_target_pairs={{4,8},{8,4},{12,16},{16,12},{20,24},{24,20},{28,32},{32,28},{36,40... | collective-permute-start | bytes 221192 | tf_op jit(solution)/shard_map/ppermute | solution.py:646
  76.8 15.7 %copy-start.1 = (f32[3,4,16,128]{3,2,1,0:T(8,128)S(1)}, f32[3,4,16,128]{3,2,1,0:T(8,128)}, u32[]{:S(2)}) copy-start(f32[3,4,16,128]{3,2,1,0:T(8,128)} %velocity.1) | copy-start | bytes 294916

commit v11 on v7

--- a/solution.py
+++ b/solution.py
@@ -286,10 +286,9 @@
                 sent[8 + 4 * k + x, rows] = t
         edge[0, rows] = gathered[2 * c, 128:144]
         edge[1, rows] = gathered[2 * c + 1, 144:160]
-    u = edge[jnp.where(north, 0, 1)]
-    sent[16] = u
-    sent_far[0] = sent[jnp.where(north, 0, 7)]
-    sent_far[1] = u
+    sent[16] = edge[jnp.where(north, 0, 1)]
+    sent_far[0] = sent[jnp.where(north, 7, 0)]
+    sent_far[1] = edge[jnp.where(north, 1, 0)]
 
 
 def species_edges(n_chips, species, near, beside, edge_low, edge_high):
@@ -345,10 +344,10 @@
         target_w[(i + 16).index()] = right
 
     loop(0, 8, copy)
-    left, right = sides(17)
+    right, left = sides(17)
     mobile_w.put(Place(0, -9), left)
     mobile_w.put(Place(0, 16), right)
-    left, right = sides(18)
+    right, left = sides(18)
     target_w[0] = target_w[0] - 0.5 * left
     target_w[23] = target_w[23] + 0.5 * right
     left, right = sides(16)
@@ -611,12 +610,11 @@
     for slab in (0, 2 * n_chips - 1):
         facing += [[device(slab, 0), device(slab, 1)], [device(slab, 2), device(slab, 3)]]
 
-    def beside(distance):
-        pairs = []
-        for j in range(n_chips - distance):
-            left, right = 2 * j + 1, 2 * (j + distance)
-            pairs += [(left, right), (right, left)]
-        return pairs
+    def both_ways(pairs):
+        return [pair for left, right in pairs for pair in ((left, right), (right, left))]
+
+    beside = both_ways([(2 * j + 1, 2 * j + 2) for j in range(n_chips - 1)])
+    two_away = both_ways([(2 * j, 2 * j + 5) for j in range(n_chips - 2)])
 
     within = [pair for j in range(n_chips) for pair in ((2 * j, 2 * j + 1), (2 * j + 1, 2 * j))]
     upward = [(c, c + 1) for c in range(3)]
@@ -641,8 +639,8 @@
     )
     gathered = gathered_over(own, chips)
     sent, sent_far, edge = call(bind(assemble), [plane(17), plane(2), plane(2)], [], gathered)
-    near = lax.ppermute(sent, "slab", beside(1))
-    far = lax.ppermute(sent_far, "slab", beside(2))
+    near = lax.ppermute(sent, "slab", beside)
+    far = lax.ppermute(sent_far, "slab", two_away)
     species_near, species_beside, edge_low, edge_high = call(
         bind(species_edges), [(144, LANES), (144, LANES), (40, LANES), (40, LANES)], [], species
     )

time: 92.1 us -> 89.9 us (0.976)
  waiting for transfers between devices: 6.24 us -> 4.25 us
    ppermute x1, starting transfers between devices: 9.01 us -> 3.76 us  [local(): swapped = lax.ppermute(mine, 'slab', within)]
    ppermute x2, starting transfers between devices: 6.62 us -> 11.7 us  [the longest x1 8.45 us: local(): far = lax.ppermute(sent_far, 'slab', two_away)]
    ppermute x2, waiting for transfers between devices: 6.23 us -> 4.25 us  [the longest x1 4.24 us: local(): far = lax.ppermute(sent_far, 'slab', two_away)]
  transfers between devices with their start and end apart: 5 -> 5, of which waited for: 2 -> 1; matrix products, arithmetic and copies ran while one was open for 0% -> 0% of each run, Pallas kernels for 8% -> 8%
where the time goes in v11:
time: 89.9 us; the launch traced here: 89.7 us
  blocking collectives  49.4 us (55%)
  starting transfers between devices  23.8 us (26%)
  Pallas kernels  11.4 us (13%)
  waiting for transfers between devices  4.25 us (5%)
    all_gather x5, blocking collectives, gathered_over(): return lax.all_gather(array, ('slab', 'cross'), axis_index_groups=groups)  49.4 us
    pallas_call x7, Pallas kernels, call(): pl.pallas_call(kernel, out_shape=shapes, in_specs=[pl.BlockSpec(memory_sp...  11.4 us
    ppermute x1, starting transfers between devices, local(): far = lax.ppermute(sent_far, 'slab', two_away)  8.45 us
    ppermute x1, starting transfers between devices, local(): y_high = lax.ppermute(edge_low, 'cross', downward)  6.37 us
    ppermute x1, waiting for transfers between devices, local(): far = lax.ppermute(sent_far, 'slab', two_away)  4.24 us
    ppermute x1, starting transfers between devices, local(): swapped = lax.ppermute(mine, 'slab', within)  3.76 us
    ppermute x1, starting transfers between devices, local(): near = lax.ppermute(sent, 'slab', beside)  3.3 us
    ppermute x1, starting transfers between devices, local(): y_low = lax.ppermute(edge_high, 'cross', upward)  1.92 us
  transfers between devices with their start and end apart: 5, of which 1 were waited for; matrix products, arithmetic and copies ran while one was open for 0% of the time, Pallas kernels for 8%

profile of v11, /device:TPU:257, one launch (start us, length us, event | category | flops | bytes accessed | tf_op | source)
XLA Modules:
  0.0 89.7 jit_solution(9567257966529411437)
XLA Ops:
  0.6 0.0 copy-start
  0.6 1.7 %shard_map.67 = f32[168,128]{1,0:T(8,128)} custom-call(f32[3,4,16,128]{3,2,1,0:T(8,128)} %velocity.1, f32[4,16,128]{2,1,0:T(8,128)} %density_in.1, f32[4,16,128]{2,1,0:T(8,128)} %source_in.1), custom_call_target="tpu_custom_call" | custom-call | flops 1000000 | bytes 1000000 | tf_op jit(solution)/shard_map/pallas_call | solution.py:583
  2.4 24.6 %all-gather = f32[1344,128]{1,0:T(8,128)S(1)} all-gather(f32[168,128]{1,0:T(8,128)} %shard_map.67), channel_id=2, replica_groups={{0,4,1,5,2,6,3,7},{8,12,9,13,10,14,11,15},{16,20,17,21,18,22,19,23},{24..., dimensions={0}, use_global_device_ids=true | all-gather | bytes 774144 | tf_op jit(solution)/shard_map/all_gather | solution.py:596
  27.0 0.1 shard_map.68
  27.0 3.3 %collective-permute-start = (f32[17,64,128]{2,1,0:T(8,128)S(1)}, f32[17,64,128]{2,1,0:T(8,128)S(1)}, u32[]{:S(2)}, u32[]{:S(2)}) collective-permute-start(f32[17,64,128]{2,1,0:T(8,128)S(1)} %get-tuple-element.23.own), channel_id=1, source_target_pairs={{4,8},{8,4},{12,16},{16,12},{20,24},{24,20},{28,32},{32,28},{36,40... | collective-permute-start | bytes 1671176 | tf_op jit(solution)/shard_map/ppermute | solution.py:642
  30.4 8.4 %collective-permute-start.1 = (f32[2,64,128]{2,1,0:T(8,128)S(1)}, f32[2,64,128]{2,1,0:T(8,128)S(1)}, u32[]{:S(2)}, u32[]{:S(2)}) collective-permute-start(f32[2,64,128]{2,1,0:T(8,128)S(1)} %get-tuple-element.25), channel_id=1, source_target_pairs={{0,20},{20,0},{8,28},{28,8},{16,36},{36,16},{24,44},{44,24},{32,52... | collective-permute-start | bytes 196616 | tf_op jit(solution)/shard_map/ppermute | solution.py:643
  38.8 0.0 collective-permute-done
  38.9 4.2 %collective-permute-done.1 = f32[2,64,128]{2,1,0:T(8,128)S(1)} collective-permute-done((f32[2,64,128]{2,1,0:T(8,128)S(1)}, f32[2,64,128]{2,1,0:T(8,128)S(1)}, u32[]{:S(2)}, u32[]{:S(2)}) %collective-permute-start.1) | collective-permute-done | bytes 65568 | tf_op jit(solution)/shard_map/ppermute | solution.py:643
  43.1 3.8 %collective-permute-start.2 = (f32[19,64,128]{2,1,0:T(8,128)S(1)}, f32[19,64,128]{2,1,0:T(8,128)S(1)}, u32[]{:S(2)}, u32[]{:S(2)}) collective-permute-start(f32[19,64,128]{2,1,0:T(8,128)S(1)} %constant_dynamic-update-slice_fusion.mine), channel_id=1, source_target_pairs={{0,4},{4,0},{8,12},{12,8},{16,20},{20,16},{24,28},{28,24},{32,36},... | collective-permute-start | bytes 1867784 | tf_op jit(solution)/shard_map/ppermute | solution.py:651
  46.9 0.0 copy-done
  46.9 1.9 %collective-permute-start.3 = (f32[40,128]{1,0:T(8,128)S(1)}, f32[40,128]{1,0:T(8,128)S(1)}, u32[]{:S(2)}, u32[]{:S(2)}) collective-permute-start(f32[40,128]{1,0:T(8,128)S(1)} %get-tuple-element.41), channel_id=1, source_target_pairs={{0,1},{1,2},{2,3},{4,5},{5,6},{6,7},{8,9},{9,10},{10,11},{12,13},{... | collective-permute-start | bytes 61448 | tf_op jit(solution)/shard_map/ppermute | solution.py:647
  48.9 6.4 %collective-permute-start.4 = (f32[40,128]{1,0:T(8,128)S(1)}, f32[40,128]{1,0:T(8,128)S(1)}, u32[]{:S(2)}, u32[]{:S(2)}) collective-permute-start(f32[40,128]{1,0:T(8,128)S(1)} %get-tuple-element.42), channel_id=1, source_target_pairs={{1,0},{2,1},{3,2},{5,4},{6,5},{7,6},{9,8},{10,9},{11,10},{13,12},{... | collective-permute-start | bytes 61448 | tf_op jit(solution)/shard_map/ppermute | solution.py:648
  55.3 0.0 collective-permute-done.2.swapped
  55.3 3.3 %shard_map.70 = (f32[26,80,128]{2,1,0:T(8,128)S(1)}, f32[8,24,64,128]{3,2,1,0:T(8,128)S(1)}, f32[24,80,128]{2,1,0:T(8,128)S(1)}, f32[10,32,128]{2,1,0:T(8,128)S(...) custom-call(f32[17,64,128]{2,1,0:T(8,128)S(1)} %get-tuple-element.23.own, ...), custom_call_target="tpu_custom_call" | custom-call | flops 1000000 | bytes 1000000 | tf_op jit(solution)/shard_map/pallas_call | solution.py:583
  58.6 5.2 %all-gather.1 = f32[544,128]{1,0:T(8,128)S(1)} all-gather(f32[272,128]{1,0:T(8,128)S(1)} %get-tuple-element.32), channel_id=3, replica_groups={{4,8},{5,9},{6,10},{7,11},{12,16},{13,17},{14,18},{15,19},{20,24},{21,2..., dimensions={0}, use_global_device_ids=true | all-gather | bytes 417792 | tf_op jit(solution)/shard_map/all_gather | solution.py:596
  63.8 7.9 %all-gather.2 = f32[1376,128]{1,0:T(8,128)S(1)} all-gather(f32[688,128]{1,0:T(8,128)S(1)} %pad_maximum_fusion), channel_id=4, replica_groups={{0,4},{1,5},{2,6},{3,7},{8,12},{9,13},{10,14},{11,15},{16,20},{17,21},{..., dimensions={0}, use_global_device_ids=true | all-gather | bytes 1056768 | tf_op jit(solution)/shard_map/all_gather | solution.py:596
  71.7 0.0 copy-start.1
  71.7 3.9 %shard_map.71 = (f32[14,80,128]{2,1,0:T(8,128)S(1)}, f32[6,32,128]{2,1,0:T(8,128)S(1)}, f32[8,18,32,128]{3,2,1,0:T(8,128)S(1)}, f32[2,64,128]{2,1,0:T(8,128)S(1)}) custom-call(f32[8,24,64,128]{3,2,1,0:T(8,128)S(1)} %get-tuple-element.28.weights_ref, f32[24,80,128]{2,1,0:T(8,128)S(1)} %get-tuple-element.29.pressure_ref, ...), custom_call_target="tpu_custom_call" | custom-call | flops 1000000 | bytes 1000000 | tf_op jit(solution)/shard_map/pallas_call | solution.py:583
  75.6 4.4 %all-gather.3 = f32[4,64,128]{2,1,0:T(8,128)S(1)} all-gather(f32[2,64,128]{2,1,0:T(8,128)S(1)} %get-tuple-element.37), channel_id=5, replica_groups={{4,8},{5,9},{6,10},{7,11},{12,16},{13,17},{14,18},{15,19},{20,24},{21,2..., dimensions={0}, use_global_device_ids=true | all-gather | bytes 196608 | tf_op jit(solution)/shard_map/all_gather | solution.py:596
  80.0 7.3 %all-gather.4 = f32[4,1,64,128]{3,2,1,0:T(8,128)S(1)} all-gather(f32[2,1,64,128]{3,2,1,0:T(8,128)S(1)} %slice.4), channel_id=6, replica_groups={{0,4},{1,5},{2,6},{3,7},{8,12},{9,13},{10,14},{11,15},{16,20},{17,21},{..., dimensions={0}, use_global_device_ids=true | all-gather | bytes 196608 | tf_op jit(solution)/shard_map/all_gather | solution.py:596
  87.3 0.0 collective-permute-done.3.y_low
  87.3 0.0 collective-permute-done.4.y_high
  87.3 0.0 copy-done.1
  87.4 2.3 %shard_map.73 = (f32[3,4,16,128]{3,2,1,0:T(8,128)}, f32[4,16,128]{2,1,0:T(8,128)}, f32[9,4,16,128]{3,2,1,0:T(8,128)}) custom-call(f32[26,80,128]{2,1,0:T(8,128)S(1)} %get-tuple-element.27.mobile_ref, f32[8,24,64,128]{3,2,1,0:T(8,128)S(1)} %get-tuple-element.28.weights_ref, f32[14,80,128]{2,1,0:T(8,128)S(1)} %get-tuple-element.34.pressure, ...), custom_call_target="tpu_custom_call" | custom-call | flops 1000000 | bytes 1000000 | tf_op jit(solution)/shard_map/pallas_call | solution.py:583
  (6 shorter events, 0.1 us)
Async XLA Ops:
  0.6 46.3 %copy-start = (f32[9,4,16,128]{3,2,1,0:T(8,128)S(1)}, f32[9,4,16,128]{3,2,1,0:T(8,128)}, u32[]{:S(2)}) copy-start(f32[9,4,16,128]{3,2,1,0:T(8,128)} %species.3) | copy-start | bytes 884740
  27.0 11.8 %collective-permute-start = (f32[17,64,128]{2,1,0:T(8,128)S(1)}, f32[17,64,128]{2,1,0:T(8,128)S(1)}, u32[]{:S(2)}, u32[]{:S(2)}) collective-permute-start(f32[17,64,128]{2,1,0:T(8,128)S(1)} %get-tuple-element.23.own), channel_id=1, source_target_pairs={{4,8},{8,4},{12,16},{16,12},{20,24},{24,20},{28,32},{32,28},{36,40... | collective-permute-start | bytes 1671176 | tf_op jit(solution)/shard_map/ppermute | solution.py:642
  30.4 12.8 %collective-permute-start.1 = (f32[2,64,128]{2,1,0:T(8,128)S(1)}, f32[2,64,128]{2,1,0:T(8,128)S(1)}, u32[]{:S(2)}, u32[]{:S(2)}) collective-permute-start(f32[2,64,128]{2,1,0:T(8,128)S(1)} %get-tuple-element.25), channel_id=1, source_target_pairs={{0,20},{20,0},{8,28},{28,8},{16,36},{36,16},{24,44},{44,24},{32,52... | collective-permute-start | bytes 196616 | tf_op jit(solution)/shard_map/ppermute | solution.py:643
  43.1 12.2 %collective-permute-start.2 = (f32[19,64,128]{2,1,0:T(8,128)S(1)}, f32[19,64,128]{2,1,0:T(8,128)S(1)}, u32[]{:S(2)}, u32[]{:S(2)}) collective-permute-start(f32[19,64,128]{2,1,0:T(8,128)S(1)} %constant_dynamic-update-slice_fusion.mine), channel_id=1, source_target_pairs={{0,4},{4,0},{8,12},{12,8},{16,20},{20,16},{24,28},{28,24},{32,36},... | collective-permute-start | bytes 1867784 | tf_op jit(solution)/shard_map/ppermute | solution.py:651
  46.9 40.4 %collective-permute-start.3 = (f32[40,128]{1,0:T(8,128)S(1)}, f32[40,128]{1,0:T(8,128)S(1)}, u32[]{:S(2)}, u32[]{:S(2)}) collective-permute-start(f32[40,128]{1,0:T(8,128)S(1)} %get-tuple-element.41), channel_id=1, source_target_pairs={{0,1},{1,2},{2,3},{4,5},{5,6},{6,7},{8,9},{9,10},{10,11},{12,13},{... | collective-permute-start | bytes 61448 | tf_op jit(solution)/shard_map/ppermute | solution.py:647
  48.9 38.5 %collective-permute-start.4 = (f32[40,128]{1,0:T(8,128)S(1)}, f32[40,128]{1,0:T(8,128)S(1)}, u32[]{:S(2)}, u32[]{:S(2)}) collective-permute-start(f32[40,128]{1,0:T(8,128)S(1)} %get-tuple-element.42), channel_id=1, source_target_pairs={{1,0},{2,1},{3,2},{5,4},{6,5},{7,6},{9,8},{10,9},{11,10},{13,12},{... | collective-permute-start | bytes 61448 | tf_op jit(solution)/shard_map/ppermute | solution.py:648
  71.7 15.7 %copy-start.1 = (f32[3,4,16,128]{3,2,1,0:T(8,128)S(1)}, f32[3,4,16,128]{3,2,1,0:T(8,128)}, u32[]{:S(2)}) copy-start(f32[3,4,16,128]{3,2,1,0:T(8,128)} %velocity.1) | copy-start | bytes 294916
